TPU v7x, 32 devices: a whole 2x2x4 slice. The times are simulated.
32 devices in a mesh: ctx: 8 (over z, x), fsdp: 4 (over y, core).
Axes of the slice: x: 2, y: 2, z: 4, core: 2. Of those that a mesh axis runs over, the one named last changes fastest.
Arguments:
- inputs: bfloat16 [8, 1024, 1600], P('fsdp', 'ctx'), may hold values from -6 to 6
- cotangent: bfloat16 [8, 1024, 1600], P('fsdp', 'ctx'), may hold values from -6 to 6
- w_query: bfloat16 [1600, 1600], P('fsdp'), may hold values from -0.15625 to 0.15625
- w_key: bfloat16 [1600, 1600], P('fsdp'), may hold values from -0.15625 to 0.15625
- w_value: bfloat16 [1600, 1600], P('fsdp'), may hold values from -0.15625 to 0.15625
- w_out: bfloat16 [1600, 1600], P('fsdp'), may hold values from -1.25 to 1.25
- w_fc: bfloat16 [1600, 6400], P('fsdp'), may hold values from -0.15625 to 0.15625
- w_proj: bfloat16 [6400, 1600], P('fsdp'), may hold values from -0.078125 to 0.078125
- ln1_gain: bfloat16 [1600], P('fsdp'), may hold values from 0.099609375 to 1.8984375
- ln1_bias: bfloat16 [1600], P('fsdp'), may hold values from -3 to 3
- query_bias: bfloat16 [1600], P('fsdp'), may hold values from -3 to 3
- value_bias: bfloat16 [1600], P('fsdp'), may hold values from -3 to 3
- out_bias: bfloat16 [1600], P('fsdp'), may hold values from -3 to 3
- ln2_gain: bfloat16 [1600], P('fsdp'), may hold values from 0.099609375 to 1.8984375
- ln2_bias: bfloat16 [1600], P('fsdp'), may hold values from -3 to 3
- fc_bias: bfloat16 [6400], P('fsdp'), may hold values from -3 to 3
- proj_bias: bfloat16 [1600], P('fsdp'), may hold values from -3 to 3
Outputs:
- outputs: bfloat16 [8, 1024, 1600], P('fsdp', 'ctx')
- input_grad: float32 [8, 1024, 1600], P('fsdp', 'ctx')
- grad_query: float32 [1600, 1600], P('fsdp')
- grad_key: float32 [1600, 1600], P('fsdp')
- grad_value: float32 [1600, 1600], P('fsdp')
- grad_out: float32 [1600, 1600], P('fsdp')
- grad_fc: float32 [1600, 6400], P('fsdp')
- grad_proj: float32 [6400, 1600], P('fsdp')
- grad_ln1_gain: float32 [1600], P('fsdp')
- grad_ln1_bias: float32 [1600], P('fsdp')
- grad_query_bias: float32 [1600], P('fsdp')
- grad_value_bias: float32 [1600], P('fsdp')
- grad_out_bias: float32 [1600], P('fsdp')
- grad_ln2_gain: float32 [1600], P('fsdp')
- grad_ln2_bias: float32 [1600], P('fsdp')
- grad_fc_bias: float32 [6400], P('fsdp')
- grad_proj_bias: float32 [1600], P('fsdp')
All inputs are finite; a program needn't handle non-finite values.
Results may differ from a plain program's by a relative error of at most 0.03.
Values may be sent and summed in bfloat16 or wider, within the bound.
A program may use at most 448 MiB of HBM per device.

v0:
```python
import jax
import jax.numpy as jnp
from jax import lax
from jax.sharding import PartitionSpec as P

HEADS = 25
HEAD = 64


EPS = 1e-05
SCALE = 0.125
NEGATIVE = -1000000000.0
ROOT = 0.7978845608028654
CUBIC = 0.044715


def normalize(values):
    centre = jnp.mean(values, axis=-1, keepdims=True)
    centred = values - centre
    spread = jnp.mean(centred * centred, axis=-1, keepdims=True)
    inv_std = lax.rsqrt(spread + EPS)
    return (centred * inv_std, inv_std)


def norm_back(grad_norm, gain, normal, inv_std):
    scaled = grad_norm * gain
    return inv_std * (
        scaled
        - jnp.mean(scaled, axis=-1, keepdims=True)
        - normal * jnp.mean(scaled * normal, axis=-1, keepdims=True)
    )


def gelu_value(values):
    return 0.5 * values * (1.0 + jnp.tanh(ROOT * (values + CUBIC * values * values * values)))


def gelu_slope(values):
    tangent = jnp.tanh(ROOT * (values + CUBIC * values * values * values))
    return 0.5 * (1.0 + tangent) + 0.5 * values * (1.0 - tangent * tangent) * ROOT * (
        1.0 + 3.0 * CUBIC * values * values
    )


def contract_last(left, right):
    return lax.dot_general(
        left, right, (((1,), (1,)), ((), ())), preferred_element_type=jnp.float32
    )


def contract_first(left, right):
    return lax.dot_general(
        left, right, (((0,), (0,)), ((), ())), preferred_element_type=jnp.float32
    )


def token_places(count, rows, device, n_ctx):
    index = jnp.arange(count, dtype=jnp.int32)
    owner = index // rows + device
    inner = index % rows
    half = rows // 2
    second = inner // half
    blocks = jnp.where(second == 0, owner, 2 * n_ctx - 1 - owner)
    return blocks * half + inner % half


def by_heads(array):
    return array.reshape(array.shape[0], array.shape[1], HEADS, HEAD)


def unpack(gathered, widths):
    pieces = []
    start = 0
    for width in widths:
        pieces.append(gathered[:, start : start + width].reshape(-1))
        start = start + width
    return pieces


def pack_parts(vectors, parts):
    return jnp.concatenate([vector.reshape(parts, -1) for vector in vectors], axis=1)


def masked_scores(queries, keys, query_places, key_places):
    raw = jnp.einsum("sqhd,skhd->shqk", queries, keys, preferred_element_type=jnp.float32) * SCALE
    allowed = key_places[None, None, None, :] <= query_places[None, None, :, None]
    return jnp.where(allowed, raw, NEGATIVE)


def log_totals(queries, keys_all, query_places, key_places, block):
    count = keys_all.shape[1] // block
    shape = (queries.shape[0], queries.shape[2], queries.shape[1])

    def log_step(carry, index):
        top, total = carry
        key_block = lax.dynamic_slice_in_dim(keys_all, index * block, block, 1)
        place_block = lax.dynamic_slice_in_dim(key_places, index * block, block, 0)
        scores = masked_scores(queries, key_block, query_places, place_block)
        new_top = jnp.maximum(top, jnp.max(scores, axis=-1))
        total = total * jnp.exp(top - new_top) + jnp.sum(
            jnp.exp(scores - new_top[..., None]), axis=-1
        )
        return ((new_top, total), None)

    start = (jnp.full(shape, NEGATIVE, jnp.float32), jnp.zeros(shape, jnp.float32))
    (top, total), _ = lax.scan(log_step, start, jnp.arange(count))
    return top + jnp.log(total)


def attend_out(queries, keys_all, values_all, query_places, key_places, log_total, block):
    count = keys_all.shape[1] // block

    def attend_step(summed, index):
        key_block = lax.dynamic_slice_in_dim(keys_all, index * block, block, 1)
        value_block = lax.dynamic_slice_in_dim(values_all, index * block, block, 1)
        place_block = lax.dynamic_slice_in_dim(key_places, index * block, block, 0)
        scores = masked_scores(queries, key_block, query_places, place_block)
        weights = jnp.exp(scores - log_total[..., None]).astype(jnp.bfloat16)
        return (
            summed
            + jnp.einsum(
                "shqk,skhd->sqhd", weights, value_block, preferred_element_type=jnp.float32
            ),
            None,
        )

    start = jnp.zeros(queries.shape, jnp.float32)
    summed, _ = lax.scan(attend_step, start, jnp.arange(count))
    return summed


def grads_by_keys(
    queries, grad_low, keys_all, values_all, query_places, key_places, log_total, totals, block
):
    count = keys_all.shape[1] // block

    def block_terms(index):
        key_block = lax.dynamic_slice_in_dim(keys_all, index * block, block, 1)
        value_block = lax.dynamic_slice_in_dim(values_all, index * block, block, 1)
        place_block = lax.dynamic_slice_in_dim(key_places, index * block, block, 0)
        scores = masked_scores(queries, key_block, query_places, place_block)
        probs = jnp.exp(scores - log_total[..., None])
        grad_probs = jnp.einsum(
            "sqhd,skhd->shqk", grad_low, value_block, preferred_element_type=jnp.float32
        )
        grad_scores = (probs * (grad_probs - totals[..., None])).astype(jnp.bfloat16)
        return (key_block, probs.astype(jnp.bfloat16), grad_scores)

    def grads_step(index, carry):
        grad_query, grad_keys, grad_values = carry
        key_block, weights, grad_scores = block_terms(index)
        grad_query = (
            grad_query
            + jnp.einsum(
                "shqk,skhd->sqhd", grad_scores, key_block, preferred_element_type=jnp.float32
            )
            * SCALE
        )
        key_part = (
            jnp.einsum("shqk,sqhd->skhd", grad_scores, queries, preferred_element_type=jnp.float32)
            * SCALE
        )
        value_part = jnp.einsum(
            "shqk,sqhd->skhd", weights, grad_low, preferred_element_type=jnp.float32
        )
        grad_keys = lax.dynamic_update_slice_in_dim(grad_keys, key_part, index * block, 1)
        grad_values = lax.dynamic_update_slice_in_dim(grad_values, value_part, index * block, 1)
        return (grad_query, grad_keys, grad_values)

    start = (
        jnp.zeros(queries.shape, jnp.float32),
        jnp.zeros(keys_all.shape, jnp.float32),
        jnp.zeros(keys_all.shape, jnp.float32),
    )
    return lax.fori_loop(0, count, grads_step, start)


def on_device(
    inputs,
    cotangent,
    w_query,
    w_key,
    w_value,
    w_out,
    w_fc,
    w_proj,
    ln1_gain,
    ln1_bias,
    query_bias,
    value_bias,
    out_bias,
    ln2_gain,
    ln2_bias,
    fc_bias,
    proj_bias,
):
    parts = lax.axis_size("fsdp")
    n_ctx = lax.axis_size("ctx")
    device = lax.axis_index("ctx")
    seqs, rows, width = inputs.shape
    hidden = w_fc.shape[1]
    quarter = width // parts
    hidden_part = hidden // parts
    tokens = seqs * rows
    first_pack = jnp.concatenate([ln1_gain, ln1_bias, query_bias, value_bias, out_bias])[None, :]
    query_full, key_full, value_full, out_full, first_small = (
        lax.all_gather(w_query, "fsdp", axis=0, tiled=True),
        lax.all_gather(w_key, "fsdp", axis=0, tiled=True),
        lax.all_gather(w_value, "fsdp", axis=0, tiled=True),
        lax.all_gather(w_out, "fsdp", axis=0, tiled=True),
        lax.all_gather(first_pack, "fsdp", axis=0, tiled=True),
    )
    gain_one, shift_one, bias_query, bias_value, bias_out = [
        piece.astype(jnp.float32) for piece in unpack(first_small, [quarter] * 5)
    ]
    x_full = inputs.astype(jnp.float32)
    hat_one, inv_one = normalize(x_full)
    normed_one = (hat_one * gain_one + shift_one).astype(jnp.bfloat16).reshape(tokens, width)
    queries = (
        (jnp.dot(normed_one, query_full, preferred_element_type=jnp.float32) + bias_query)
        .astype(jnp.bfloat16)
        .reshape(seqs, rows, width)
    )
    keys_own = (
        jnp.dot(normed_one, key_full, preferred_element_type=jnp.float32)
        .astype(jnp.bfloat16)
        .reshape(seqs, rows, width)
    )
    values_own = (
        (jnp.dot(normed_one, value_full, preferred_element_type=jnp.float32) + bias_value)
        .astype(jnp.bfloat16)
        .reshape(seqs, rows, width)
    )
    keys_all, values_all = (
        lax.all_gather(keys_own, "ctx", axis=1, tiled=True),
        lax.all_gather(values_own, "ctx", axis=1, tiled=True),
    )
    length = keys_all.shape[1]
    block = min(512, length)
    own_place = token_places(rows, rows, device, n_ctx)
    all_place = token_places(length, rows, 0, n_ctx)
    heads_query = by_heads(queries)
    log_total = log_totals(heads_query, by_heads(keys_all), own_place, all_place, block)
    attended = attend_out(
        heads_query,
        by_heads(keys_all),
        by_heads(values_all),
        own_place,
        all_place,
        log_total,
        block,
    )
    attended_low = attended.astype(jnp.bfloat16).reshape(tokens, width)
    branch_out = jnp.dot(attended_low, out_full, preferred_element_type=jnp.float32) + bias_out
    resid = x_full + branch_out.reshape(seqs, rows, width)
    second_pack = jnp.concatenate([ln2_gain, ln2_bias, proj_bias, fc_bias])[None, :]
    fc_full, proj_full, second_small = (
        lax.all_gather(w_fc, "fsdp", axis=0, tiled=True),
        lax.all_gather(w_proj, "fsdp", axis=0, tiled=True),
        lax.all_gather(second_pack, "fsdp", axis=0, tiled=True),
    )
    gain_two, shift_two, bias_proj, bias_fc = [
        piece.astype(jnp.float32)
        for piece in unpack(second_small, [quarter, quarter, quarter, hidden_part])
    ]
    hat_two, inv_two = normalize(resid)
    normed_two = (hat_two * gain_two + shift_two).astype(jnp.bfloat16).reshape(tokens, width)
    pre_act = jnp.dot(normed_two, fc_full, preferred_element_type=jnp.float32) + bias_fc
    activated = gelu_value(pre_act).astype(jnp.bfloat16)
    mlp_out = jnp.dot(activated, proj_full, preferred_element_type=jnp.float32) + bias_proj
    outputs = (resid + mlp_out.reshape(seqs, rows, width)).astype(jnp.bfloat16)
    grad_y = cotangent.reshape(tokens, width)
    grad_y_full = grad_y.astype(jnp.float32)
    fc_again, proj_again = (
        lax.all_gather(w_fc, "fsdp", axis=0, tiled=True),
        lax.all_gather(w_proj, "fsdp", axis=0, tiled=True),
    )
    grad_act = contract_last(grad_y, proj_again)
    grad_pre = (grad_act * gelu_slope(pre_act)).astype(jnp.bfloat16)
    grad_norm_two = contract_last(grad_pre, fc_again).reshape(seqs, rows, width)
    grad_gain_two = jnp.sum(grad_norm_two * hat_two, axis=(0, 1))
    grad_shift_two = jnp.sum(grad_norm_two, axis=(0, 1))
    grad_bias_fc = jnp.sum(grad_pre.astype(jnp.float32), axis=0)
    grad_bias_proj = jnp.sum(grad_y_full, axis=0)
    grad_resid = cotangent.astype(jnp.float32) + norm_back(
        grad_norm_two, gain_two, hat_two, inv_two
    )
    second_grads = pack_parts([grad_gain_two, grad_shift_two, grad_bias_proj, grad_bias_fc], parts)
    grad_proj_full = contract_first(activated, grad_y)
    grad_fc_full = contract_first(normed_two, grad_pre)
    fc_shard, proj_shard, second_shard = (
        lax.psum_scatter(
            grad_fc_full.astype(jnp.bfloat16), "fsdp", scatter_dimension=0, tiled=True
        ).astype(jnp.float32),
        lax.psum_scatter(
            grad_proj_full.astype(jnp.bfloat16), "fsdp", scatter_dimension=0, tiled=True
        ).astype(jnp.float32),
        lax.psum_scatter(
            second_grads.astype(jnp.bfloat16), "fsdp", scatter_dimension=0, tiled=True
        ).astype(jnp.float32),
    )
    fc_shard, proj_shard, second_shard = (
        lax.psum(fc_shard.astype(jnp.bfloat16), "ctx").astype(jnp.float32),
        lax.psum(proj_shard.astype(jnp.bfloat16), "ctx").astype(jnp.float32),
        lax.psum(second_shard.astype(jnp.bfloat16), "ctx").astype(jnp.float32),
    )
    gain_two_grad, shift_two_grad, proj_bias_grad, fc_bias_grad = unpack(
        second_shard, [quarter, quarter, quarter, hidden_part]
    )
    grad_branch = grad_resid.astype(jnp.bfloat16).reshape(tokens, width)
    query_again, key_again, value_again, out_again = (
        lax.all_gather(w_query, "fsdp", axis=0, tiled=True),
        lax.all_gather(w_key, "fsdp", axis=0, tiled=True),
        lax.all_gather(w_value, "fsdp", axis=0, tiled=True),
        lax.all_gather(w_out, "fsdp", axis=0, tiled=True),
    )
    grad_bias_out = jnp.sum(grad_branch.astype(jnp.float32), axis=0)
    grad_attended = (
        contract_last(grad_branch, out_again).astype(jnp.bfloat16).reshape(seqs, rows, width)
    )
    heads_grad = by_heads(grad_attended)
    totals = jnp.transpose(jnp.sum(heads_grad.astype(jnp.float32) * attended, axis=-1), (0, 2, 1))
    keys_back, values_back = (keys_all, values_all)
    grad_query, key_terms, value_terms = grads_by_keys(
        heads_query,
        heads_grad,
        by_heads(keys_back),
        by_heads(values_back),
        own_place,
        all_place,
        log_total,
        totals,
        block,
    )
    grad_keys, grad_values = (
        lax.psum_scatter(
            key_terms.reshape(seqs, length, width).astype(jnp.bfloat16),
            "ctx",
            scatter_dimension=1,
            tiled=True,
        ).astype(jnp.float32),
        lax.psum_scatter(
            value_terms.reshape(seqs, length, width).astype(jnp.bfloat16),
            "ctx",
            scatter_dimension=1,
            tiled=True,
        ).astype(jnp.float32),
    )
    grad_keys = grad_keys.reshape(tokens, width)
    grad_values = grad_values.reshape(tokens, width)
    query_low = grad_query.reshape(tokens, width).astype(jnp.bfloat16)
    key_low = grad_keys.astype(jnp.bfloat16)
    value_low = grad_values.astype(jnp.bfloat16)
    grad_bias_query = jnp.sum(query_low.astype(jnp.float32), axis=0)
    grad_bias_value = jnp.sum(value_low.astype(jnp.float32), axis=0)
    grad_norm_one = (
        contract_last(query_low, query_again)
        + contract_last(key_low, key_again)
        + contract_last(value_low, value_again)
    ).reshape(seqs, rows, width)
    grad_gain_one = jnp.sum(grad_norm_one * hat_one, axis=(0, 1))
    grad_shift_one = jnp.sum(grad_norm_one, axis=(0, 1))
    input_grad = grad_resid + norm_back(grad_norm_one, gain_one, hat_one, inv_one)
    first_grads = pack_parts(
        [grad_gain_one, grad_shift_one, grad_bias_query, grad_bias_value, grad_bias_out], parts
    )
    grad_out_full = contract_first(attended_low, grad_branch)
    grad_query_full = contract_first(normed_one, query_low)
    grad_key_full = contract_first(normed_one, key_low)
    grad_value_full = contract_first(normed_one, value_low)
    query_shard, key_shard, value_shard, out_shard, first_shard = (
        lax.psum_scatter(
            grad_query_full.astype(jnp.bfloat16), "fsdp", scatter_dimension=0, tiled=True
        ).astype(jnp.float32),
        lax.psum_scatter(
            grad_key_full.astype(jnp.bfloat16), "fsdp", scatter_dimension=0, tiled=True
        ).astype(jnp.float32),
        lax.psum_scatter(
            grad_value_full.astype(jnp.bfloat16), "fsdp", scatter_dimension=0, tiled=True
        ).astype(jnp.float32),
        lax.psum_scatter(
            grad_out_full.astype(jnp.bfloat16), "fsdp", scatter_dimension=0, tiled=True
        ).astype(jnp.float32),
        lax.psum_scatter(
            first_grads.astype(jnp.bfloat16), "fsdp", scatter_dimension=0, tiled=True
        ).astype(jnp.float32),
    )
    query_shard, key_shard, value_shard, out_shard, first_shard = (
        lax.psum(query_shard.astype(jnp.bfloat16), "ctx").astype(jnp.float32),
        lax.psum(key_shard.astype(jnp.bfloat16), "ctx").astype(jnp.float32),
        lax.psum(value_shard.astype(jnp.bfloat16), "ctx").astype(jnp.float32),
        lax.psum(out_shard.astype(jnp.bfloat16), "ctx").astype(jnp.float32),
        lax.psum(first_shard.astype(jnp.bfloat16), "ctx").astype(jnp.float32),
    )
    gain_one_grad, shift_one_grad, query_bias_grad, value_bias_grad, out_bias_grad = unpack(
        first_shard, [quarter] * 5
    )
    return (
        outputs,
        input_grad,
        query_shard,
        key_shard,
        value_shard,
        out_shard,
        fc_shard,
        proj_shard,
        gain_one_grad,
        shift_one_grad,
        query_bias_grad,
        value_bias_grad,
        out_bias_grad,
        gain_two_grad,
        shift_two_grad,
        fc_bias_grad,
        proj_bias_grad,
    )


def solution(mesh):
    in_specs = (
        P("fsdp", "ctx", None),
        P("fsdp", "ctx", None),
        P("fsdp", None),
        P("fsdp", None),
        P("fsdp", None),
        P("fsdp", None),
        P("fsdp", None),
        P("fsdp", None),
        P("fsdp"),
        P("fsdp"),
        P("fsdp"),
        P("fsdp"),
        P("fsdp"),
        P("fsdp"),
        P("fsdp"),
        P("fsdp"),
        P("fsdp"),
    )
    out_specs = (
        P("fsdp", "ctx", None),
        P("fsdp", "ctx", None),
        P("fsdp", None),
        P("fsdp", None),
        P("fsdp", None),
        P("fsdp", None),
        P("fsdp", None),
        P("fsdp", None),
        P("fsdp"),
        P("fsdp"),
        P("fsdp"),
        P("fsdp"),
        P("fsdp"),
        P("fsdp"),
        P("fsdp"),
        P("fsdp"),
        P("fsdp"),
    )
    return jax.shard_map(
        on_device, mesh=mesh, in_specs=in_specs, out_specs=out_specs, check_vma=False
    )
```

profile of v0, /device:TPU:0, one launch (start us, length us, event | category | flops | bytes accessed | tf_op | source)
XLA Modules:
  0.0 2183.9 jit_solution(6269473050918741912)
XLA Ops:
  19.1 15.2 all-reduce.7
  37.8 16.2 all-gather.11.cloned.1.call-done
  60.1 36.4 %all-gather.15.cloned.1.call-done = bf16[1600,1600]{1,0:T(8,128)(2,1)} async-done(((bf16[400,1600]{1,0:T(8,128)(2,1)}), bf16[1600,1600]{1,0:T(8,128)(2,1)}) %all-gather.15.cloned.1.call-update) | async-done | bytes 5120016 | tf_op jit(solution)/shard_map/all_gather | solution.py:208
  107.3 31.6 %all-gather.19.cloned.1.call-done = bf16[1600,1600]{1,0:T(8,128)(2,1)} async-done(((bf16[400,1600]{1,0:T(8,128)(2,1)}), bf16[1600,1600]{1,0:T(8,128)(2,1)}) %all-gather.19.cloned.1.call-update) | async-done | bytes 5120016 | tf_op jit(solution)/shard_map/all_gather | solution.py:207
  146.6 144.9 %all-gather.13.cloned.1.call-done = bf16[2,1024,1600]{1,0,2:T(2,128)(2,1)} async-done(((bf16[2,128,1600]{1,0,2:T(2,128)(2,1)}), bf16[2,1024,1600]{1,0,2:T(2,128)(2,1)}) %all-gather.13.cloned.1.call-update) | async-done | bytes 6553616 | tf_op jit(solution)/shard_map/all_gather | solution.py:236
  299.2 144.8 %all-gather.17.cloned.1.call-done = bf16[2,1024,1600]{1,0,2:T(2,128)(2,1)} async-done(((bf16[2,128,1600]{1,0,2:T(2,128)(2,1)}), bf16[2,1024,1600]{1,0,2:T(2,128)(2,1)}) %all-gather.17.cloned.1.call-update) | async-done | bytes 6553616 | tf_op jit(solution)/shard_map/all_gather | solution.py:235
  451.7 20.5 while.42
  472.2 19.3 while.43
  503.9 112.8 %all-gather.23.cloned.1.call-done = bf16[1600,6400]{1,0:T(8,128)(2,1)} async-done(((bf16[400,6400]{1,0:T(8,128)(2,1)}), bf16[1600,6400]{1,0:T(8,128)(2,1)}) %all-gather.23.cloned.1.call-update) | async-done | bytes 20480016 | tf_op jit(solution)/shard_map/all_gather | solution.py:258
  616.7 15.0 convolution_add_fusion
  631.8 120.0 %all-gather.25.cloned.1.call-done = bf16[6400,1600]{1,0:T(8,128)(2,1)} async-done(((bf16[1600,1600]{1,0:T(8,128)(2,1)}), bf16[6400,1600]{1,0:T(8,128)(2,1)}) %all-gather.25.cloned.1.call-update) | async-done | bytes 20480016 | tf_op jit(solution)/shard_map/all_gather | solution.py:259
  751.7 14.3 fusion.125
  800.3 75.2 %while.44 = (s32[]{:T(128)}, f32[2,128,25,64]{1,3,2,0:T(8,128)S(1)}, bf16[2,1024,25,64]{1,3,2,0:T(8,128)(2,1)}, bf16[2,1024,25,64]{1,3,2,0:T(8,128)(2,1)}, bf16[...) while((s32[]{:T(128)}, ...), condition=%wide.region_14.15_spmd.clone, body=%wide.region_13.14_spmd.clone.sunk | while | flops 2132857472 | bytes 170674512 | solution.py:175
  907.2 103.4 %reduce-scatter.11.cloned.1.call-done = bf16[2,128,1600]{2,1,0:T(8,128)(2,1)} async-done(((bf16[2,1024,1600]{2,1,0:T(8,128)(2,1)}), bf16[2,128,1600]{2,1,0:T(8,128)(2,1)}) %reduce-scatter.11.cloned.1.call-update) | async-done | bytes 819216 | tf_op jit(solution)/shard_map/reduce_scatter | solution.py:342
  1015.2 124.2 %reduce-scatter.9.cloned.1.call-done = bf16[2,128,1600]{2,1,0:T(8,128)(2,1)} async-done(((bf16[2,1024,1600]{2,1,0:T(8,128)(2,1)}), bf16[2,128,1600]{2,1,0:T(8,128)(2,1)}) %reduce-scatter.9.cloned.1.call-update) | async-done | bytes 819216 | tf_op jit(solution)/shard_map/reduce_scatter | solution.py:336
  1170.3 22.7 %reduce-scatter.19.cloned.1.call-done = bf16[400,1600]{1,0:T(8,128)(2,1)} async-done(((bf16[1600,1600]{1,0:T(8,128)(2,1)}), bf16[400,1600]{1,0:T(8,128)(2,1)}) %reduce-scatter.19.cloned.1.call-update) | async-done | bytes 1280016 | tf_op jit(solution)/shard_map/reduce_scatter | solution.py:381
  1193.0 54.3 %reduce-scatter.13.cloned.1.call-done = bf16[400,1600]{1,0:T(8,128)(2,1)} async-done(((bf16[1600,1600]{1,0:T(8,128)(2,1)}), bf16[400,1600]{1,0:T(8,128)(2,1)}) %reduce-scatter.13.cloned.1.call-update) | async-done | bytes 1280016 | tf_op jit(solution)/shard_map/reduce_scatter | solution.py:372
  1247.3 54.5 %reduce-scatter.17.cloned.1.call-done = bf16[400,1600]{1,0:T(8,128)(2,1)} async-done(((bf16[1600,1600]{1,0:T(8,128)(2,1)}), bf16[400,1600]{1,0:T(8,128)(2,1)}) %reduce-scatter.17.cloned.1.call-update) | async-done | bytes 1280016 | tf_op jit(solution)/shard_map/reduce_scatter | solution.py:378
  1301.8 54.9 %reduce-scatter.15.cloned.1.call-done = bf16[400,1600]{1,0:T(8,128)(2,1)} async-done(((bf16[1600,1600]{1,0:T(8,128)(2,1)}), bf16[400,1600]{1,0:T(8,128)(2,1)}) %reduce-scatter.15.cloned.1.call-update) | async-done | bytes 1280016 | tf_op jit(solution)/shard_map/reduce_scatter | solution.py:375
  1356.7 155.0 %reduce-scatter.23.cloned.1.call-done = bf16[1600,1600]{1,0:T(8,128)(2,1)} async-done(((bf16[6400,1600]{1,0:T(8,128)(2,1)}), bf16[1600,1600]{1,0:T(8,128)(2,1)}) %reduce-scatter.23.cloned.1.call-update) | async-done | bytes 5120016 | tf_op jit(solution)/shard_map/reduce_scatter | solution.py:295
  1511.7 158.0 %reduce-scatter.21.cloned.1.call-done = bf16[400,6400]{1,0:T(8,128)(2,1)} async-done(((bf16[1600,6400]{1,0:T(8,128)(2,1)}), bf16[400,6400]{1,0:T(8,128)(2,1)}) %reduce-scatter.21.cloned.1.call-update) | async-done | bytes 5120016 | tf_op jit(solution)/shard_map/reduce_scatter | solution.py:292
  1671.1 17.5 fusion.91
  1716.1 39.8 %all-reduce.4 = (bf16[1,2000]{1,0:T(2,128)(2,1)S(1)}, bf16[1,2800]{1,0:T(2,128)(2,1)S(1)}) all-reduce(bf16[1,2000]{1,0:T(2,128)(2,1)S(1)} %constant_dynamic-slice_fusion.1, bf16[1,2800]{1,0:T(2,128)(2,1)S(1)} %constant_dynamic-slice_fusion), channel_id=1, replica_groups=mesh['ctx'=8,'fsdp'=4] {'ctx'}, use_global_device_ids=true, to_apply=%region_37.38 | all-reduce | flops 4800 | bytes 19200 | tf_op jit(solution)/shard_map/psum | solution.py:393
  1761.5 396.2 %all-reduce.10.cloned.1.call-done = (bf16[400,1600]{1,0:T(8,128)(2,1)}, bf16[400,1600]{1,0:T(8,128)(2,1)}, bf16[400,1600]{1,0:T(8,128)(2,1)}, bf16[400,1600]{1,0...) async-done(((bf16[400,1600]{1,0:T(8,128)(2,1)}, bf16[400,1600]{1,0:T(8,128)(2,1)}, bf16[400,1600]{1,0:T(8,128)(2,1)}, bf16[400,1600]{1,0:T(8,128)(2,1)}, ...) | async-done | bytes 15360016 | tf_op jit(solution)/shard_map/psum | solution.py:389
  (307 shorter events, 331.8 us)
Async XLA Ops:
  7.2 46.8 %all-gather.11.cloned.1.call-start = ((), (), s32[]{:S(2)}) async-start(), calls=%async_computation.8 | async-start | bytes 6656000 | tf_op jit(solution)/shard_map/all_gather | solution.py:209
  7.9 88.6 %all-gather.15.cloned.1.call-start = ((), (), s32[]{:S(2)}) async-start(), calls=%async_computation.10 | async-start | bytes 6656000 | tf_op jit(solution)/shard_map/all_gather | solution.py:208
  8.7 130.3 %all-gather.19.cloned.1.call-start = ((), (), s32[]{:S(2)}) async-start(), calls=%async_computation.12 | async-start | bytes 6656000 | tf_op jit(solution)/shard_map/all_gather | solution.py:207
  9.4 282.1 %all-gather.13.cloned.1.call-start = ((), (), s32[]{:S(2)}) async-start(), calls=%async_computation.9 | async-start | bytes 7372800 | tf_op jit(solution)/shard_map/all_gather | solution.py:236
  60.0 384.0 %all-gather.17.cloned.1.call-start = ((), (), s32[]{:S(2)}) async-start(), calls=%async_computation.11 | async-start | bytes 7372800 | tf_op jit(solution)/shard_map/all_gather | solution.py:235
  102.4 391.0 %all-gather.21.cloned.1.call-start = ((), (), s32[]{:S(2)}) async-start(), calls=%async_computation.13 | async-start | bytes 6656000 | tf_op jit(solution)/shard_map/all_gather | solution.py:210
  103.0 513.8 %all-gather.23.cloned.1.call-start = ((), (), s32[]{:S(2)}) async-start(), calls=%async_computation.14 | async-start | bytes 25600000 | tf_op jit(solution)/shard_map/all_gather | solution.py:258
  103.7 648.0 %all-gather.25.cloned.1.call-start = ((), (), s32[]{:S(2)}) async-start(), calls=%async_computation.15 | async-start | bytes 26624000 | tf_op jit(solution)/shard_map/all_gather | solution.py:259
  104.5 906.1 %reduce-scatter.11.cloned.1.call-start = ((), (), s32[]{:S(2)}) async-start(), calls=%async_computation.17 | async-start | bytes 7667712 | tf_op jit(solution)/shard_map/reduce_scatter | solution.py:342
  105.8 675.1 %copy-start.28 = (f32[1600]{0:T(1024)}, f32[1600]{0:T(1024)S(1)}, u32[]{:S(2)}) copy-start(f32[1600]{0:T(1024)S(1)} %reshape.418) | copy-start | bytes 19204
  500.1 280.8 %copy-start.2 = (f32[2,128,1600]{1,2,0:T(8,128)}, f32[2,128,1600]{1,2,0:T(8,128)S(1)}, u32[]{:S(2)}) copy-start(f32[2,128,1600]{1,2,0:T(8,128)S(1)} %get-tuple-element.589) | copy-start | bytes 4915204
  500.1 280.8 %copy-start.32 = (f32[2,128]{1,0:T(2,128)}, f32[2,128]{1,0:T(2,128)S(1)}, u32[]{:S(2)}) copy-start(f32[2,128]{1,0:T(2,128)S(1)} %broadcast_multiply_fusion.2) | copy-start | bytes 3076
  500.3 280.5 %copy-start.37 = (f32[2,128]{1,0:T(2,128)}, f32[2,128]{1,0:T(2,128)S(1)}, u32[]{:S(2)}) copy-start(f32[2,128]{1,0:T(2,128)S(1)} %add_rsqrt_fusion) | copy-start | bytes 3076
  885.0 254.3 %reduce-scatter.9.cloned.1.call-start = ((), (), s32[]{:S(2)}) async-start(), calls=%async_computation.16 | async-start | bytes 7667712 | tf_op jit(solution)/shard_map/reduce_scatter | solution.py:336
  894.6 298.4 %reduce-scatter.19.cloned.1.call-start = ((), (), s32[]{:S(2)}) async-start(), calls=%async_computation.21 | async-start | bytes 6656000 | tf_op jit(solution)/shard_map/reduce_scatter | solution.py:381
  900.9 346.4 %reduce-scatter.13.cloned.1.call-start = ((), (), s32[]{:S(2)}) async-start(), calls=%async_computation.18 | async-start | bytes 6656000 | tf_op jit(solution)/shard_map/reduce_scatter | solution.py:372
  907.1 103.5 %copy-start.9 = (bf16[2,128,1600]{1,2,0:T(8,128)(2,1)S(1)}, bf16[2,128,1600]{1,2,0:T(8,128)(2,1)}, u32[]{:S(2)}) copy-start(bf16[2,128,1600]{1,2,0:T(8,128)(2,1)} %copy-done.8) | copy-start | bytes 2457604
  907.2 394.6 %reduce-scatter.17.cloned.1.call-start = ((), (), s32[]{:S(2)}) async-start(), calls=%async_computation.20 | async-start | bytes 6656000 | tf_op jit(solution)/shard_map/reduce_scatter | solution.py:378
  1015.1 128.8 %copy-start.26 = (bf16[2,128,1600]{2,1,0:T(8,128)(2,1)S(1)}, bf16[2,128,1600]{2,1,0:T(8,128)(2,1)}, u32[]{:S(2)}) copy-start(bf16[2,128,1600]{2,1,0:T(8,128)(2,1)} %copy.91) | copy-start | bytes 2457604
  1015.1 341.6 %reduce-scatter.15.cloned.1.call-start = ((), (), s32[]{:S(2)}) async-start(), calls=%async_computation.19 | async-start | bytes 6656000 | tf_op jit(solution)/shard_map/reduce_scatter | solution.py:375
  1143.9 367.8 %reduce-scatter.23.cloned.1.call-start = ((), (), s32[]{:S(2)}) async-start(), calls=%async_computation.23 | async-start | bytes 26624000 | tf_op jit(solution)/shard_map/reduce_scatter | solution.py:295
  1157.6 512.0 %reduce-scatter.21.cloned.1.call-start = ((), (), s32[]{:S(2)}) async-start(), calls=%async_computation.22 | async-start | bytes 25600000 | tf_op jit(solution)/shard_map/reduce_scatter | solution.py:292
  1170.0 987.7 %all-reduce.10.cloned.1.call-start = ((), (), s32[]{:S(2)}) async-start(), calls=%async_computation.24 | async-start | bytes 31539200 | tf_op jit(solution)/shard_map/psum | solution.py:389
  1697.9 59.4 %copy-start.3 = (f32[2,128,1600]{1,2,0:T(8,128)S(1)}, f32[2,128,1600]{1,2,0:T(8,128)}, u32[]{:S(2)}) copy-start(f32[2,128,1600]{1,2,0:T(8,128)} %copy-done.2) | copy-start | bytes 4915204
  (52 other events, 686.8 us)
Sparse Core Ops, SparseCore 0:
  9.6 44.3 all-gather.10
  55.5 40.8 all-gather.14
  98.1 40.8 all-gather.18
  141.4 150.0 all-gather.12
  293.9 149.9 all-gather.16
  445.4 40.8 all-gather.20
  487.8 128.8 all-gather.22
  618.3 133.3 all-gather.24
  885.1 125.4 reduce-scatter.10
  1014.7 124.6 reduce-scatter.8
  1141.9 51.0 reduce-scatter.18
  1195.4 51.8 reduce-scatter.12
  1249.9 51.8 reduce-scatter.16
  1304.8 51.8 reduce-scatter.14
  1359.1 152.4 reduce-scatter.22
  1514.1 155.4 reduce-scatter.20
  1674.9 482.7 all-reduce.9
where the time goes:
time: 2190 us; the launch traced here: 2180 us
  waiting for transfers between devices  1730 us (79%)
  matrix products  232 us (11%)
  local copies, waits for them, and re-layouts  85.9 us (4%)
  blocking collectives  66.3 us (3%)
  other arithmetic  43.9 us (2%)
    psum x1, waiting for transfers between devices, on_device(): lax.psum(query_shard.astype(jnp.bfloat16), 'ctx').astype(jnp.float32)  396 us
    reduce_scatter x1, waiting for transfers between devices, on_device(): lax.psum_scatter(grad_fc_full.astype(jnp.bfloat16), 'fsdp', scatter_dimen...  158 us
    reduce_scatter x1, waiting for transfers between devices, on_device(): lax.psum_scatter(grad_proj_full.astype(jnp.bfloat16), 'fsdp', scatter_dim...  155 us
    all_gather x1, waiting for transfers between devices, on_device(): lax.all_gather(values_own, 'ctx', axis=1, tiled=True)  145 us
    all_gather x1, waiting for transfers between devices, on_device(): lax.all_gather(keys_own, 'ctx', axis=1, tiled=True)  145 us
    reduce_scatter x1, waiting for transfers between devices, on_device(): lax.psum_scatter(key_terms.reshape(seqs, length, width).astype(jnp.bfloat...  124 us
    all_gather x1, waiting for transfers between devices, on_device(): lax.all_gather(w_proj, 'fsdp', axis=0, tiled=True)  120 us
    all_gather x1, waiting for transfers between devices, on_device(): lax.all_gather(w_fc, 'fsdp', axis=0, tiled=True)  113 us
  transfers between devices with their start and end apart: 17, of which 16 were waited for; matrix products, arithmetic and copies ran while one was open for 9% of the time, Pallas kernels for 0%

commit v1 on v0

v1 whole, which is shorter than its diff:
```python
import functools

import jax
import jax.numpy as jnp
from jax import lax
from jax.experimental import pallas as pl
from jax.experimental.pallas import tpu as pltpu
from jax.sharding import PartitionSpec as P

HEADS = 25
HEAD = 64
EPS = 1e-05
SCALE = 0.125
NEGATIVE = -1000000000.0
ROOT = 0.7978845608028654
CUBIC = 0.044715
LANES = 128
F32 = jnp.float32
BF16 = jnp.bfloat16


def normalize(values):
    centre = jnp.mean(values, axis=-1, keepdims=True)
    centred = values - centre
    spread = jnp.mean(centred * centred, axis=-1, keepdims=True)
    inv_std = lax.rsqrt(spread + EPS)
    return (centred * inv_std, inv_std)


def norm_back(grad_norm, gain, normal, inv_std):
    scaled = grad_norm * gain
    return inv_std * (
        scaled
        - jnp.mean(scaled, axis=-1, keepdims=True)
        - normal * jnp.mean(scaled * normal, axis=-1, keepdims=True)
    )


def gelu_both(values):
    tangent = jnp.tanh(ROOT * (values + CUBIC * values * values * values))
    value = 0.5 * values * (1.0 + tangent)
    slope = 0.5 * (1.0 + tangent) + 0.5 * values * (1.0 - tangent * tangent) * ROOT * (
        1.0 + 3.0 * CUBIC * values * values
    )
    return value, slope


def dot(left, right):
    return jnp.dot(left, right, preferred_element_type=F32)


def dot_nt(left, right):
    return lax.dot_general(left, right, (((1,), (1,)), ((), ())), preferred_element_type=F32)


def dot_tn(left, right):
    return lax.dot_general(left, right, (((0,), (0,)), ((), ())), preferred_element_type=F32)


def lane_half(shape, half):
    lane = lax.broadcasted_iota(jnp.int32, shape, 1)
    return (lane < HEAD) if half == 0 else (lane >= HEAD)


def keep_half(array, half):
    return jnp.where(lane_half(array.shape, half), array, jnp.zeros_like(array))


def causal_tail(scores, first_row, block):
    keys = lax.broadcasted_iota(jnp.int32, scores.shape, 0) + first_row
    queries = lax.broadcasted_iota(jnp.int32, scores.shape, 1)
    return jnp.where(keys <= queries, scores, NEGATIVE)


def attend_kernel(block, heads, q_ref, k_ref, v_ref, o_ref, ot_ref, lse_ref):
    length = q_ref.shape[0]
    pair = pl.program_id(0)
    v_t = jnp.transpose(v_ref[...].astype(F32)).astype(BF16)

    def one_head(half):
        for index in range(length // block):
            rows = slice(index * block, (index + 1) * block)
            count = (index + 1) * block
            query = keep_half(q_ref[rows, :], half) * jnp.asarray(SCALE, BF16)
            scores = dot_nt(k_ref[:count, :], query)
            scores = causal_tail(scores, -index * block, block)
            top = jnp.max(scores, axis=0, keepdims=True)
            weights = jnp.exp(scores - top)
            total = jnp.sum(weights, axis=0, keepdims=True)
            lse_ref[0, half : half + 1, rows] = top + jnp.log(total)
            weights = weights * (1.0 / total)
            ot = dot(v_t[half * HEAD : (half + 1) * HEAD, :count], weights.astype(BF16))
            ot_ref[0, half * HEAD : (half + 1) * HEAD, rows] = ot

    one_head(0)

    @pl.when(2 * pair + 1 < heads)
    def _():
        one_head(1)

    @pl.when(2 * pair + 1 >= heads)
    def _():
        ot_ref[0, HEAD:, :] = jnp.zeros((HEAD, length), F32)
        lse_ref[0, 1:2, :] = jnp.zeros((1, length), F32)

    o_ref[...] = jnp.transpose(ot_ref[0]).astype(BF16)


def attend(queries, keys, values, heads):
    length, width = queries.shape
    pairs = width // LANES
    block = min(256, length)
    column = pl.BlockSpec((length, LANES), lambda p: (0, p))
    return pl.pallas_call(
        functools.partial(attend_kernel, block, heads),
        grid=(pairs,),
        in_specs=[column] * 3,
        out_specs=[
            column,
            pl.BlockSpec((1, LANES, length), lambda p: (p, 0, 0)),
            pl.BlockSpec((1, 2, length), lambda p: (p, 0, 0)),
        ],
        out_shape=[
            jax.ShapeDtypeStruct((length, width), BF16),
            jax.ShapeDtypeStruct((pairs, LANES, length), F32),
            jax.ShapeDtypeStruct((pairs, 2, length), F32),
        ],
        name="attend",
    )(queries, keys, values)


def attend_back_kernel(
    block, heads, q_ref, k_ref, v_ref, do_ref, ot_ref, lse_ref, dq_ref, dk_ref, dv_ref, dk_sum, dv_sum
):
    length = q_ref.shape[0]
    pair = pl.program_id(0)
    k_t = jnp.transpose(k_ref[...].astype(F32)).astype(BF16)
    do_t = jnp.transpose(do_ref[...].astype(F32))
    dk_sum[...] = jnp.zeros_like(dk_sum)
    dv_sum[...] = jnp.zeros_like(dv_sum)
    dq_ref[...] = jnp.zeros_like(dq_ref)

    def one_head(half):
        span = slice(half * HEAD, (half + 1) * HEAD)
        shared = jnp.sum(do_t[span, :] * ot_ref[0, span, :], axis=0, keepdims=True)
        for index in range(length // block):
            rows = slice(index * block, (index + 1) * block)
            count = (index + 1) * block
            query = keep_half(q_ref[rows, :], half) * jnp.asarray(SCALE, BF16)
            grad = keep_half(do_ref[rows, :], half)
            scores = dot_nt(k_ref[:count, :], query)
            scores = causal_tail(scores, -index * block, block)
            probs = jnp.exp(scores - lse_ref[0, half : half + 1, rows])
            grad_probs = dot_nt(v_ref[:count, :], grad)
            grad_scores = (probs * (grad_probs - shared[:, rows])).astype(BF16)
            dv_sum[:count, :] += dot(probs.astype(BF16), grad)
            dk_sum[:count, :] += dot(grad_scores, query)
            dq_t = dot(k_t[span, :count], grad_scores) * SCALE
            pad = jnp.zeros_like(dq_t)
            both = jnp.concatenate([dq_t, pad] if half == 0 else [pad, dq_t], axis=0)
            dq_ref[rows, :] = dq_ref[rows, :] + jnp.transpose(both).astype(BF16)

    one_head(0)

    @pl.when(2 * pair + 1 < heads)
    def _():
        one_head(1)

    dk_ref[...] = dk_sum[...].astype(BF16)
    dv_ref[...] = dv_sum[...].astype(BF16)


def attend_back(queries, keys, values, grad, ot, lse, heads):
    length, width = queries.shape
    pairs = width // LANES
    block = min(256, length)
    column = pl.BlockSpec((length, LANES), lambda p: (0, p))
    return pl.pallas_call(
        functools.partial(attend_back_kernel, block, heads),
        grid=(pairs,),
        in_specs=[column] * 4
        + [
            pl.BlockSpec((1, LANES, length), lambda p: (p, 0, 0)),
            pl.BlockSpec((1, 2, length), lambda p: (p, 0, 0)),
        ],
        out_specs=[column] * 3,
        out_shape=[jax.ShapeDtypeStruct((length, width), BF16)] * 3,
        scratch_shapes=[pltpu.VMEM((length, LANES), F32)] * 2,
        name="attend_back",
    )(queries, keys, values, grad, ot, lse)


def on_device(
    inputs,
    cotangent,
    w_query,
    w_key,
    w_value,
    w_out,
    w_fc,
    w_proj,
    ln1_gain,
    ln1_bias,
    query_bias,
    value_bias,
    out_bias,
    ln2_gain,
    ln2_bias,
    fc_bias,
    proj_bias,
):
    parts = lax.axis_size("fsdp")
    n_ctx = lax.axis_size("ctx")
    me_ctx = lax.axis_index("ctx")
    me_part = lax.axis_index("fsdp")
    seqs, rows, width = inputs.shape
    hidden = w_fc.shape[1]
    quarter = width // parts
    hidden_part = hidden // parts
    own = seqs * rows
    all_seqs = seqs * parts
    tokens = all_seqs * rows
    length = rows * n_ctx
    half_rows = rows // 2
    groups = n_ctx // all_seqs
    heads_part = -(-HEADS // parts)
    live = heads_part * HEAD
    slots = -(-heads_part // (2 * groups)) * 2 * groups
    cols = slots * HEAD
    piece = cols // groups
    heads_here = heads_part if groups == 1 else slots // groups
    near = (live - quarter) * parts

    def gather(array):
        return lax.all_gather(array, "fsdp", axis=0, tiled=True)

    def scatter(array):
        return lax.psum_scatter(array.astype(BF16), "fsdp", scatter_dimension=0, tiled=True)

    def to_slots(array):
        lead = array.shape[:-1]
        array = jnp.pad(array, [(0, 0)] * len(lead) + [(0, parts * live - width)])
        array = array.reshape(*lead, parts, live)
        array = jnp.pad(array, [(0, 0)] * len(lead) + [(0, 0), (0, cols - live)])
        return array.reshape(*lead, parts * cols)

    small = jnp.concatenate(
        [ln1_gain, ln1_bias, query_bias, value_bias, out_bias, ln2_gain, ln2_bias, proj_bias]
    )[None, :]
    small = gather(small).astype(F32).reshape(parts, 8, quarter)
    gain_one, shift_one, bias_query, bias_value, bias_out, gain_two, shift_two, bias_proj = [
        small[:, i].reshape(-1) for i in range(8)
    ]
    bias_query = lax.dynamic_slice_in_dim(to_slots(bias_query), me_part * cols, cols, 0)
    bias_value = lax.dynamic_slice_in_dim(to_slots(bias_value), me_part * cols, cols, 0)
    bias_fc = fc_bias.astype(F32)

    qkv = to_slots(jnp.stack([w_query, w_key, w_value]))
    qkv = lax.all_to_all(qkv, "fsdp", split_axis=2, concat_axis=1, tiled=True)
    fc = lax.all_to_all(w_fc, "fsdp", split_axis=1, concat_axis=0, tiled=True)
    proj = w_proj
    from_right = lax.ppermute(w_out[:near], "fsdp", [(i + 1, i) for i in range(parts - 1)])
    out_w = lax.dynamic_slice_in_dim(
        jnp.concatenate([w_out, from_right]), me_part * (live - quarter), live, 0
    )
    out_w = jnp.pad(out_w, ((0, cols - live), (0, 0)))

    x_full = inputs.astype(F32).reshape(own, width)
    hat_one, inv_one = normalize(x_full)
    normed_one = gather((hat_one * gain_one + shift_one).astype(BF16))
    grad_y = gather(cotangent.reshape(own, width))
    queries = (dot(normed_one, qkv[0]) + bias_query).astype(BF16)
    keys = dot(normed_one, qkv[1]).astype(BF16)
    values = (dot(normed_one, qkv[2]) + bias_value).astype(BF16)

    def to_heads(array):
        array = array.reshape(all_seqs, rows, groups, piece)
        array = jnp.transpose(array, (0, 2, 1, 3)).reshape(n_ctx, rows, piece)
        array = lax.all_to_all(array, "ctx", split_axis=0, concat_axis=0, tiled=True)
        first, second = array[:, :half_rows], array[:, half_rows:]
        return jnp.concatenate([first, second[::-1]]).reshape(length, piece)

    def from_heads(array):
        array = array.reshape(2 * n_ctx, half_rows, piece)
        array = jnp.concatenate([array[:n_ctx], array[n_ctx:][::-1]], axis=1)
        array = lax.all_to_all(array, "ctx", split_axis=0, concat_axis=0, tiled=True)
        array = array.reshape(all_seqs, groups, rows, piece)
        return jnp.transpose(array, (0, 2, 1, 3)).reshape(tokens, cols)

    q_seq, k_seq, v_seq = to_heads(queries), to_heads(keys), to_heads(values)
    o_seq, ot, lse = attend(q_seq, k_seq, v_seq, heads_here)
    attended = from_heads(o_seq)
    resid = x_full + scatter(dot(attended, out_w)).astype(F32) + bias_out

    hat_two, inv_two = normalize(resid)
    normed_two = gather((hat_two * gain_two + shift_two).astype(BF16))
    pre_act = dot(normed_two, fc) + bias_fc
    value, slope = gelu_both(pre_act)
    activated = value.astype(BF16)
    mlp = scatter(dot(activated, proj)).astype(F32)
    outputs = (resid + mlp + bias_proj).astype(BF16).reshape(seqs, rows, width)

    grad_pre = (dot_nt(grad_y, proj) * slope).astype(BF16)
    grad_norm_two = scatter(dot_nt(grad_pre, fc)).astype(F32)
    grad_y_own = cotangent.reshape(own, width).astype(F32)
    grad_gain_two = jnp.sum(grad_norm_two * hat_two, axis=0)
    grad_shift_two = jnp.sum(grad_norm_two, axis=0)
    grad_bias_proj = jnp.sum(grad_y_own, axis=0)
    grad_bias_fc = jnp.sum(grad_pre.astype(F32), axis=0)
    grad_resid = grad_y_own + norm_back(grad_norm_two, gain_two, hat_two, inv_two)
    grad_branch = grad_resid.astype(BF16)
    grad_bias_out = jnp.sum(grad_branch.astype(F32), axis=0)
    grad_branch = gather(grad_branch)
    grad_attended = dot_nt(grad_branch, out_w).astype(BF16)

    dq_seq, dk_seq, dv_seq = attend_back(
        q_seq, k_seq, v_seq, to_heads(grad_attended), ot, lse, heads_here
    )
    grad_qkv = jnp.stack([from_heads(dq_seq), from_heads(dk_seq), from_heads(dv_seq)])
    grad_norm_one = scatter(
        dot_nt(grad_qkv[0], qkv[0]) + dot_nt(grad_qkv[1], qkv[1]) + dot_nt(grad_qkv[2], qkv[2])
    ).astype(F32)
    grad_bias_query = jnp.sum(grad_qkv[0].astype(F32), axis=0)
    grad_bias_value = jnp.sum(grad_qkv[2].astype(F32), axis=0)
    grad_gain_one = jnp.sum(grad_norm_one * hat_one, axis=0)
    grad_shift_one = jnp.sum(grad_norm_one, axis=0)
    input_grad = grad_resid + norm_back(grad_norm_one, gain_one, hat_one, inv_one)
    input_grad = input_grad.reshape(seqs, rows, width)

    per = n_ctx // parts
    slab = width // n_ctx
    proj_part = dot_tn(activated, grad_y).astype(BF16)
    fc_part = dot_tn(normed_two, grad_pre).astype(BF16)
    qkv_part = [dot_tn(normed_one, grad_qkv[i]).astype(BF16) for i in range(3)]
    out_part = dot_tn(attended, grad_branch).astype(BF16)

    def total(array):
        return lax.all_gather(
            lax.psum_scatter(array, "ctx", scatter_dimension=0, tiled=True), "ctx", axis=0, tiled=True
        )

    proj_grad = total(proj_part).astype(F32)
    out_grad = total(out_part)

    def across(array):
        n = array.shape[1]
        array = array.reshape(n_ctx, slab, n)
        array = jnp.roll(array, -per * me_part, axis=0)
        array = lax.psum_scatter(array, "ctx", scatter_dimension=0, tiled=True)
        pairs = [
            (c * parts + f, c * parts + (f + c // per) % parts)
            for c in range(n_ctx)
            for f in range(parts)
        ]
        array = lax.ppermute(array, ("ctx", "fsdp"), pairs)
        array = lax.all_gather(array, "ctx", axis=0, tiled=True)
        array = array.reshape(parts, per, slab, n)
        order = (me_part - jnp.arange(parts)) % parts
        array = jnp.take(array, order, axis=0)
        return jnp.transpose(array, (1, 2, 0, 3)).reshape(quarter, parts, n)

    fc_grad = across(fc_part).reshape(quarter, hidden).astype(F32)
    qkv_grad = [
        across(part)[:, :, :live].reshape(quarter, parts * live)[:, :width].astype(F32)
        for part in qkv_part
    ]
    out_rows = out_grad[:live]
    from_left = lax.ppermute(out_rows[live - near :], "fsdp", [(i, i + 1) for i in range(parts - 1)])
    out_rows = lax.dynamic_slice_in_dim(
        jnp.concatenate([from_left, out_rows]), near - me_part * (live - quarter), quarter, 0
    ).astype(F32)

    def window(vector):
        whole = jnp.zeros((parts * live,), F32)
        return lax.dynamic_update_slice_in_dim(whole, vector[:live], me_part * live, 0)[:width]

    small_grads = jnp.stack(
        [
            grad_gain_one,
            grad_shift_one,
            window(grad_bias_query),
            window(grad_bias_value),
            grad_bias_out,
            grad_gain_two,
            grad_shift_two,
            grad_bias_proj,
        ]
    )
    small_grads = lax.psum(small_grads, ("ctx", "fsdp"))
    small_grads = lax.dynamic_slice_in_dim(small_grads, me_part * quarter, quarter, 1)
    fc_bias_grad = lax.psum(grad_bias_fc, "ctx")
    return (
        outputs,
        input_grad,
        qkv_grad[0],
        qkv_grad[1],
        qkv_grad[2],
        out_rows,
        fc_grad,
        proj_grad,
        small_grads[0],
        small_grads[1],
        small_grads[2],
        small_grads[3],
        small_grads[4],
        small_grads[5],
        small_grads[6],
        fc_bias_grad,
        small_grads[7],
    )


def solution(mesh):
    tokens = P("fsdp", "ctx", None)
    matrix = P("fsdp", None)
    vector = P("fsdp")
    return jax.shard_map(
        on_device,
        mesh=mesh,
        in_specs=(tokens, tokens) + (matrix,) * 6 + (vector,) * 9,
        out_specs=(tokens, tokens) + (matrix,) * 6 + (vector,) * 9,
        check_vma=False,
    )
```

time: 2190 us -> 1660 us (0.76)
  waiting for transfers between devices: 1730 us -> 978 us
  blocking collectives: 66.3 us -> 228 us
  matrix products: 232 us -> 112 us
  local copies, waits for them, and re-layouts: 85.9 us -> 162 us
  starting transfers between devices: 1.28 us -> 49.9 us
  Pallas kernels: 0 us -> 34.5 us
  other arithmetic: 43.9 us -> 72.6 us
    reduce_scatter x8, waiting for transfers between devices: 727 us -> 306 us  [the longest x3 191 us: across(): array = lax.psum_scatter(array, 'ctx', scatter_dimension=0, tiled=True)]
    psum x1 -> x0, waiting for transfers between devices: 396 us -> none  [on_device(): lax.psum(query_shard.astype(jnp.bfloat16), 'ctx').astype(jnp.float32)]
    all_gather x8 -> x10, waiting for transfers between devices: 607 us -> 284 us  [the longest x4 180 us: across(): array = lax.all_gather(array, 'ctx', axis=0, tiled=True)]
    all_to_all x0 -> x6, waiting for transfers between devices: none -> 250 us  [the longest x1 93 us: on_device(): qkv = lax.all_to_all(qkv, 'fsdp', split_axis=2, concat_axis=1, tiled=True)]
    all_to_all x0 -> x4, blocking collectives: none -> 159 us  [the longest x3 122 us: from_heads(): lax.all_to_all(array, 'ctx', split_axis=0, concat_axis=0, tiled=True)]
    unnamed x17 -> x22, waiting for transfers between devices: 4.15 us -> 134 us
    dot_general x32 -> x18, matrix products: 232 us -> 112 us  [the longest x6 40.6 us: dot(): return jnp.dot(left, right, preferred_element_type=F32)]
    pallas_call x0 -> x2, Pallas kernels: none -> 34.5 us  [the longest x1 18.6 us: attend(): pl.pallas_call(functools.partial(attend_kernel, block, heads), grid=(pair...]
  transfers between devices with their start and end apart: 17 -> 32, of which waited for: 16 -> 22; matrix products, arithmetic and copies ran while one was open for 9% -> 15% of each run, Pallas kernels for 0% -> 1%
where the time goes in v1:
time: 1660 us; the launch traced here: 1650 us
  waiting for transfers between devices  978 us (59%)
  blocking collectives  228 us (14%)
  local copies, waits for them, and re-layouts  162 us (10%)
  matrix products  112 us (7%)
  other arithmetic  72.6 us (4%)
  starting transfers between devices  49.9 us (3%)
  Pallas kernels  34.5 us (2%)
    reduce_scatter x3, waiting for transfers between devices, across(): array = lax.psum_scatter(array, 'ctx', scatter_dimension=0, tiled=True)  191 us
    all_gather x4, waiting for transfers between devices, across(): array = lax.all_gather(array, 'ctx', axis=0, tiled=True)  180 us
    unnamed x22, waiting for transfers between devices  134 us
    all_to_all x3, blocking collectives, from_heads(): lax.all_to_all(array, 'ctx', split_axis=0, concat_axis=0, tiled=True)  122 us
    reduce_scatter x4, waiting for transfers between devices, scatter(): lax.psum_scatter(array.astype(BF16), 'fsdp', scatter_dimension=0, tiled=T...  115 us
    all_to_all x1, waiting for transfers between devices, on_device(): qkv = lax.all_to_all(qkv, 'fsdp', split_axis=2, concat_axis=1, tiled=True)  93 us
    all_to_all x1, waiting for transfers between devices, on_device(): fc = lax.all_to_all(w_fc, 'fsdp', split_axis=1, concat_axis=0, tiled=True)  78.5 us
    all_gather x2, waiting for transfers between devices, total(): lax.all_gather(lax.psum_scatter(array, 'ctx', scatter_dimension=0, tiled=...  74.6 us
  transfers between devices with their start and end apart: 32, of which 22 were waited for; matrix products, arithmetic and copies ran while one was open for 15% of the time, Pallas kernels for 1%

profile of v1, /device:TPU:0, one launch (start us, length us, event | category | flops | bytes accessed | tf_op | source)
XLA Modules:
  0.0 1651.8 jit_solution(15657567125513092882)
XLA Ops:
  58.6 93.0 %all-to-all-done = bf16[3,400,2048]{1,0,2:T(4,128)(2,1)} async-done(((bf16[3,400,2048]{1,0,2:T(4,128)(2,1)}), bf16[3,400,2048]{1,0,2:T(4,128)(2,1)}, u32[]{:S(2)}, u32[]{:S(2)}) %all-to-all-start) | async-done | bytes 4915232 | tf_op jit(solution)/shard_map/all_to_all | solution.py:259
  188.5 19.4 %all-to-all-done.3 = bf16[8,128,512]{2,1,0:T(8,128)(2,1)S(1)} async-done(((bf16[8,128,512]{2,1,0:T(8,128)(2,1)}), bf16[8,128,512]{2,1,0:T(8,128)(2,1)S(1)}, u32[]{:S(2)}, u32[]{:S(2)}) %all-to-all-start.3) | async-done | bytes 1048608 | tf_op jit(solution)/shard_map/all_to_all | solution.py:279
  218.0 19.7 %all-to-all-done.2 = bf16[8,128,512]{2,1,0:T(8,128)(2,1)} async-done(((bf16[8,128,512]{2,1,0:T(8,128)(2,1)}), bf16[8,128,512]{2,1,0:T(8,128)(2,1)}, u32[]{:S(2)}, u32[]{:S(2)}) %all-to-all-start.2) | async-done | bytes 1048608 | tf_op jit(solution)/shard_map/all_to_all | solution.py:279
  245.8 21.3 %all-to-all-done.1 = bf16[8,128,512]{2,1,0:T(8,128)(2,1)S(1)} async-done(((bf16[8,128,512]{2,1,0:T(8,128)(2,1)}), bf16[8,128,512]{2,1,0:T(8,128)(2,1)S(1)}, u32[]{:S(2)}, u32[]{:S(2)}) %all-to-all-start.1) | async-done | bytes 1048608 | tf_op jit(solution)/shard_map/all_to_all | solution.py:279
  272.4 18.6 %attend.1 = (bf16[1024,512]{1,0:T(8,128)(2,1)}, f32[4,128,1024]{2,1,0:T(8,128)}, f32[4,2,1024]{2,1,0:T(2,128)}) custom-call(bf16[1024,512]{1,0:T(8,128)(2,1)} %bitcast.167, bf16[1024,512]{1,0:T(8,128)(2,1)} %bitcast.165, bf16[1024,512]{1,0:T(8,128)(2,1)} %bitcast.163), custom_call_target="tpu_custom_call" | custom-call | tf_op jit(solution)/shard_map/attend/pallas_call | solution.py:114
  328.6 36.8 %reduce-scatter.15.cloned.1.call-done = bf16[256,1600]{0,1:T(8,128)(2,1)} async-done(((bf16[1024,1600]{0,1:T(8,128)(2,1)}), bf16[256,1600]{0,1:T(8,128)(2,1)}) %reduce-scatter.15.cloned.1.call-update) | async-done | bytes 819216 | tf_op jit(solution)/shard_map/reduce_scatter | solution.py:238
  392.6 78.5 %all-to-all-done.5 = bf16[400,4,1600]{2,0,1:T(8,128)(2,1)} async-done(((bf16[400,4,1600]{2,0,1:T(8,128)(2,1)}), bf16[400,4,1600]{2,0,1:T(8,128)(2,1)}, u32[]{:S(2)}, u32[]{:S(2)}) %all-to-all-start.5) | async-done | bytes 5120032 | tf_op jit(solution)/shard_map/all_to_all | solution.py:260
  509.3 38.5 %reduce-scatter.19.cloned.1.call-done = bf16[256,1600]{0,1:T(8,128)(2,1)} async-done(((bf16[1024,1600]{0,1:T(8,128)(2,1)}), bf16[256,1600]{0,1:T(8,128)(2,1)}) %reduce-scatter.19.cloned.1.call-update) | async-done | bytes 819216 | tf_op jit(solution)/shard_map/reduce_scatter | solution.py:238
  551.7 29.7 %all-gather.19.cloned.1.call-done = bf16[1024,1600]{0,1:T(8,128)(2,1)} async-done(((bf16[256,1600]{0,1:T(8,128)(2,1)}), bf16[1024,1600]{0,1:T(8,128)(2,1)}) %all-gather.19.cloned.1.call-update) | async-done | bytes 3276816 | tf_op jit(solution)/shard_map/all_gather | solution.py:235
  617.5 36.6 %all_to_all.74 = bf16[8,128,512]{2,1,0:T(8,128)(2,1)S(1)} all-to-all(bf16[8,128,512]{2,1,0:T(8,128)(2,1)S(1)} %bitcast.208), channel_id=1, replica_groups=mesh['ctx'=8,'fsdp'=4] {'ctx'}, dimensions={0} | all-to-all | bytes 2097152 | tf_op jit(solution)/shard_map/all_to_all | solution.py:279
  676.4 47.9 %all_to_all.75 = bf16[8,128,512]{2,1,0:T(8,128)(2,1)S(1)} all-to-all(bf16[8,128,512]{2,1,0:T(8,128)(2,1)S(1)} %pad_maximum_fusion.8), channel_id=1, replica_groups=mesh['ctx'=8,'fsdp'=4] {'ctx'}, dimensions={0} | all-to-all | bytes 2097152 | tf_op jit(solution)/shard_map/all_to_all | solution.py:286
  733.5 31.3 %all_to_all.76 = bf16[8,128,512]{2,1,0:T(8,128)(2,1)S(1)} all-to-all(bf16[8,128,512]{2,1,0:T(8,128)(2,1)S(1)} %pad_maximum_fusion.6), channel_id=1, replica_groups=mesh['ctx'=8,'fsdp'=4] {'ctx'}, dimensions={0} | all-to-all | bytes 2097152 | tf_op jit(solution)/shard_map/all_to_all | solution.py:286
  774.3 42.9 %all_to_all.77 = bf16[8,128,512]{2,1,0:T(8,128)(2,1)S(1)} all-to-all(bf16[8,128,512]{2,1,0:T(8,128)(2,1)S(1)} %pad_maximum_fusion.7), channel_id=1, replica_groups=mesh['ctx'=8,'fsdp'=4] {'ctx'}, dimensions={0} | all-to-all | bytes 2097152 | tf_op jit(solution)/shard_map/all_to_all | solution.py:286
  826.4 128.7 %reduce-scatter.31.cloned.1.call-done = bf16[1,200,1600]{2,1,0:T(8,128)(2,1)} async-done(((bf16[8,200,1600]{2,1,0:T(8,128)(2,1)}), bf16[1,200,1600]{2,1,0:T(8,128)(2,1)}) %reduce-scatter.31.cloned.1.call-update) | async-done | bytes 640016
  961.9 62.1 %reduce-scatter.27.cloned.1.call-done = bf16[1,200,512]{2,1,0:T(8,128)(2,1)} async-done(((bf16[8,200,512]{2,1,0:T(8,128)(2,1)}), bf16[1,200,512]{2,1,0:T(8,128)(2,1)}) %reduce-scatter.27.cloned.1.call-update) | async-done | bytes 204816 | tf_op jit(solution)/shard_map/reduce_scatter | solution.py:349
  1027.4 64.8 %reduce-scatter.23.cloned.1.call-done = bf16[1,200,512]{2,1,0:T(8,128)(2,1)} async-done(((bf16[8,200,512]{2,1,0:T(8,128)(2,1)}), bf16[1,200,512]{2,1,0:T(8,128)(2,1)}) %reduce-scatter.23.cloned.1.call-update) | async-done | bytes 204816 | tf_op jit(solution)/shard_map/reduce_scatter | solution.py:349
  1095.7 64.6 %reduce-scatter.25.cloned.1.call-done = bf16[1,200,512]{2,1,0:T(8,128)(2,1)} async-done(((bf16[8,200,512]{2,1,0:T(8,128)(2,1)}), bf16[1,200,512]{2,1,0:T(8,128)(2,1)}) %reduce-scatter.25.cloned.1.call-update) | async-done | bytes 204816 | tf_op jit(solution)/shard_map/reduce_scatter | solution.py:349
  1189.6 23.2 %psum.15 = f32[1600]{0:T(1024)} all-reduce(f32[1600]{0:T(1024)} %get-tuple-element.153), channel_id=1, replica_groups=mesh['ctx'=8,'fsdp'=4] {'ctx'}, use_global_device_ids=true, to_apply=%region_28.31 | all-reduce | flops 1600 | bytes 12800 | tf_op jit(solution)/shard_map/psum | solution.py:391
  1220.3 74.5 %all-gather.31.cloned.1.call-done = bf16[1600,1600]{1,0:T(8,128)(2,1)} async-done(((bf16[200,1600]{1,0:T(8,128)(2,1)}), bf16[1600,1600]{1,0:T(8,128)(2,1)}) %all-gather.31.cloned.1.call-update) | async-done | bytes 5120016 | tf_op jit(solution)/shard_map/all_gather | solution.py:338
  1302.2 79.8 %all-gather.29.cloned.1.call-done = bf16[8,200,1600]{2,1,0:T(8,128)(2,1)} async-done(((bf16[1,200,1600]{2,1,0:T(8,128)(2,1)}), bf16[8,200,1600]{2,1,0:T(8,128)(2,1)}) %all-gather.29.cloned.1.call-update) | async-done | bytes 5120016 | tf_op jit(solution)/shard_map/all_gather | solution.py:356
  1430.4 41.9 %all-gather.21.cloned.1.call-done = bf16[8,200,512]{2,1,0:T(8,128)(2,1)} async-done(((bf16[1,200,512]{2,1,0:T(8,128)(2,1)}), bf16[8,200,512]{2,1,0:T(8,128)(2,1)}) %all-gather.21.cloned.1.call-update) | async-done | bytes 1638416 | tf_op jit(solution)/shard_map/all_gather | solution.py:356
  1475.7 41.9 %all-gather.23.cloned.1.call-done = bf16[8,200,512]{2,1,0:T(8,128)(2,1)} async-done(((bf16[1,200,512]{2,1,0:T(8,128)(2,1)}), bf16[8,200,512]{2,1,0:T(8,128)(2,1)}) %all-gather.23.cloned.1.call-update) | async-done | bytes 1638416 | tf_op jit(solution)/shard_map/all_gather | solution.py:356
  1559.3 38.8 %reduce-scatter.17.cloned.1.call-done = bf16[256,1600]{0,1:T(8,128)(2,1)} async-done(((bf16[1024,1600]{0,1:T(8,128)(2,1)}), bf16[256,1600]{0,1:T(8,128)(2,1)}) %reduce-scatter.17.cloned.1.call-update) | async-done | bytes 819216 | tf_op jit(solution)/shard_map/reduce_scatter | solution.py:238
  1603.1 39.8 %psum.14 = f32[8,1600]{1,0:T(8,128)S(1)} all-reduce(f32[8,1600]{1,0:T(8,128)S(1)} %stack.51), channel_id=1, replica_groups=mesh['ctx'=8,'fsdp'=4] {'ctx','fsdp'}, use_global_device_ids=true, to_apply=%region_26.29 | all-reduce | flops 12800 | bytes 102400 | tf_op jit(solution)/shard_map/psum | solution.py:389
  (302 shorter events, 462.0 us)
Async XLA Ops:
  7.2 163.7 %all-gather.13.cloned.1.call-start = ((), (), s32[]{:S(2)}) async-start(), calls=%async_computation.20 | async-start | bytes 4096000 | tf_op jit(solution)/shard_map/all_gather | solution.py:235
  52.5 99.0 %all-to-all-start = ((bf16[3,400,2048]{1,0,2:T(4,128)(2,1)}), bf16[3,400,2048]{1,0,2:T(4,128)(2,1)}, u32[]{:S(2)}, u32[]{:S(2)}) async-start(bf16[3,400,2048]{1,0,2:T(4,128)(2,1)} %bitcast.158), calls=%async_computation | async-start | bytes 16777216 | tf_op jit(solution)/shard_map/all_to_all | solution.py:259
  176.3 31.6 %all-to-all-start.3 = ((bf16[8,128,512]{2,1,0:T(8,128)(2,1)}), bf16[8,128,512]{2,1,0:T(8,128)(2,1)S(1)}, u32[]{:S(2)}, u32[]{:S(2)}) async-start(bf16[8,128,512]{2,1,0:T(8,128)(2,1)} %bitcast.207), calls=%async_computation.3 | async-start | bytes 2097152 | tf_op jit(solution)/shard_map/all_to_all | solution.py:279
  208.0 29.7 %all-to-all-start.2 = ((bf16[8,128,512]{2,1,0:T(8,128)(2,1)}), bf16[8,128,512]{2,1,0:T(8,128)(2,1)}, u32[]{:S(2)}, u32[]{:S(2)}) async-start(bf16[8,128,512]{2,1,0:T(8,128)(2,1)} %bitcast.205), calls=%async_computation.2 | async-start | bytes 2097152 | tf_op jit(solution)/shard_map/all_to_all | solution.py:279
  297.0 68.4 %reduce-scatter.15.cloned.1.call-start = ((), (), s32[]{:S(2)}) async-start(), calls=%async_computation.21 | async-start | bytes 4096000 | tf_op jit(solution)/shard_map/reduce_scatter | solution.py:238
  328.3 142.7 %all-gather.15.cloned.1.call-start = ((), (), s32[]{:S(2)}) async-start(), calls=%async_computation.22 | async-start | bytes 4096000 | tf_op jit(solution)/shard_map/all_gather | solution.py:235
  385.8 85.3 %all-to-all-start.5 = ((bf16[400,4,1600]{2,0,1:T(8,128)(2,1)}), bf16[400,4,1600]{2,0,1:T(8,128)(2,1)}, u32[]{:S(2)}, u32[]{:S(2)}) async-start(bf16[400,4,1600]{2,0,1:T(8,128)(2,1)} %copy.66), calls=%async_computation.6 | async-start | bytes 10649600 | tf_op jit(solution)/shard_map/all_to_all | solution.py:260
  391.0 91.1 %all-gather.17.cloned.1.call-start = ((), (), s32[]{:S(2)}) async-start(), calls=%async_computation.24 | async-start | bytes 4096000 | tf_op jit(solution)/shard_map/all_gather | solution.py:235
  392.1 155.7 %reduce-scatter.19.cloned.1.call-start = ((), (), s32[]{:S(2)}) async-start(), calls=%async_computation.25 | async-start | bytes 4096000 | tf_op jit(solution)/shard_map/reduce_scatter | solution.py:238
  509.1 72.3 %all-gather.19.cloned.1.call-start = ((), (), s32[]{:S(2)}) async-start(), calls=%async_computation.26 | async-start | bytes 4096000 | tf_op jit(solution)/shard_map/all_gather | solution.py:235
  551.6 269.4 %reduce-scatter.29.cloned.1.call-start = ((), (), s32[]{:S(2)}) async-start(), calls=%async_computation.34 | async-start | bytes 1916928 | tf_op jit(solution)/shard_map/reduce_scatter | solution.py:339
  586.7 239.7 %reduce-scatter.33.cloned.1.call-start = ((), (), s32[]{:S(2)}) async-start(), calls=%async_computation.39 | async-start | bytes 5990400
  599.2 355.9 %reduce-scatter.31.cloned.1.call-start = ((), (), s32[]{:S(2)}) async-start(), calls=%async_computation.38 | async-start | bytes 5990400
  612.9 411.0 %reduce-scatter.27.cloned.1.call-start = ((), (), s32[]{:S(2)}) async-start(), calls=%async_computation.32 | async-start | bytes 1843200 | tf_op jit(solution)/shard_map/reduce_scatter | solution.py:349
  728.0 364.2 %reduce-scatter.23.cloned.1.call-start = ((), (), s32[]{:S(2)}) async-start(), calls=%async_computation.28 | async-start | bytes 1843200 | tf_op jit(solution)/shard_map/reduce_scatter | solution.py:349
  768.7 391.7 %reduce-scatter.25.cloned.1.call-start = ((), (), s32[]{:S(2)}) async-start(), calls=%async_computation.30 | async-start | bytes 1843200 | tf_op jit(solution)/shard_map/reduce_scatter | solution.py:349
  820.9 391.9 %all-gather.27.cloned.1.call-start = ((), (), s32[]{:S(2)}) async-start(), calls=%async_computation.35 | async-start | bytes 1916928 | tf_op jit(solution)/shard_map/all_gather | solution.py:338
  821.7 473.1 %all-gather.31.cloned.1.call-start = ((), (), s32[]{:S(2)}) async-start(), calls=%async_computation.37 | async-start | bytes 5990400 | tf_op jit(solution)/shard_map/all_gather | solution.py:338
  826.4 555.6 %all-gather.29.cloned.1.call-start = ((), (), s32[]{:S(2)}) async-start(), calls=%async_computation.36 | async-start | bytes 5990400 | tf_op jit(solution)/shard_map/all_gather | solution.py:356
  961.8 465.2 %all-gather.25.cloned.1.call-start = ((), (), s32[]{:S(2)}) async-start(), calls=%async_computation.33 | async-start | bytes 1843200 | tf_op jit(solution)/shard_map/all_gather | solution.py:356
  1027.4 444.9 %all-gather.21.cloned.1.call-start = ((), (), s32[]{:S(2)}) async-start(), calls=%async_computation.29 | async-start | bytes 1843200 | tf_op jit(solution)/shard_map/all_gather | solution.py:356
  1095.7 421.9 %all-gather.23.cloned.1.call-start = ((), (), s32[]{:S(2)}) async-start(), calls=%async_computation.31 | async-start | bytes 1843200 | tf_op jit(solution)/shard_map/all_gather | solution.py:356
  1163.8 393.3 %reduce-scatter.21.cloned.1.call-start = ((), (), s32[]{:S(2)}) async-start(), calls=%async_computation.27 | async-start | bytes 4096000 | tf_op jit(solution)/shard_map/reduce_scatter | solution.py:238
  1173.7 424.4 %reduce-scatter.17.cloned.1.call-start = ((), (), s32[]{:S(2)}) async-start(), calls=%async_computation.23 | async-start | bytes 4096000 | tf_op jit(solution)/shard_map/reduce_scatter | solution.py:238
  (52 other events, 689.1 us)
Sparse Core Ops, SparseCore 0:
  24.8 31.3 all-gather.12
  328.4 36.8 reduce-scatter.14
  368.6 31.8 all-gather.14
  401.9 47.5 all-gather.16
  509.2 38.5 reduce-scatter.18
  551.7 29.6 all-gather.18
  586.8 70.8 reduce-scatter.28
  661.1 165.1 reduce-scatter.32
  830.4 124.6 reduce-scatter.30
  959.0 64.9 reduce-scatter.26
  1027.4 64.7 reduce-scatter.22
  1095.5 64.7 reduce-scatter.24
  1162.5 44.5 all-gather.26
  1209.2 85.6 all-gather.30
  1296.9 85.0 all-gather.28
  1384.0 42.9 all-gather.24
  1429.1 43.1 all-gather.20
  1474.3 43.1 all-gather.22
  1520.1 36.9 reduce-scatter.20
  1559.5 38.4 reduce-scatter.16

commit v2 on v1

--- a/solution.py
+++ b/solution.py
@@ -190,6 +190,575 @@
     )(queries, keys, values, grad, ot, lse)
 
 
+class Place:
+    def __init__(self):
+        self.parts = lax.axis_size("fsdp")
+        self.n_ctx = lax.axis_size("ctx")
+        self.part = lax.axis_index("fsdp")
+        self.ctx = lax.axis_index("ctx")
+        self.beside = self.part + 1 - 2 * (self.part % 2)
+        self.far = (self.part + 2) % self.parts
+        self.diagonal = (self.beside + 2) % self.parts
+
+    def at(self, position):
+        n = self.n_ctx
+        position = (position + 2 * n) % n
+        upper = position // (n // 2)
+        return (1 - upper) * 2 * position + upper * (2 * (n - 1 - position) + 1)
+
+    @property
+    def position(self):
+        odd = self.ctx % 2
+        return (1 - odd) * (self.ctx // 2) + odd * (self.n_ctx - 1 - self.ctx // 2)
+
+
+def remote(source, target, send, recv, **where):
+    return pltpu.make_async_remote_copy(
+        src_ref=source,
+        dst_ref=target,
+        send_sem=send,
+        recv_sem=recv,
+        device_id=where,
+        device_id_type=pl.DeviceIdType.MESH,
+    )
+
+
+def cut(rows):
+    step = 64 if rows % 64 == 0 else rows
+    return [slice(start, start + step) for start in range(0, rows, step)]
+
+
+class Gather:
+    reach = ("fsdp",)
+
+    def __init__(self, array):
+        self.ins = [array]
+        self.parts = lax.axis_size("fsdp")
+        self.pieces = cut(array.shape[0])
+        self.outs = [jax.ShapeDtypeStruct((self.parts, *array.shape), array.dtype)]
+        self.scratch = [pltpu.SemaphoreType.DMA((3, len(self.pieces)))] * 2
+
+    def phases(self, place, ins, outs, scratch):
+        (source,), (out,), (send, recv) = ins, outs, scratch
+        count = range(len(self.pieces))
+
+        def copy(kind, k, index, target):
+            piece = self.pieces[k]
+            start = source.at[piece] if kind < 2 else out.at[index, piece]
+            return remote(start, out.at[index, piece], send.at[kind, k], recv.at[kind, k], fsdp=target)
+
+        def first():
+            for k in count:
+                copy(1, k, place.part, place.far).start()
+            for k in count:
+                copy(0, k, place.part, place.beside).start()
+            out[place.part] = source[...]
+
+        def second():
+            for k in count:
+                copy(1, k, place.far, place.far).wait_recv()
+                copy(2, k, place.far, place.beside).start()
+
+        def third():
+            for k in count:
+                copy(0, k, place.beside, place.beside).wait_recv()
+                copy(2, k, place.diagonal, place.beside).wait_recv()
+            for k in count:
+                copy(0, k, place.part, place.beside).wait_send()
+                copy(1, k, place.part, place.far).wait_send()
+                copy(2, k, place.far, place.beside).wait_send()
+
+        return [first, second, third]
+
+
+class Scatter:
+    reach = ("fsdp",)
+
+    def __init__(self, array):
+        parts, rows, columns = array.shape
+        self.ins = [array]
+        self.pieces = cut(rows)
+        self.outs = [jax.ShapeDtypeStruct((rows, columns), F32)]
+        self.scratch = [pltpu.VMEM((rows, columns), array.dtype)] * 3
+        self.scratch += [pltpu.SemaphoreType.DMA((3, len(self.pieces)))] * 2
+
+    def phases(self, place, ins, outs, scratch):
+        (source,), (out,) = ins, outs
+        for_far, for_own, from_far, send, recv = scratch
+        count = range(len(self.pieces))
+
+        def copy(kind, k):
+            piece = self.pieces[k]
+            start, target, where = [
+                (source.at[place.diagonal, piece], for_far, place.beside),
+                (source.at[place.beside, piece], for_own, place.beside),
+                (for_far.at[piece], from_far, place.far),
+            ][kind]
+            return remote(start, target.at[piece], send.at[kind, k], recv.at[kind, k], fsdp=where)
+
+        def first():
+            for k in count:
+                copy(0, k).start()
+            for k in count:
+                copy(1, k).start()
+
+        def second():
+            for k in count:
+                piece = self.pieces[k]
+                copy(0, k).wait_recv()
+                total = for_far[piece].astype(F32) + source[place.far, piece].astype(F32)
+                for_far[piece] = total.astype(for_far.dtype)
+                copy(2, k).start()
+
+        def third():
+            for k in count:
+                piece = self.pieces[k]
+                copy(1, k).wait_recv()
+                out[piece] = for_own[piece].astype(F32) + source[place.part, piece].astype(F32)
+
+        def fourth():
+            for k in count:
+                piece = self.pieces[k]
+                copy(2, k).wait_recv()
+                out[piece] += from_far[piece].astype(F32)
+            for k in count:
+                for kind in range(3):
+                    copy(kind, k).wait_send()
+
+        return [first, second, third, fourth]
+
+
+class ToHeads:
+    reach = ("ctx",)
+
+    def __init__(self, arrays):
+        seqs, _, half, columns = arrays[0].shape
+        self.n = lax.axis_size("ctx")
+        self.groups = self.n // seqs
+        self.piece = columns // self.groups
+        self.ins = list(arrays)
+        self.outs = [jax.ShapeDtypeStruct((2 * self.n, half, self.piece), a.dtype) for a in arrays]
+        self.scratch = [pltpu.SemaphoreType.DMA((len(arrays), 2, self.n))] * 2
+
+    def whole(self, ref, other, half):
+        if self.groups == 1:
+            return ref.at[other, half]
+        column = pl.multiple_of((other % self.groups) * self.piece, LANES)
+        return ref.at[other // self.groups, half, :, pl.ds(column, self.piece)]
+
+    def block(self, ref, other, half):
+        return ref.at[other if half == 0 else 2 * self.n - 1 - other]
+
+    def source(self, ref, other, half):
+        return self.whole(ref, other, half)
+
+    def target(self, ref, other, half):
+        return self.block(ref, other, half)
+
+    def phases(self, place, ins, outs, scratch):
+        send, recv = scratch
+        n, me = self.n, place.ctx
+        every = [(i, half) for i in range(len(ins)) for half in range(2)]
+
+        def first():
+            def begin(step, _):
+                other = (me + step) % n
+                for i, half in every:
+                    remote(
+                        self.source(ins[i], other, half),
+                        self.target(outs[i], me, half),
+                        send.at[i, half, step],
+                        recv.at[i, half, step],
+                        ctx=other,
+                    ).start()
+                return 0
+
+            lax.fori_loop(1, n, begin, 0)
+            for i, half in every:
+                self.target(outs[i], me, half)[...] = self.source(ins[i], me, half)[...]
+
+        def second():
+            def end(step, _):
+                other = (me + n - step) % n
+                for i, half in every:
+                    copy = remote(
+                        self.source(ins[i], other, half),
+                        self.target(outs[i], other, half),
+                        send.at[i, half, step],
+                        recv.at[i, half, step],
+                        ctx=other,
+                    )
+                    copy.wait_recv()
+                    copy.wait_send()
+                return 0
+
+            lax.fori_loop(1, n, end, 0)
+
+        return [first, second]
+
+
+class FromHeads(ToHeads):
+    def __init__(self, arrays, seqs):
+        blocks, half, piece = arrays[0].shape
+        self.n = blocks // 2
+        self.groups = self.n // seqs
+        self.piece = piece
+        self.ins = list(arrays)
+        shape = (seqs, 2, half, piece * self.groups)
+        self.outs = [jax.ShapeDtypeStruct(shape, a.dtype) for a in arrays]
+        self.scratch = [pltpu.SemaphoreType.DMA((len(arrays), 2, self.n))] * 2
+
+    def source(self, ref, other, half):
+        return self.block(ref, other, half)
+
+    def target(self, ref, other, half):
+        return self.whole(ref, other, half)
+
+
+class Swap:
+    reach = ("fsdp",)
+
+    def __init__(self, arrays, live, wide):
+        self.parts = lax.axis_size("fsdp")
+        self.live, self.wide = live, wide
+        self.ins = list(arrays)
+        rows = arrays[0].shape[0]
+        shape = (len(arrays), self.parts, rows, wide)
+        self.outs = [jax.ShapeDtypeStruct(shape, arrays[0].dtype)]
+        self.scratch = [pltpu.VMEM(shape, arrays[0].dtype)]
+        self.scratch += [pltpu.SemaphoreType.DMA((len(arrays), self.parts))] * 2
+
+    def phases(self, place, ins, outs, scratch):
+        (out,), (stage, send, recv) = outs, scratch
+        parts, live = self.parts, self.live
+        every = [(i, step) for step in (2, 3, 1) for i in range(len(ins))]
+
+        def copy(i, step, index):
+            other = (place.part + step) % parts
+            return remote(
+                stage.at[i, other], out.at[i, index], send.at[i, step], recv.at[i, step], fsdp=other
+            )
+
+        def first():
+            for i, ref in enumerate(ins):
+                for part in range(parts):
+                    start = part * live
+                    stop = min(start + live, ref.shape[1])
+                    stage[i, part, :, : stop - start] = ref[:, start:stop]
+                    if stop - start < self.wide:
+                        shape = (ref.shape[0], self.wide - stop + start)
+                        stage[i, part, :, stop - start :] = jnp.zeros(shape, ref.dtype)
+            for i, step in every:
+                copy(i, step, place.part).start()
+            for i in range(len(ins)):
+                out[i, place.part] = stage[i, place.part]
+
+        def second():
+            for i, step in every:
+                copy(i, step, (place.part + parts - step) % parts).wait_recv()
+                copy(i, step, place.part).wait_send()
+
+        return [first, second]
+
+
+class Window:
+    reach = ("fsdp",)
+
+    def __init__(self, array, live, wide):
+        self.parts = lax.axis_size("fsdp")
+        self.quarter, columns = array.shape
+        self.live, self.wide = live, wide
+        self.near = (live - self.quarter) * self.parts
+        self.ins = [array]
+        self.outs = [jax.ShapeDtypeStruct((wide, columns), array.dtype)]
+        self.scratch = [pltpu.VMEM((self.quarter + self.near, columns), array.dtype)]
+        self.scratch += [pltpu.SemaphoreType.DMA] * 2
+
+    def phases(self, place, ins, outs, scratch):
+        (source,), (out,), (both, send, recv) = ins, outs, scratch
+        left = (place.part + self.parts - 1) % self.parts
+        copy = remote(
+            source.at[: self.near], both.at[self.quarter :], send, recv, fsdp=left
+        )
+
+        def first():
+            copy.start()
+            both[: self.quarter] = source[...]
+
+        def second():
+            copy.wait()
+            start = pl.multiple_of(place.part * (self.live - self.quarter), 16)
+            rows = both[pl.ds(start, self.live), :]
+            index = lax.broadcasted_iota(jnp.int32, rows.shape, 0) + place.part * self.live
+            inside = index < self.quarter * self.parts
+            out[: self.live] = jnp.where(inside, rows, jnp.zeros_like(rows))
+            if self.wide > self.live:
+                out[self.live :] = jnp.zeros((self.wide - self.live, rows.shape[1]), rows.dtype)
+
+        return [first, second]
+
+
+class Total:
+    reach = ("ctx",)
+
+    def __init__(self, array):
+        self.n = lax.axis_size("ctx")
+        self.ins = [array]
+        self.outs = [jax.ShapeDtypeStruct(array.shape, F32)]
+        self.scratch = [pltpu.VMEM((self.n, *array.shape), array.dtype)]
+        self.scratch += [pltpu.SemaphoreType.DMA((self.n,))] * 2
+
+    def phases(self, place, ins, outs, scratch):
+        (source,), (out,), (held, send, recv) = ins, outs, scratch
+        n, me = self.n, place.ctx
+
+        def copy(step, index):
+            return remote(source, held.at[index], send.at[step], recv.at[step], ctx=(me + step) % n)
+
+        def first():
+            lax.fori_loop(1, n, lambda step, _: (copy(step, me).start(), 0)[1], 0)
+            held[me] = source[...]
+
+        def last():
+            def end(step, _):
+                copy(step, (me + n - step) % n).wait_recv()
+                copy(step, me).wait_send()
+                return 0
+
+            lax.fori_loop(1, n, end, 0)
+            total = held[0].astype(F32)
+            for i in range(1, n):
+                total = total + held[i].astype(F32)
+            out[...] = total
+
+        return [first, last]
+
+
+class Ring:
+    reach = ("ring", "fsdp")
+
+    def __init__(self, streams):
+        self.n = lax.axis_size("ctx")
+        self.parts = lax.axis_size("fsdp")
+        self.per = self.n // self.parts
+        self.streams = []
+        self.ins, self.outs, self.scratch = [], [], []
+        for array, direction, crossing in streams:
+            n, rows, columns = array.shape
+            self.ins.append(array)
+            self.outs.append(jax.ShapeDtypeStruct(array.shape, array.dtype))
+            self.scratch.append(pltpu.VMEM((n - 1, rows, columns), array.dtype))
+            middle = (columns // 2 + LANES - 1) // LANES * LANES
+            for low, high in ((0, middle), (middle, columns)):
+                self.streams.append((len(self.ins) - 1, direction, crossing, slice(low, high)))
+        self.scratch += [pltpu.SemaphoreType.DMA((len(self.streams), 2, self.n))] * 2
+
+    def phases(self, place, ins, outs, scratch):
+        slots, (send, recv) = scratch[:-2], scratch[-2:]
+        n, parts, per, here = self.n, self.parts, self.per, place.position
+        shift = place.ctx // per
+        owner = (place.part + shift) % parts
+
+        def slab(stream, position):
+            index = place.at(position)
+            return (index + per * place.part) % n if self.streams[stream][2] else index
+
+        def reducing(stream, step):
+            array, direction, _, columns = self.streams[stream]
+            if step == 0:
+                source = ins[array].at[slab(stream, here - direction), :, columns]
+            else:
+                source = slots[array].at[step - 1, :, columns]
+            return remote(
+                source,
+                slots[array].at[step, :, columns],
+                send.at[stream, 0, step],
+                recv.at[stream, 0, step],
+                ctx=place.at(here + direction),
+            )
+
+        def crossing(stream):
+            array, _, _, columns = self.streams[stream]
+            return remote(
+                slots[array].at[n - 2, :, columns],
+                outs[array].at[place.ctx, :, columns],
+                send.at[stream, 0, n - 1],
+                recv.at[stream, 0, n - 1],
+                fsdp=owner,
+            )
+
+        def gathering(stream, step, back=0):
+            array, direction, _, columns = self.streams[stream]
+            index = place.at(here - direction * (step + back))
+            return remote(
+                outs[array].at[index, :, columns],
+                outs[array].at[index, :, columns],
+                send.at[stream, 1, step],
+                recv.at[stream, 1, step],
+                ctx=place.at(here + direction),
+            )
+
+        every = range(len(self.streams))
+
+        def begin():
+            for stream in every:
+                reducing(stream, 0).start()
+
+        def add(stream, step):
+            array, direction, _, columns = self.streams[stream]
+            reducing(stream, step).wait_recv()
+            own = ins[array][slab(stream, here - direction * (step + 2)), :, columns]
+            return (slots[array][step, :, columns].astype(F32) + own.astype(F32)).astype(own.dtype)
+
+        def reduce(step):
+            for stream in every:
+                array, _, _, columns = self.streams[stream]
+                slots[array][step - 1, :, columns] = add(stream, step - 1)
+                reducing(stream, step).start()
+
+        def turn():
+            for stream in every:
+                array, _, crosses, columns = self.streams[stream]
+                total = add(stream, n - 2)
+                if not crosses:
+                    outs[array][place.ctx, :, columns] = total
+                    gathering(stream, 0).start()
+                    continue
+
+                @pl.when(shift == 0)
+                def _():
+                    outs[array][place.ctx, :, columns] = total
+
+                @pl.when(shift != 0)
+                def _():
+                    slots[array][n - 2, :, columns] = total
+                    crossing(stream).start()
+
+        def launch():
+            for stream in every:
+                if self.streams[stream][2]:
+
+                    @pl.when(shift != 0)
+                    def _():
+                        crossing(stream).wait()
+
+                    gathering(stream, 0).start()
+
+        def forward(step):
+            for stream in every:
+                gathering(stream, step - 1, 1).wait_recv()
+                gathering(stream, step).start()
+
+        def end():
+            for stream in every:
+                gathering(stream, n - 2, 1).wait_recv()
+            for stream in every:
+                for step in range(n - 1):
+                    reducing(stream, step).wait_send()
+                    gathering(stream, step).wait_send()
+
+        steps = [begin]
+        steps += [functools.partial(reduce, step) for step in range(1, n - 1)]
+        steps += [turn, launch]
+        steps += [functools.partial(forward, step) for step in range(1, n - 1)]
+        return steps + [end]
+
+
+def exchange_kernel(transfers, *refs):
+    refs = list(refs)
+
+    def take(lists):
+        taken = []
+        for items in lists:
+            taken.append(refs[: len(items)])
+            del refs[: len(items)]
+        return taken
+
+    ins = take([t.ins for t in transfers])
+    outs = take([t.outs for t in transfers])
+    scratch = take([t.scratch for t in transfers])
+    place = Place()
+    reach = {name for t in transfers for name in t.reach}
+    peers = []
+    if "fsdp" in reach:
+        peers += [dict(fsdp=(place.part + k) % place.parts) for k in range(1, place.parts)]
+    if "ctx" in reach:
+        peers += [dict(ctx=(place.ctx + k) % place.n_ctx) for k in range(1, place.n_ctx)]
+    if "ring" in reach:
+        peers += [dict(ctx=place.at(place.position + k)) for k in (1, -1)]
+    barrier = pltpu.get_barrier_semaphore()
+    for peer in peers:
+        pl.semaphore_signal(barrier, inc=1, device_id=peer, device_id_type=pl.DeviceIdType.MESH)
+    pl.semaphore_wait(barrier, len(peers))
+    lists = [t.phases(place, *each) for t, *each in zip(transfers, ins, outs, scratch)]
+    for index in range(max(map(len, lists))):
+        for phases in lists:
+            if index < len(phases):
+                phases[index]()
+
+
+def exchange(number, name, *transfers):
+    memory = pl.BlockSpec(memory_space=pltpu.VMEM)
+    ins = [a for t in transfers for a in t.ins]
+    outs = [a for t in transfers for a in t.outs]
+    results = pl.pallas_call(
+        functools.partial(exchange_kernel, transfers),
+        out_shape=outs,
+        in_specs=[memory] * len(ins),
+        out_specs=[memory] * len(outs),
+        scratch_shapes=[s for t in transfers for s in t.scratch],
+        compiler_params=pltpu.CompilerParams(collective_id=number, has_side_effects=True),
+        name=name,
+    )(*ins)
+    results = list(results)
+    split = []
+    for t in transfers:
+        split.append(results[: len(t.outs)])
+        del results[: len(t.outs)]
+    return split
+
+
+def results_kernel(widths, parts, order_ref, *refs):
+    for index, (live, total) in enumerate(widths):
+        out = refs[len(widths) * parts + index]
+        for part in range(parts):
+            stop = min((part + 1) * live, total)
+            block = refs[index * parts + part][0, :, : stop - part * live]
+            out[:, part * live : stop] = block.astype(F32)
+
+
+def by_rows(arrays, widths, per, part, parts):
+    slabs, rows, _ = arrays[0].shape
+    order = (part - jnp.arange(parts, dtype=jnp.int32) + parts) % parts
+    if rows % 8:
+        outs = []
+        for array, (live, total) in zip(arrays, widths):
+            array = jnp.take(array.reshape(parts, per, rows, -1), order, axis=0)[..., :live]
+            array = jnp.transpose(array, (1, 2, 0, 3)).reshape(per * rows, parts * live)
+            outs.append(array[:, :total].astype(F32))
+        return outs
+    step = 40 if rows % 40 == 0 else rows
+    inner = rows // step
+
+    def source(column, array):
+        return pl.BlockSpec(
+            (1, step, array.shape[2]),
+            lambda i, order: (order[column] * per + i // inner, i % inner, 0),
+        )
+
+    return pl.pallas_call(
+        functools.partial(results_kernel, widths, parts),
+        out_shape=[jax.ShapeDtypeStruct((per * rows, total), F32) for _, total in widths],
+        grid_spec=pltpu.PrefetchScalarGridSpec(
+            num_scalar_prefetch=1,
+            grid=(per * inner,),
+            in_specs=[source(column, array) for array in arrays for column in range(parts)],
+            out_specs=[pl.BlockSpec((step, total), lambda i, order: (i, 0)) for _, total in widths],
+        ),
+        name="by_rows",
+    )(order, *[array for array in arrays for _ in range(parts)])
+
+
 def on_device(
     inputs,
     cotangent,
@@ -211,7 +780,6 @@
 ):
     parts = lax.axis_size("fsdp")
     n_ctx = lax.axis_size("ctx")
-    me_ctx = lax.axis_index("ctx")
     me_part = lax.axis_index("fsdp")
     seqs, rows, width = inputs.shape
     hidden = w_fc.shape[1]
@@ -230,78 +798,81 @@
     piece = cols // groups
     heads_here = heads_part if groups == 1 else slots // groups
     near = (live - quarter) * parts
-
-    def gather(array):
-        return lax.all_gather(array, "fsdp", axis=0, tiled=True)
-
-    def scatter(array):
-        return lax.psum_scatter(array.astype(BF16), "fsdp", scatter_dimension=0, tiled=True)
-
-    def to_slots(array):
-        lead = array.shape[:-1]
-        array = jnp.pad(array, [(0, 0)] * len(lead) + [(0, parts * live - width)])
-        array = array.reshape(*lead, parts, live)
-        array = jnp.pad(array, [(0, 0)] * len(lead) + [(0, 0), (0, cols - live)])
-        return array.reshape(*lead, parts * cols)
+    per = n_ctx // parts
+    slab = width // n_ctx
+
+    def to_slots(vector):
+        vector = jnp.pad(vector, (0, parts * live - width)).reshape(parts, live)
+        return jnp.pad(vector, ((0, 0), (0, cols - live)))[me_part]
+
+    def by_parts(array):
+        return array.astype(BF16).reshape(parts, own, width)
+
+    def by_sequences(array):
+        return array.reshape(all_seqs, 2, half_rows, cols)
+
+    def by_slabs(array, count):
+        return array.astype(BF16).reshape(count, -1, array.shape[1])
 
     small = jnp.concatenate(
         [ln1_gain, ln1_bias, query_bias, value_bias, out_bias, ln2_gain, ln2_bias, proj_bias]
     )[None, :]
-    small = gather(small).astype(F32).reshape(parts, 8, quarter)
+    small = lax.all_gather(small, "fsdp", axis=0, tiled=True).astype(F32).reshape(parts, 8, quarter)
     gain_one, shift_one, bias_query, bias_value, bias_out, gain_two, shift_two, bias_proj = [
         small[:, i].reshape(-1) for i in range(8)
     ]
-    bias_query = lax.dynamic_slice_in_dim(to_slots(bias_query), me_part * cols, cols, 0)
-    bias_value = lax.dynamic_slice_in_dim(to_slots(bias_value), me_part * cols, cols, 0)
+    bias_query, bias_value = to_slots(bias_query), to_slots(bias_value)
     bias_fc = fc_bias.astype(F32)
-
-    qkv = to_slots(jnp.stack([w_query, w_key, w_value]))
-    qkv = lax.all_to_all(qkv, "fsdp", split_axis=2, concat_axis=1, tiled=True)
-    fc = lax.all_to_all(w_fc, "fsdp", split_axis=1, concat_axis=0, tiled=True)
-    proj = w_proj
-    from_right = lax.ppermute(w_out[:near], "fsdp", [(i + 1, i) for i in range(parts - 1)])
-    out_w = lax.dynamic_slice_in_dim(
-        jnp.concatenate([w_out, from_right]), me_part * (live - quarter), live, 0
-    )
-    out_w = jnp.pad(out_w, ((0, cols - live), (0, 0)))
 
     x_full = inputs.astype(F32).reshape(own, width)
     hat_one, inv_one = normalize(x_full)
-    normed_one = gather((hat_one * gain_one + shift_one).astype(BF16))
-    grad_y = gather(cotangent.reshape(own, width))
+    (qkv,), (out_w,), (normed_one,) = exchange(
+        0,
+        "start",
+        Swap([w_query, w_key, w_value], live, cols),
+        Window(w_out, live, cols),
+        Gather((hat_one * gain_one + shift_one).astype(BF16)),
+    )
+    qkv = qkv.reshape(3, width, cols)
+    normed_one = normed_one.reshape(tokens, width)
     queries = (dot(normed_one, qkv[0]) + bias_query).astype(BF16)
     keys = dot(normed_one, qkv[1]).astype(BF16)
     values = (dot(normed_one, qkv[2]) + bias_value).astype(BF16)
-
-    def to_heads(array):
-        array = array.reshape(all_seqs, rows, groups, piece)
-        array = jnp.transpose(array, (0, 2, 1, 3)).reshape(n_ctx, rows, piece)
-        array = lax.all_to_all(array, "ctx", split_axis=0, concat_axis=0, tiled=True)
-        first, second = array[:, :half_rows], array[:, half_rows:]
-        return jnp.concatenate([first, second[::-1]]).reshape(length, piece)
-
-    def from_heads(array):
-        array = array.reshape(2 * n_ctx, half_rows, piece)
-        array = jnp.concatenate([array[:n_ctx], array[n_ctx:][::-1]], axis=1)
-        array = lax.all_to_all(array, "ctx", split_axis=0, concat_axis=0, tiled=True)
-        array = array.reshape(all_seqs, groups, rows, piece)
-        return jnp.transpose(array, (0, 2, 1, 3)).reshape(tokens, cols)
-
-    q_seq, k_seq, v_seq = to_heads(queries), to_heads(keys), to_heads(values)
+    heads, (fc,), (grad_y,) = exchange(
+        1,
+        "to_heads",
+        ToHeads([by_sequences(a) for a in (queries, keys, values)]),
+        Swap([w_fc], hidden_part, hidden_part),
+        Gather(cotangent.reshape(own, width)),
+    )
+    fc = fc.reshape(width, hidden_part)
+    grad_y = grad_y.reshape(tokens, width)
+    proj = w_proj
+
+    q_seq, k_seq, v_seq = [a.reshape(length, piece) for a in heads]
     o_seq, ot, lse = attend(q_seq, k_seq, v_seq, heads_here)
-    attended = from_heads(o_seq)
-    resid = x_full + scatter(dot(attended, out_w)).astype(F32) + bias_out
+
+    def blocks(array):
+        return array.reshape(2 * n_ctx, half_rows, piece)
+
+    (attended,) = exchange(2, "from_heads", FromHeads([blocks(o_seq)], all_seqs))[0]
+    attended = attended.reshape(tokens, cols)
+    (branch,) = exchange(3, "branch", Scatter(by_parts(dot(attended, out_w))))[0]
+    resid = x_full + branch + bias_out
 
     hat_two, inv_two = normalize(resid)
-    normed_two = gather((hat_two * gain_two + shift_two).astype(BF16))
+    (normed_two,) = exchange(4, "second", Gather((hat_two * gain_two + shift_two).astype(BF16)))[0]
+    normed_two = normed_two.reshape(tokens, width)
     pre_act = dot(normed_two, fc) + bias_fc
     value, slope = gelu_both(pre_act)
     activated = value.astype(BF16)
-    mlp = scatter(dot(activated, proj)).astype(F32)
+    mlp = by_parts(dot(activated, proj))
+
+    grad_pre = (dot_nt(grad_y, proj) * slope).astype(BF16)
+    (grad_norm_two,), (mlp,) = exchange(
+        5, "second_back", Scatter(by_parts(dot_nt(grad_pre, fc))), Scatter(mlp)
+    )
     outputs = (resid + mlp + bias_proj).astype(BF16).reshape(seqs, rows, width)
-
-    grad_pre = (dot_nt(grad_y, proj) * slope).astype(BF16)
-    grad_norm_two = scatter(dot_nt(grad_pre, fc)).astype(F32)
     grad_y_own = cotangent.reshape(own, width).astype(F32)
     grad_gain_two = jnp.sum(grad_norm_two * hat_two, axis=0)
     grad_shift_two = jnp.sum(grad_norm_two, axis=0)
@@ -310,65 +881,37 @@
     grad_resid = grad_y_own + norm_back(grad_norm_two, gain_two, hat_two, inv_two)
     grad_branch = grad_resid.astype(BF16)
     grad_bias_out = jnp.sum(grad_branch.astype(F32), axis=0)
-    grad_branch = gather(grad_branch)
+    proj_part = by_slabs(dot_tn(activated, grad_y), n_ctx)
+    fc_part = by_slabs(dot_tn(normed_two, grad_pre), n_ctx)
+    (proj_grad, fc_grad), (grad_branch,) = exchange(
+        6, "wide_grads", Ring([(proj_part, 1, False), (fc_part, -1, True)]), Gather(grad_branch)
+    )
+    grad_branch = grad_branch.reshape(tokens, width)
     grad_attended = dot_nt(grad_branch, out_w).astype(BF16)
 
+    ((grad_heads,),) = exchange(7, "to_heads_back", ToHeads([by_sequences(grad_attended)]))
     dq_seq, dk_seq, dv_seq = attend_back(
-        q_seq, k_seq, v_seq, to_heads(grad_attended), ot, lse, heads_here
-    )
-    grad_qkv = jnp.stack([from_heads(dq_seq), from_heads(dk_seq), from_heads(dv_seq)])
-    grad_norm_one = scatter(
-        dot_nt(grad_qkv[0], qkv[0]) + dot_nt(grad_qkv[1], qkv[1]) + dot_nt(grad_qkv[2], qkv[2])
-    ).astype(F32)
+        q_seq, k_seq, v_seq, grad_heads.reshape(length, piece), ot, lse, heads_here
+    )
+    (grad_qkv,) = exchange(
+        8, "from_heads_back", FromHeads([blocks(a) for a in (dq_seq, dk_seq, dv_seq)], all_seqs)
+    )
+    grad_qkv = [a.reshape(tokens, cols) for a in grad_qkv]
+    ((grad_norm_one,),) = exchange(
+        9,
+        "first_back",
+        Scatter(
+            by_parts(
+                dot_nt(grad_qkv[0], qkv[0]) + dot_nt(grad_qkv[1], qkv[1]) + dot_nt(grad_qkv[2], qkv[2])
+            )
+        ),
+    )
     grad_bias_query = jnp.sum(grad_qkv[0].astype(F32), axis=0)
     grad_bias_value = jnp.sum(grad_qkv[2].astype(F32), axis=0)
     grad_gain_one = jnp.sum(grad_norm_one * hat_one, axis=0)
     grad_shift_one = jnp.sum(grad_norm_one, axis=0)
     input_grad = grad_resid + norm_back(grad_norm_one, gain_one, hat_one, inv_one)
     input_grad = input_grad.reshape(seqs, rows, width)
-
-    per = n_ctx // parts
-    slab = width // n_ctx
-    proj_part = dot_tn(activated, grad_y).astype(BF16)
-    fc_part = dot_tn(normed_two, grad_pre).astype(BF16)
-    qkv_part = [dot_tn(normed_one, grad_qkv[i]).astype(BF16) for i in range(3)]
-    out_part = dot_tn(attended, grad_branch).astype(BF16)
-
-    def total(array):
-        return lax.all_gather(
-            lax.psum_scatter(array, "ctx", scatter_dimension=0, tiled=True), "ctx", axis=0, tiled=True
-        )
-
-    proj_grad = total(proj_part).astype(F32)
-    out_grad = total(out_part)
-
-    def across(array):
-        n = array.shape[1]
-        array = array.reshape(n_ctx, slab, n)
-        array = jnp.roll(array, -per * me_part, axis=0)
-        array = lax.psum_scatter(array, "ctx", scatter_dimension=0, tiled=True)
-        pairs = [
-            (c * parts + f, c * parts + (f + c // per) % parts)
-            for c in range(n_ctx)
-            for f in range(parts)
-        ]
-        array = lax.ppermute(array, ("ctx", "fsdp"), pairs)
-        array = lax.all_gather(array, "ctx", axis=0, tiled=True)
-        array = array.reshape(parts, per, slab, n)
-        order = (me_part - jnp.arange(parts)) % parts
-        array = jnp.take(array, order, axis=0)
-        return jnp.transpose(array, (1, 2, 0, 3)).reshape(quarter, parts, n)
-
-    fc_grad = across(fc_part).reshape(quarter, hidden).astype(F32)
-    qkv_grad = [
-        across(part)[:, :, :live].reshape(quarter, parts * live)[:, :width].astype(F32)
-        for part in qkv_part
-    ]
-    out_rows = out_grad[:live]
-    from_left = lax.ppermute(out_rows[live - near :], "fsdp", [(i, i + 1) for i in range(parts - 1)])
-    out_rows = lax.dynamic_slice_in_dim(
-        jnp.concatenate([from_left, out_rows]), near - me_part * (live - quarter), quarter, 0
-    ).astype(F32)
 
     def window(vector):
         whole = jnp.zeros((parts * live,), F32)
@@ -386,18 +929,39 @@
             grad_bias_proj,
         ]
     )
-    small_grads = lax.psum(small_grads, ("ctx", "fsdp"))
-    small_grads = lax.dynamic_slice_in_dim(small_grads, me_part * quarter, quarter, 1)
-    fc_bias_grad = lax.psum(grad_bias_fc, "ctx")
+    small_grads = jnp.transpose(small_grads.reshape(8, parts, quarter), (1, 0, 2))
+    ((small_grads,),) = exchange(10, "small", Scatter(small_grads))
+    small_grads = jnp.concatenate([small_grads, grad_bias_fc.reshape(-1, quarter)])
+
+    q_part, k_part, v_part = [by_slabs(dot_tn(normed_one, a), n_ctx) for a in grad_qkv]
+    out_part = by_slabs(dot_tn(attended, grad_branch), n_ctx)
+    (out_grad, q_grad, k_grad, v_grad), (small_grads,) = exchange(
+        11,
+        "narrow_grads",
+        Ring([(out_part, 1, False), (q_part, 1, True), (k_part, -1, True), (v_part, -1, True)]),
+        Total(small_grads),
+    )
+    fc_out, q_out, k_out, v_out = by_rows(
+        [fc_grad, q_grad, k_grad, v_grad],
+        [(hidden_part, hidden)] + [(live, width)] * 3,
+        per,
+        me_part,
+        parts,
+    )
+    out_rows = out_grad.reshape(cols, width)[:live]
+    from_left = lax.ppermute(out_rows[live - near :], "fsdp", [(i, i + 1) for i in range(parts - 1)])
+    out_rows = lax.dynamic_slice_in_dim(
+        jnp.concatenate([from_left, out_rows]), near - me_part * (live - quarter), quarter, 0
+    ).astype(F32)
     return (
         outputs,
         input_grad,
-        qkv_grad[0],
-        qkv_grad[1],
-        qkv_grad[2],
+        q_out,
+        k_out,
+        v_out,
         out_rows,
-        fc_grad,
-        proj_grad,
+        fc_out,
+        proj_grad.reshape(hidden_part, width).astype(F32),
         small_grads[0],
         small_grads[1],
         small_grads[2],
@@ -405,7 +969,7 @@
         small_grads[4],
         small_grads[5],
         small_grads[6],
-        fc_bias_grad,
+        small_grads[8:].reshape(-1),
         small_grads[7],
     )
 

time: 1660 us -> 1060 us (0.64)
  waiting for transfers between devices: 978 us -> 0.01 us
  Pallas kernels: 34.5 us -> 863 us
  blocking collectives: 228 us -> 6.24 us
  local copies, waits for them, and re-layouts: 162 us -> 44.4 us
  starting transfers between devices: 49.9 us -> 2.18 us
  other arithmetic: 72.6 us -> 28.4 us
    pallas_call x0 -> x13, Pallas kernels: none -> 829 us  [the longest x12 815 us: exchange(): pl.pallas_call(functools.partial(exchange_kernel, transfers), out_shape=o...]
    reduce_scatter x8 -> x0, waiting for transfers between devices: 306 us -> none  [the longest x3 191 us: across(): array = lax.psum_scatter(array, 'ctx', scatter_dimension=0, tiled=True)]
    all_gather x10 -> x0, waiting for transfers between devices: 284 us -> none  [the longest x4 180 us: across(): array = lax.all_gather(array, 'ctx', axis=0, tiled=True)]
    all_to_all x6 -> x0, waiting for transfers between devices: 250 us -> none  [the longest x1 93 us: on_device(): qkv = lax.all_to_all(qkv, 'fsdp', split_axis=2, concat_axis=1, tiled=True)]
    all_to_all x4 -> x0, blocking collectives: 159 us -> none  [the longest x3 122 us: from_heads(): lax.all_to_all(array, 'ctx', split_axis=0, concat_axis=0, tiled=True)]
    unnamed x22 -> x0, waiting for transfers between devices: 134 us -> none
    psum x2 -> x0, blocking collectives: 63 us -> none  [the longest x1 39.8 us: on_device(): small_grads = lax.psum(small_grads, ('ctx', 'fsdp'))]
    all_to_all x3 -> x0, local copies, waits for them, and re-layouts: 30.9 us -> none  [the longest x2 17.3 us: on_device(): fc = lax.all_to_all(w_fc, 'fsdp', split_axis=1, concat_axis=0, tiled=True)]
  transfers between devices with their start and end apart: 32 -> 1, of which waited for: 22 -> 0; matrix products, arithmetic and copies ran while one was open for 15% -> 1% of each run, Pallas kernels for 1% -> 1%
where the time goes in v2:
time: 1060 us; the launch traced here: 1050 us
  Pallas kernels  863 us (81%)
  matrix products  103 us (10%)
  local copies, waits for them, and re-layouts  44.4 us (4%)
  other arithmetic  28.4 us (3%)
    pallas_call x12, Pallas kernels, exchange(): pl.pallas_call(functools.partial(exchange_kernel, transfers), out_shape=o...  815 us
    dot_general x6, matrix products, dot(): return jnp.dot(left, right, preferred_element_type=F32)  38.8 us
    dot_general x6, matrix products, dot_nt(): lax.dot_general(left, right, (((1,), (1,)), ((), ())), preferred_element_...  33.5 us
    dot_general x6, matrix products, dot_tn(): lax.dot_general(left, right, (((0,), (0,)), ((), ())), preferred_element_...  30.7 us
    convert_element_type x4, local copies, waits for them, and re-layouts, by_parts(): return array.astype(BF16).reshape(parts, own, width)  22.2 us
  transfers between devices with their start and end apart: 1, of which 0 were waited for; matrix products, arithmetic and copies ran while one was open for 1% of the time, Pallas kernels for 1%

profile of v2, /device:TPU:0, one launch (start us, length us, event | category | flops | bytes accessed | tf_op | source)
XLA Modules:
  0.0 1049.3 jit_solution(2664736190217335571)
XLA Ops:
  3.9 6.2 all-gather.1
  12.3 90.0 %start.1 = (bf16[3,4,400,512]{3,2,1,0:T(8,128)(2,1)}, bf16[512,1600]{1,0:T(8,128)(2,1)}, bf16[4,256,1600]{2,1,0:T(8,128)(2,1)}) custom-call(bf16[400,1600]{1,0:T(8,128)(2,1)} %refs_0_.1, bf16[400,1600]{1,0:T(8,128)(2,1)} %refs_1_.1, bf16[400,1600]{1,0:T(8,128)(2,1)} %refs_2_.1, bf16[400,1600]{1,0:T(8,128)(2,1)} %refs_3_.2, ...), custom_call_target="tpu_custom_call" | custom-call | tf_op jit(solution)/shard_map/start/pallas_call | solution.py:704
  110.0 5.6 convolution_convert_fusion.10
  121.7 93.8 %to_heads.1 = (bf16[16,64,512]{2,1,0:T(8,128)(2,1)}, bf16[16,64,512]{2,1,0:T(8,128)(2,1)}, bf16[16,64,512]{2,1,0:T(8,128)(2,1)}, bf16[1,4,400,1600]{3,2,1,0:T(8,128)(2,1)}, bf16[4,256,1600]{2,1,0:T(8,128)(2,1)}) custom-call(bf16[8,2,64,512]{3,2,1,0:T(8,128)(2,1)} %bitcast.152, bf16[8,2,64,512]{3,2,1,0:T(8,128)(2,1)} %bitcast.151, ...), custom_call_target="tpu_custom_call" | custom-call | tf_op jit(solution)/shard_map/to_heads/pallas_call | solution.py:704
  215.5 18.6 %attend.1 = (bf16[1024,512]{1,0:T(8,128)(2,1)}, f32[4,128,1024]{2,1,0:T(8,128)}, f32[4,2,1024]{2,1,0:T(2,128)}) custom-call(bf16[1024,512]{1,0:T(8,128)(2,1)} %bitcast.125, bf16[1024,512]{1,0:T(8,128)(2,1)} %bitcast.127, bf16[1024,512]{1,0:T(8,128)(2,1)} %bitcast.129), custom_call_target="tpu_custom_call" | custom-call | tf_op jit(solution)/shard_map/attend/pallas_call | solution.py:114
  234.1 22.0 %from_heads.1 = bf16[8,2,64,512]{3,2,1,0:T(8,128)(2,1)} custom-call(bf16[16,64,512]{2,1,0:T(8,128)(2,1)} %bitcast.150), custom_call_target="tpu_custom_call" | custom-call | tf_op jit(solution)/shard_map/from_heads/pallas_call | solution.py:704
  267.1 26.1 %branch.1 = f32[256,1600]{1,0:T(8,128)} custom-call(bf16[4,256,1600]{2,1,0:T(8,128)(2,1)} %bitcast.111), custom_call_target="tpu_custom_call" | custom-call | tf_op jit(solution)/shard_map/branch/pallas_call | solution.py:704
  296.7 25.5 %second.1 = bf16[4,256,1600]{2,1,0:T(8,128)(2,1)} custom-call(bf16[256,1600]{1,0:T(8,128)(2,1)} %add_convert_fusion.4.refs_0_), custom_call_target="tpu_custom_call" | custom-call | tf_op jit(solution)/shard_map/second/pallas_call | solution.py:704
  322.2 9.8 fusion.17
  332.1 11.9 %convolution_convert_fusion.3 = bf16[1024,1600]{0,1:T(8,128)(2,1)} fusion(bf16[1600,1600]{1,0:T(8,128)(2,1)} %param.24, f32[1024,1600]{0,1:T(8,128)S(1)} %fusion.17, f32[1600]{0:T(1024)S(1)} %convert_element_type.109), kind=kOutput, calls=%fused_computation.16 | convolution fusion | flops 5260902400 | bytes 14956800 | tf_op jit(solution)/shard_map/dot_general | solution.py:49
  344.0 11.8 %convert_reduce_fusion = (f32[1600]{0:T(1024)S(1)}, bf16[1024,1600]{0,1:T(8,128)(2,1)}) fusion(f32[1024,1600]{0,1:T(8,128)S(1)} %fusion.17, f32[1600]{0:T(1024)S(1)} %convert_element_type.109, bf16[1024,1600]{1,0:T(8,128)(2,1)S(1)} %bitcast.179, bf16[1600,1600]{1,0:T(8,128)(2,1)S(1)} %bitcast.168), kind=kOutput, calls=%fused_computation.11 | convolution fusion | flops 5278923264 | bytes 18240000 | tf_op jit(solution)/shard_map/dot_general | solution.py:53
  355.8 9.9 convolution_convert_fusion.1
  365.7 7.5 convolution_convert_fusion.2
  373.1 8.5 convolution_convert_fusion
  392.7 46.2 %second_back.1 = (f32[256,1600]{1,0:T(8,128)}, f32[256,1600]{1,0:T(8,128)}) custom-call(bf16[4,256,1600]{2,1,0:T(8,128)(2,1)} %bitcast.113, bf16[4,256,1600]{2,1,0:T(8,128)(2,1)} %bitcast.114), custom_call_target="tpu_custom_call" | custom-call | tf_op jit(solution)/shard_map/second_back/pallas_call | solution.py:704
  446.1 223.4 %wide_grads.1 = (bf16[8,200,1600]{2,1,0:T(8,128)(2,1)}, bf16[8,200,1600]{2,1,0:T(8,128)(2,1)}, bf16[4,256,1600]{2,1,0:T(8,128)(2,1)}) custom-call(bf16[8,200,1600]{2,1,0:T(8,128)(2,1)} %bitcast.123, bf16[8,200,1600]{2,1,0:T(8,128)(2,1)} %bitcast.124, bf16[256,1600]{1,0:T(8,128)(2,1)} %get-tuple-element.130.refs_2_), custom_call_target="tpu_custom_call" | custom-call | tf_op jit(solution)/shard_map/wide_grads/pallas_call | solution.py:704
  677.8 27.4 %to_heads_back.1 = bf16[16,64,512]{2,1,0:T(8,128)(2,1)} custom-call(bf16[8,2,64,512]{3,2,1,0:T(8,128)(2,1)} %bitcast.149), custom_call_target="tpu_custom_call" | custom-call | tf_op jit(solution)/shard_map/to_heads_back/pallas_call | solution.py:704
  705.2 16.0 %attend_back.1 = (bf16[1024,512]{1,0:T(8,128)(2,1)}, bf16[1024,512]{1,0:T(8,128)(2,1)}, bf16[1024,512]{1,0:T(8,128)(2,1)}) custom-call(bf16[1024,512]{1,0:T(8,128)(2,1)} %bitcast.126, bf16[1024,512]{1,0:T(8,128)(2,1)} %bitcast.128, bf16[1024,512]{1,0:T(8,128)(2,1)} %bitcast.130, bf16[1024,512]{1,0:T(8,128)(2,1)} %bitcast.131, ...), custom_call_target="tpu_custom_call" | custom-call | tf_op jit(solution)/shard_map/attend_back/pallas_call | solution.py:178
  721.2 63.5 %from_heads_back.1 = (bf16[8,2,64,512]{3,2,1,0:T(8,128)(2,1)}, bf16[8,2,64,512]{3,2,1,0:T(8,128)(2,1)}, bf16[8,2,64,512]{3,2,1,0:T(8,128)(2,1)}) custom-call(bf16[16,64,512]{2,1,0:T(8,128)(2,1)} %bitcast.142, bf16[16,64,512]{2,1,0:T(8,128)(2,1)} %bitcast.143, bf16[16,64,512]{2,1,0:T(8,128)(2,1)} %bitcast.144), custom_call_target="tpu_custom_call" | custom-call | tf_op jit(solution)/shard_map/from_heads_back/pallas_call | solution.py:704
  809.5 26.2 %first_back.1 = f32[256,1600]{1,0:T(8,128)} custom-call(bf16[4,256,1600]{2,1,0:T(8,128)(2,1)} %bitcast.112), custom_call_target="tpu_custom_call" | custom-call | tf_op jit(solution)/shard_map/first_back/pallas_call | solution.py:704
  842.1 6.0 small.1
  849.5 165.0 %narrow_grads.1 = (bf16[8,64,1600]{2,1,0:T(8,128)(2,1)}, bf16[8,200,512]{2,1,0:T(8,128)(2,1)}, bf16[8,200,512]{2,1,0:T(8,128)(2,1)}, bf16[8,200,512]{2,1,0:T(8,128)(2,1)}, f32[12,400]{1,0:T(8,128)}) custom-call(bf16[8,64,1600]{2,1,0:T(8,128)(2,1)} %bitcast.118, bf16[8,200,512]{2,1,0:T(8,128)(2,1)} %bitcast.139, bf16[8,200,512]{2,1,0:T(8,128)(2,1)} %bitcast.140, ...), custom_call_target="tpu_custom_call" | custom-call | tf_op jit(solution)/shard_map/narrow_grads/pallas_call | solution.py:704
  1018.6 7.5 bitcast_convert_fusion
  1032.6 13.7 %by_rows.1 = (f32[400,6400]{1,0:T(8,128)}, f32[400,1600]{1,0:T(8,128)}, f32[400,1600]{1,0:T(8,128)}, f32[400,1600]{1,0:T(8,128)}) custom-call(s32[4]{0:T(128)} %and_select_fusion.order_ref, bf16[8,200,1600]{2,1,0:T(8,128)(2,1)} %get-tuple-element.68.refs_0_.refs_1_.refs_2_.refs_3_, bf16[8,200,1600]{2,1,0:T(8,128)(2,1)} %get-tuple-element.68.refs_0_.refs_1_.refs_2_.refs_3_, ...), custom_call_target="tpu_custom_call" | custom-call | tf_op jit(solution)/shard_map/by_rows/pallas_call | solution.py:749
  (171 shorter events, 105.5 us)
Async XLA Ops:
  0.7 10.1 copy-start.2
  10.7 91.6 %copy-start.15 = (f32[1600]{0:T(1024)}, f32[1600]{0:T(1024)S(1)}, u32[]{:S(2)}) copy-start(f32[1600]{0:T(1024)S(1)} %mul.154) | copy-start | bytes 19204
  10.7 91.6 %copy-start.18 = (f32[256]{0:T(256)}, f32[256]{0:T(256)S(1)}, u32[]{:S(2)}) copy-start(f32[256]{0:T(256)S(1)} %get-tuple-element.146) | copy-start | bytes 3076
  11.0 91.3 %copy-start.20 = (f32[256]{0:T(256)}, f32[256]{0:T(256)S(1)}, u32[]{:S(2)}) copy-start(f32[256]{0:T(256)S(1)} %rsqrt_bitcast_fusion) | copy-start | bytes 3076
  106.8 11.8 %copy-start.4 = (bf16[1,4,400,512]{3,2,1,0:T(8,128)(2,1)}, bf16[1,4,400,512]{3,2,1,0:T(8,128)(2,1)S(1)}, u32[]{:S(2)}) copy-start(bf16[1,4,400,512]{3,2,1,0:T(8,128)(2,1)S(1)} %get-tuple-element.134) | copy-start | bytes 4915204
  110.0 5.7 copy-start.10
  110.0 5.7 copy-start.31
  295.4 26.8 %copy-start.22 = (bf16[1600]{0:T(1024)(128)(2,1)S(1)}, bf16[1600]{0:T(1024)(128)(2,1)}, u32[]{:S(2)}) copy-start(bf16[1600]{0:T(1024)(128)(2,1)} %param.32) | copy-start | bytes 9604
  322.2 21.8 %slice-start = ((s8[5324800]{0:T(1024)(128)(4,1)}), s8[4194304]{0:T(1024)(128)(4,1)S(1)}, s32[]{:S(2)}) async-start(s8[5324800]{0:T(1024)(128)(4,1)} %bitcast.167), calls=%async_computation | async-start | bytes 8388608
  332.1 11.9 %slice-start.1 = ((s8[5324800]{0:T(1024)(128)(4,1)}), s8[1130496]{0:T(1024)(128)(4,1)S(1)}, s32[]{:S(2)}) async-start(s8[5324800]{0:T(1024)(128)(4,1)} %bitcast.167), calls=%async_computation.1 | async-start | bytes 2260992
  332.1 11.9 %copy-start.33 = (bf16[4,256,1600]{2,1,0:T(8,128)(2,1)S(1)}, bf16[4,256,1600]{2,1,0:T(8,128)(2,1)}, u32[]{:S(2)}) copy-start(bf16[4,256,1600]{2,1,0:T(8,128)(2,1)} %get-tuple-element.55) | copy-start | bytes 9830404
  332.1 33.6 %slice-start.2 = ((s8[5324800]{0:T(1024)(128)(4,1)}), s8[4194304]{0:T(1024)(128)(4,1)S(1)}, s32[]{:S(2)}) async-start(s8[5324800]{0:T(1024)(128)(4,1)} %bitcast.170), calls=%async_computation.2 | async-start | bytes 8388608
  344.0 21.6 %slice-start.3 = ((s8[5324800]{0:T(1024)(128)(4,1)}), s8[1130496]{0:T(1024)(128)(4,1)S(1)}, s32[]{:S(2)}) async-start(s8[5324800]{0:T(1024)(128)(4,1)} %bitcast.170), calls=%async_computation.3 | async-start | bytes 2260992
  355.8 9.9 copy-start.37
  365.7 7.5 copy-start.6
  446.1 223.4 %copy-start.35 = (bf16[512,1600]{1,0:T(8,128)(2,1)S(1)}, bf16[512,1600]{1,0:T(8,128)(2,1)}, u32[]{:S(2)}) copy-start(bf16[512,1600]{1,0:T(8,128)(2,1)} %get-tuple-element.54) | copy-start | bytes 4915204
  705.2 79.5 %copy-start.11 = (bf16[1,4,400,512]{3,2,1,0:T(8,128)(2,1)S(1)}, bf16[1,4,400,512]{3,2,1,0:T(8,128)(2,1)}, u32[]{:S(2)}) copy-start(bf16[1,4,400,512]{3,2,1,0:T(8,128)(2,1)} %get-tuple-element.136) | copy-start | bytes 4915204
  809.5 26.3 %copy-start.16 = (f32[1600]{0:T(1024)S(1)}, f32[1600]{0:T(1024)}, u32[]{:S(2)}) copy-start(f32[1600]{0:T(1024)} %copy-done.15) | copy-start | bytes 19204
  809.5 26.3 %copy-start.19 = (f32[256]{0:T(256)S(1)}, f32[256]{0:T(256)}, u32[]{:S(2)}) copy-start(f32[256]{0:T(256)} %copy-done.18) | copy-start | bytes 3076
  809.5 26.3 %copy-start.21 = (f32[256]{0:T(256)S(1)}, f32[256]{0:T(256)}, u32[]{:S(2)}) copy-start(f32[256]{0:T(256)} %copy-done.20) | copy-start | bytes 3076
  809.5 28.5 %copy-start.12 = (bf16[512,1600]{0,1:T(8,128)(2,1)S(1)}, bf16[512,1600]{0,1:T(8,128)(2,1)}, u32[]{:S(2)}) copy-start(bf16[512,1600]{0,1:T(8,128)(2,1)} %convolution_convert_fusion.8) | copy-start | bytes 4915204
  1016.4 30.6 %collective-permute-start = (bf16[192,1600]{1,0:T(8,128)(2,1)}, bf16[192,1600]{1,0:T(8,128)(2,1)}, u32[]{:S(2)}, u32[]{:S(2)}) collective-permute-start(bf16[192,1600]{1,0:T(8,128)(2,1)} %bitcast.43), channel_id=1, source_target_pairs={{0,1},{1,2},{2,3},{4,5},{5,6},{6,7},{8,9},{9,10},{10,11},{12,13},{... | collective-permute-start | bytes 1843208 | tf_op jit(solution)/shard_map/ppermute | solution.py:952
  1018.6 7.5 copy-start
  1018.6 7.5 copy-start.3
  (19 other events, 62.7 us)

commit v3 on v2

--- a/solution.py
+++ b/solution.py
@@ -424,19 +424,19 @@
         self.ins = list(arrays)
         rows = arrays[0].shape[0]
         shape = (len(arrays), self.parts, rows, wide)
-        self.outs = [jax.ShapeDtypeStruct(shape, arrays[0].dtype)]
+        self.outs = [jax.ShapeDtypeStruct(shape[1:], arrays[0].dtype)] * len(arrays)
         self.scratch = [pltpu.VMEM(shape, arrays[0].dtype)]
         self.scratch += [pltpu.SemaphoreType.DMA((len(arrays), self.parts))] * 2
 
     def phases(self, place, ins, outs, scratch):
-        (out,), (stage, send, recv) = outs, scratch
+        stage, send, recv = scratch
         parts, live = self.parts, self.live
         every = [(i, step) for step in (2, 3, 1) for i in range(len(ins))]
 
         def copy(i, step, index):
             other = (place.part + step) % parts
             return remote(
-                stage.at[i, other], out.at[i, index], send.at[i, step], recv.at[i, step], fsdp=other
+                stage.at[i, other], outs[i].at[index], send.at[i, step], recv.at[i, step], fsdp=other
             )
 
         def first():
@@ -451,7 +451,7 @@
             for i, step in every:
                 copy(i, step, place.part).start()
             for i in range(len(ins)):
-                out[i, place.part] = stage[i, place.part]
+                outs[i][place.part] = stage[i, place.part]
 
         def second():
             for i, step in every:
@@ -716,6 +716,202 @@
         split.append(results[: len(t.outs)])
         del results[: len(t.outs)]
     return split
+
+
+def like(shape, dtype):
+    return jax.ShapeDtypeStruct(shape, dtype)
+
+
+def share(transfer, place, refs, ins, outs):
+    count = len(transfer.scratch)
+    taken = refs[:count]
+    del refs[:count]
+    return transfer.phases(place, ins, outs, taken)
+
+
+def quarter_rows(place_index, own):
+    return pl.ds(pl.multiple_of(place_index * own, own), own)
+
+
+def scattered(place, partial, part, scatter_phases):
+    first, second, third, fourth = scatter_phases
+
+    def fill(index):
+        part[index] = partial(index).astype(part.dtype)
+
+    def begin():
+        fill(place.diagonal)
+        fill(place.beside)
+        first()
+
+    def middle():
+        fill(place.far)
+        second()
+
+    def later():
+        fill(place.part)
+        third()
+
+    return [begin, middle, later, fourth]
+
+
+class Middle:
+    reach = ("fsdp", "ctx")
+
+    def __init__(self, blocks, seqs, out_w, x_full, vectors):
+        own, width = x_full.shape
+        parts = lax.axis_size("fsdp")
+        self.own, self.parts = own, parts
+        self.heads = FromHeads([blocks], seqs)
+        self.scatter = Scatter(like((parts, own, width), BF16))
+        self.gather = Gather(like((own, width), BF16))
+        self.ins = [blocks, out_w, x_full, vectors]
+        self.outs = [
+            self.heads.outs[0],
+            like((own, width), F32),
+            like((own, width), F32),
+            like((own, 1), F32),
+            self.gather.outs[0],
+        ]
+        self.scratch = [
+            pltpu.VMEM((parts, own, width), BF16),
+            pltpu.VMEM((own, width), F32),
+            pltpu.VMEM((own, width), BF16),
+        ]
+        for transfer in (self.heads, self.scatter, self.gather):
+            self.scratch += transfer.scratch
+
+    def phases(self, place, ins, outs, scratch):
+        blocks, out_w, x_full, vectors = ins
+        attended, resid, hat, inv, normed_all = outs
+        part, branch, normed, *rest = scratch
+        heads = share(self.heads, place, rest, [blocks], [attended])
+        scatter = share(self.scatter, place, rest, [part], [branch])
+        gather = share(self.gather, place, rest, [normed], [normed_all])
+        seqs, _, half, cols = attended.shape
+        group = seqs // self.parts
+
+        def partial(index):
+            rows = attended[pl.ds(index * group, group)].reshape(self.own, cols)
+            return dot(rows, out_w[...])
+
+        def norm():
+            total = x_full[...] + branch[...] + vectors[0:1]
+            resid[...] = total
+            hat[...], inv[...] = normalize(total)
+            normed[...] = (hat[...] * vectors[1:2] + vectors[2:3]).astype(BF16)
+
+        return heads + scattered(place, partial, part, scatter) + [norm] + gather
+
+
+class SecondBack:
+    reach = ("fsdp",)
+
+    def __init__(self, grad_pre, fc, hat, inv, gain, grad_y, out_w):
+        own, width = hat.shape
+        parts = lax.axis_size("fsdp")
+        self.own, self.parts = own, parts
+        self.scatter = Scatter(like((parts, own, width), BF16))
+        self.gather = Gather(like((own, width), BF16))
+        self.ins = [grad_pre, fc, hat, inv, gain, grad_y, out_w]
+        self.outs = [
+            like((own, width), F32),
+            self.gather.outs[0],
+            like((parts * own, out_w.shape[0]), BF16),
+            like((4, width), F32),
+        ]
+        self.scratch = [
+            pltpu.VMEM((parts, own, width), BF16),
+            pltpu.VMEM((own, width), F32),
+            pltpu.VMEM((own, width), BF16),
+        ]
+        for transfer in (self.scatter, self.gather):
+            self.scratch += transfer.scratch
+
+    def phases(self, place, ins, outs, scratch):
+        grad_pre, fc, hat, inv, gain, grad_y, out_w = ins
+        resid, branch_all, attended, sums = outs
+        part, norm_grad, branch, *rest = scratch
+        scatter = share(self.scatter, place, rest, [part], [norm_grad])
+        gather = share(self.gather, place, rest, [branch], [branch_all])
+        own = self.own
+
+        def partial(index):
+            return dot_nt(grad_pre[quarter_rows(index, own), :], fc[...])
+
+        def norm():
+            given = grad_y[...].astype(F32)
+            total = given + norm_back(norm_grad[...], gain[...], hat[...], inv[...])
+            resid[...] = total
+            branch[...] = total.astype(BF16)
+            sums[0:1] = jnp.sum(norm_grad[...] * hat[...], axis=0, keepdims=True)
+            sums[1:2] = jnp.sum(norm_grad[...], axis=0, keepdims=True)
+            sums[2:3] = jnp.sum(branch[...].astype(F32), axis=0, keepdims=True)
+            sums[3:4] = jnp.sum(given, axis=0, keepdims=True)
+
+        def project():
+            for index in range(self.parts):
+                rows = dot_nt(branch_all[index], out_w[...])
+                attended[index * own : (index + 1) * own] = rows.astype(BF16)
+
+        return scattered(place, partial, part, scatter) + [norm] + gather + [project]
+
+
+class FirstBack:
+    reach = ("fsdp", "ctx")
+
+    def __init__(self, grads, weights, hat, inv, gain, resid, rest, bias_fc):
+        own, width = hat.shape
+        parts = lax.axis_size("fsdp")
+        self.own, self.parts, self.count = own, parts, len(grads)
+        quarter = width // parts
+        lines = rest.shape[0] + 2
+        self.scatter = Scatter(like((parts, own, width), BF16))
+        self.small = Scatter(like((parts, lines, quarter), F32))
+        self.total = Total(like((lines + bias_fc.shape[0], quarter), F32))
+        self.ins = [*grads, *weights, hat, inv, gain, resid, rest, bias_fc]
+        self.outs = [like((own, width), F32), self.total.outs[0]]
+        self.scratch = [
+            pltpu.VMEM((parts, own, width), BF16),
+            pltpu.VMEM((own, width), F32),
+            pltpu.VMEM((lines, width), F32),
+            pltpu.VMEM((parts, lines, quarter), F32),
+            pltpu.VMEM((lines, quarter), F32),
+            pltpu.VMEM((lines + bias_fc.shape[0], quarter), F32),
+        ]
+        for transfer in (self.scatter, self.small, self.total):
+            self.scratch += transfer.scratch
+
+    def phases(self, place, ins, outs, scratch):
+        grads, weights = ins[: self.count], ins[self.count : 2 * self.count]
+        hat, inv, gain, resid, others, bias_fc = ins[2 * self.count :]
+        input_grad, totals = outs
+        part, norm_grad, lines, small, small_sum, packed, *rest = scratch
+        scatter = share(self.scatter, place, rest, [part], [norm_grad])
+        small_scatter = share(self.small, place, rest, [small], [small_sum])
+        total = share(self.total, place, rest, [packed], [totals])
+        quarter = small.shape[2]
+        count = lines.shape[0]
+
+        def partial(index):
+            rows = quarter_rows(index, self.own)
+            return sum(dot_nt(grad[rows, :], weight[...]) for grad, weight in zip(grads, weights))
+
+        def norm():
+            input_grad[...] = resid[...] + norm_back(norm_grad[...], gain[...], hat[...], inv[...])
+            lines[0:1] = jnp.sum(norm_grad[...] * hat[...], axis=0, keepdims=True)
+            lines[1:2] = jnp.sum(norm_grad[...], axis=0, keepdims=True)
+            lines[2:] = others[...]
+            for index in range(self.parts):
+                small[index] = lines[:, index * quarter : (index + 1) * quarter]
+
+        def pack():
+            packed[:count] = small_sum[...]
+            packed[count:] = bias_fc[...]
+            total[0]()
+
+        phases = scattered(place, partial, part, scatter) + [norm] + small_scatter
+        return phases + [pack, total[1]]
 
 
 def results_kernel(widths, parts, order_ref, *refs):
@@ -826,27 +1022,25 @@
 
     x_full = inputs.astype(F32).reshape(own, width)
     hat_one, inv_one = normalize(x_full)
-    (qkv,), (out_w,), (normed_one,) = exchange(
+    qkv, (out_w,), (normed_one,) = exchange(
         0,
         "start",
         Swap([w_query, w_key, w_value], live, cols),
         Window(w_out, live, cols),
         Gather((hat_one * gain_one + shift_one).astype(BF16)),
     )
-    qkv = qkv.reshape(3, width, cols)
+    qkv = [weight.reshape(width, cols) for weight in qkv]
     normed_one = normed_one.reshape(tokens, width)
     queries = (dot(normed_one, qkv[0]) + bias_query).astype(BF16)
     keys = dot(normed_one, qkv[1]).astype(BF16)
     values = (dot(normed_one, qkv[2]) + bias_value).astype(BF16)
-    heads, (fc,), (grad_y,) = exchange(
+    heads, (fc,) = exchange(
         1,
         "to_heads",
         ToHeads([by_sequences(a) for a in (queries, keys, values)]),
         Swap([w_fc], hidden_part, hidden_part),
-        Gather(cotangent.reshape(own, width)),
     )
     fc = fc.reshape(width, hidden_part)
-    grad_y = grad_y.reshape(tokens, width)
     proj = w_proj
 
     q_seq, k_seq, v_seq = [a.reshape(length, piece) for a in heads]
@@ -855,92 +1049,74 @@
     def blocks(array):
         return array.reshape(2 * n_ctx, half_rows, piece)
 
-    (attended,) = exchange(2, "from_heads", FromHeads([blocks(o_seq)], all_seqs))[0]
+    (attended, resid, hat_two, inv_two, normed_two), (grad_y,) = exchange(
+        2,
+        "middle",
+        Middle(blocks(o_seq), all_seqs, out_w, x_full, jnp.stack([bias_out, gain_two, shift_two])),
+        Gather(cotangent.reshape(own, width)),
+    )
     attended = attended.reshape(tokens, cols)
-    (branch,) = exchange(3, "branch", Scatter(by_parts(dot(attended, out_w))))[0]
-    resid = x_full + branch + bias_out
-
-    hat_two, inv_two = normalize(resid)
-    (normed_two,) = exchange(4, "second", Gather((hat_two * gain_two + shift_two).astype(BF16)))[0]
     normed_two = normed_two.reshape(tokens, width)
+    grad_y = grad_y.reshape(tokens, width)
+
     pre_act = dot(normed_two, fc) + bias_fc
     value, slope = gelu_both(pre_act)
     activated = value.astype(BF16)
     mlp = by_parts(dot(activated, proj))
 
     grad_pre = (dot_nt(grad_y, proj) * slope).astype(BF16)
-    (grad_norm_two,), (mlp,) = exchange(
-        5, "second_back", Scatter(by_parts(dot_nt(grad_pre, fc))), Scatter(mlp)
-    )
-    outputs = (resid + mlp + bias_proj).astype(BF16).reshape(seqs, rows, width)
-    grad_y_own = cotangent.reshape(own, width).astype(F32)
-    grad_gain_two = jnp.sum(grad_norm_two * hat_two, axis=0)
-    grad_shift_two = jnp.sum(grad_norm_two, axis=0)
-    grad_bias_proj = jnp.sum(grad_y_own, axis=0)
     grad_bias_fc = jnp.sum(grad_pre.astype(F32), axis=0)
-    grad_resid = grad_y_own + norm_back(grad_norm_two, gain_two, hat_two, inv_two)
-    grad_branch = grad_resid.astype(BF16)
-    grad_bias_out = jnp.sum(grad_branch.astype(F32), axis=0)
     proj_part = by_slabs(dot_tn(activated, grad_y), n_ctx)
     fc_part = by_slabs(dot_tn(normed_two, grad_pre), n_ctx)
-    (proj_grad, fc_grad), (grad_branch,) = exchange(
-        6, "wide_grads", Ring([(proj_part, 1, False), (fc_part, -1, True)]), Gather(grad_branch)
+    (proj_grad, fc_grad), (grad_resid, grad_branch, grad_attended, sums_two) = exchange(
+        3,
+        "wide_grads",
+        Ring([(proj_part, 1, False), (fc_part, -1, True)]),
+        SecondBack(
+            grad_pre, fc, hat_two, inv_two, gain_two[None], cotangent.reshape(own, width), out_w
+        ),
     )
     grad_branch = grad_branch.reshape(tokens, width)
-    grad_attended = dot_nt(grad_branch, out_w).astype(BF16)
-
-    ((grad_heads,),) = exchange(7, "to_heads_back", ToHeads([by_sequences(grad_attended)]))
+
+    ((grad_heads,),) = exchange(4, "to_heads_back", ToHeads([by_sequences(grad_attended)]))
     dq_seq, dk_seq, dv_seq = attend_back(
         q_seq, k_seq, v_seq, grad_heads.reshape(length, piece), ot, lse, heads_here
     )
     (grad_qkv,) = exchange(
-        8, "from_heads_back", FromHeads([blocks(a) for a in (dq_seq, dk_seq, dv_seq)], all_seqs)
+        5, "from_heads_back", FromHeads([blocks(a) for a in (dq_seq, dk_seq, dv_seq)], all_seqs)
     )
     grad_qkv = [a.reshape(tokens, cols) for a in grad_qkv]
-    ((grad_norm_one,),) = exchange(
-        9,
-        "first_back",
-        Scatter(
-            by_parts(
-                dot_nt(grad_qkv[0], qkv[0]) + dot_nt(grad_qkv[1], qkv[1]) + dot_nt(grad_qkv[2], qkv[2])
-            )
-        ),
-    )
     grad_bias_query = jnp.sum(grad_qkv[0].astype(F32), axis=0)
     grad_bias_value = jnp.sum(grad_qkv[2].astype(F32), axis=0)
-    grad_gain_one = jnp.sum(grad_norm_one * hat_one, axis=0)
-    grad_shift_one = jnp.sum(grad_norm_one, axis=0)
-    input_grad = grad_resid + norm_back(grad_norm_one, gain_one, hat_one, inv_one)
-    input_grad = input_grad.reshape(seqs, rows, width)
 
     def window(vector):
         whole = jnp.zeros((parts * live,), F32)
         return lax.dynamic_update_slice_in_dim(whole, vector[:live], me_part * live, 0)[:width]
 
-    small_grads = jnp.stack(
-        [
-            grad_gain_one,
-            grad_shift_one,
-            window(grad_bias_query),
-            window(grad_bias_value),
-            grad_bias_out,
-            grad_gain_two,
-            grad_shift_two,
-            grad_bias_proj,
-        ]
-    )
-    small_grads = jnp.transpose(small_grads.reshape(8, parts, quarter), (1, 0, 2))
-    ((small_grads,),) = exchange(10, "small", Scatter(small_grads))
-    small_grads = jnp.concatenate([small_grads, grad_bias_fc.reshape(-1, quarter)])
+    small_grads = jnp.concatenate(
+        [window(grad_bias_query)[None], window(grad_bias_value)[None], sums_two]
+    )
 
     q_part, k_part, v_part = [by_slabs(dot_tn(normed_one, a), n_ctx) for a in grad_qkv]
     out_part = by_slabs(dot_tn(attended, grad_branch), n_ctx)
-    (out_grad, q_grad, k_grad, v_grad), (small_grads,) = exchange(
-        11,
+    (out_grad, q_grad, k_grad, v_grad), (input_grad, small_grads), (mlp,) = exchange(
+        6,
         "narrow_grads",
         Ring([(out_part, 1, False), (q_part, 1, True), (k_part, -1, True), (v_part, -1, True)]),
-        Total(small_grads),
-    )
+        FirstBack(
+            grad_qkv,
+            qkv,
+            hat_one,
+            inv_one,
+            gain_one[None],
+            grad_resid,
+            small_grads,
+            grad_bias_fc.reshape(-1, quarter),
+        ),
+        Scatter(mlp),
+    )
+    outputs = (resid + mlp + bias_proj).astype(BF16).reshape(seqs, rows, width)
+    input_grad = input_grad.reshape(seqs, rows, width)
     fc_out, q_out, k_out, v_out = by_rows(
         [fc_grad, q_grad, k_grad, v_grad],
         [(hidden_part, hidden)] + [(live, width)] * 3,
@@ -966,9 +1142,9 @@
         small_grads[1],
         small_grads[2],
         small_grads[3],
+        small_grads[6],
         small_grads[4],
         small_grads[5],
-        small_grads[6],
         small_grads[8:].reshape(-1),
         small_grads[7],
     )

time: 1060 us -> 943 us (0.89)
  Pallas kernels: 863 us -> 791 us
  matrix products: 103 us -> 81.3 us
  local copies, waits for them, and re-layouts: 44.4 us -> 28.6 us
    pallas_call x12 -> x7, Pallas kernels: 815 us -> 743 us  [exchange(): pl.pallas_call(functools.partial(exchange_kernel, transfers), out_shape=o...]
    dot_general x6 -> x1, matrix products: 33.5 us -> 11.6 us  [dot_nt(): lax.dot_general(left, right, (((1,), (1,)), ((), ())), preferred_element_...]
    convert_element_type x4 -> x1, local copies, waits for them, and re-layouts: 22.2 us -> 5.44 us  [by_parts(): return array.astype(BF16).reshape(parts, own, width)]
    dot_general x6 -> x5, matrix products: 38.8 us -> 33.6 us  [dot(): return jnp.dot(left, right, preferred_element_type=F32)]
where the time goes in v3:
time: 943 us; the launch traced here: 928 us
  Pallas kernels  791 us (84%)
  matrix products  81.3 us (9%)
  local copies, waits for them, and re-layouts  28.6 us (3%)
  other arithmetic  18 us (2%)
    pallas_call x7, Pallas kernels, exchange(): pl.pallas_call(functools.partial(exchange_kernel, transfers), out_shape=o...  743 us
    dot_general x6, matrix products, dot_tn(): lax.dot_general(left, right, (((0,), (0,)), ((), ())), preferred_element_...  36.2 us
    dot_general x5, matrix products, dot(): return jnp.dot(left, right, preferred_element_type=F32)  33.6 us
  transfers between devices with their start and end apart: 1, of which 0 were waited for; matrix products, arithmetic and copies ran while one was open for 1% of the time, Pallas kernels for 1%

profile of v3, /device:TPU:0, one launch (start us, length us, event | category | flops | bytes accessed | tf_op | source)
XLA Modules:
  0.0 928.2 jit_solution(1662847213868317975)
XLA Ops:
  0.7 5.7 concatenate.9
  6.4 6.2 all-gather.1
  20.9 90.0 %start.1 = (bf16[4,400,512]{2,1,0:T(8,128)(2,1)}, bf16[4,400,512]{2,1,0:T(8,128)(2,1)}, bf16[4,400,512]{2,1,0:T(8,128)(2,1)}, bf16[512,1600]{1,0:T(8,128)(2,1)}, bf16[4,256,1600]{2,1,0:T(8,128)(2,1)}) custom-call(bf16[400,1600]{1,0:T(8,128)(2,1)} %refs_0_.1, bf16[400,1600]{1,0:T(8,128)(2,1)} %refs_1_.1, bf16[400,1600]{1,0:T(8,128)(2,1)} %refs_2_.1, ...), custom_call_target="tpu_custom_call" | custom-call | tf_op jit(solution)/shard_map/start/pallas_call | solution.py:704
  110.9 5.6 convolution_convert_fusion.7
  123.2 72.4 %to_heads.1 = (bf16[16,64,512]{2,1,0:T(8,128)(2,1)}, bf16[16,64,512]{2,1,0:T(8,128)(2,1)}, bf16[16,64,512]{2,1,0:T(8,128)(2,1)}, bf16[4,400,1600]{2,1,0:T(8,128)(2,1)}) custom-call(bf16[8,2,64,512]{3,2,1,0:T(8,128)(2,1)} %bitcast.116, bf16[8,2,64,512]{3,2,1,0:T(8,128)(2,1)} %bitcast.115, bf16[8,2,64,512]{3,2,1,0:T(8,128)(2,1)} %bitcast.121, ...), custom_call_target="tpu_custom_call" | custom-call | tf_op jit(solution)/shard_map/to_heads/pallas_call | solution.py:704
  195.7 18.6 %attend.1 = (bf16[1024,512]{1,0:T(8,128)(2,1)}, f32[4,128,1024]{2,1,0:T(8,128)}, f32[4,2,1024]{2,1,0:T(2,128)}) custom-call(bf16[1024,512]{1,0:T(8,128)(2,1)} %bitcast.95, bf16[1024,512]{1,0:T(8,128)(2,1)} %bitcast.97, bf16[1024,512]{1,0:T(8,128)(2,1)} %bitcast.99), custom_call_target="tpu_custom_call" | custom-call | tf_op jit(solution)/shard_map/attend/pallas_call | solution.py:114
  214.2 84.7 %middle.1 = (bf16[8,2,64,512]{3,2,1,0:T(8,128)(2,1)}, f32[256,1600]{1,0:T(8,128)}, f32[256,1600]{1,0:T(8,128)}, f32[256,1]{1,0:T(8,128)}, bf16[4,256,1600]{2,1,0:T(8,128)(2,1)}, /*index=5*/bf16[4,256,1600]{2,1,0:T(8,128)(2,1)}) custom-call(bf16[16,64,512]{2,1,0:T(8,128)(2,1)} %bitcast.117, bf16[512,1600]{1,0:T(8,128)(2,1)} %get-tuple-element.66.refs_1_.refs_8_, ...), custom_call_target="tpu_custom_call" | custom-call | tf_op jit(solution)/shard_map/middle/pallas_call | solution.py:704
  298.9 11.9 %fusion.13 = f32[1024,1600]{1,0:T(8,128)} fusion(bf16[1024,1600]{1,0:T(8,128)(2,1)} %bitcast.147, bf16[1600,1600]{1,0:T(8,128)(2,1)} %bitcast.87), kind=kOutput, calls=%fused_computation.57 | convolution fusion | flops 5242880000 | bytes 14950400 | tf_op jit(solution)/shard_map/dot_general | solution.py:49
  310.8 10.1 %convolution_convert_fusion.2 = bf16[1024,1600]{0,1:T(8,128)(2,1)} fusion(bf16[1600,1600]{1,0:T(8,128)(2,1)S(1)} %bitcast.137, f32[1024,1600]{1,0:T(8,128)} %fusion.13, f32[1600]{0:T(1024)S(1)} %convert_element_type.80), kind=kOutput, calls=%fused_computation.14 | convolution fusion | flops 5260902400 | bytes 14956800 | tf_op jit(solution)/shard_map/dot_general | solution.py:49
  321.0 11.6 %convert_reduce_fusion = (f32[1600]{0:T(1024)S(1)}, bf16[1024,1600]{1,0:T(8,128)(2,1)S(1)}) fusion(f32[1024,1600]{1,0:T(8,128)} %fusion.13, f32[1600]{0:T(1024)S(1)} %convert_element_type.80, bf16[1024,1600]{1,0:T(8,128)(2,1)S(1)} %bitcast.149, bf16[1600,1600]{1,0:T(8,128)(2,1)S(1)} %bitcast.139), kind=kOutput, calls=%fused_computation.11 | convolution fusion | flops 5278923264 | bytes 18240000 | tf_op jit(solution)/shard_map/dot_general | solution.py:53
  332.6 9.5 %convolution_convert_fusion.1 = bf16[1600,1600]{1,0:T(8,128)(2,1)} fusion(bf16[1024,1600]{1,0:T(8,128)(2,1)S(1)} %bitcast.150, f32[1024,1600]{1,0:T(8,128)S(1)} %copy-done.19, f32[1600]{0:T(1024)S(1)} %convert_element_type.80), kind=kOutput, calls=%fused_computation.3 | convolution fusion | flops 5261824000 | bytes 14956800 | tf_op jit(solution)/shard_map/dot_general | solution.py:57
  342.9 5.4 copy.56
  349.0 11.0 %convolution_convert_fusion = bf16[1600,1600]{1,0:T(8,128)(2,1)} fusion(bf16[1024,1600]{1,0:T(8,128)(2,1)} %bitcast.148, bf16[1024,1600]{1,0:T(8,128)(2,1)S(1)} %get-tuple-element.173.refs_2_), kind=kOutput, calls=%fused_computation.2 | convolution fusion | flops 5245440000 | bytes 11673600 | tf_op jit(solution)/shard_map/dot_general | solution.py:57
  360.0 226.3 %wide_grads.1 = (bf16[8,200,1600]{2,1,0:T(8,128)(2,1)}, bf16[8,200,1600]{2,1,0:T(8,128)(2,1)}, f32[256,1600]{1,0:T(8,128)}, bf16[4,256,1600]{2,1,0:T(8,128)(2,1)...) custom-call(bf16[8,200,1600]{2,1,0:T(8,128)(2,1)} %bitcast.89, bf16[8,200,1600]{2,1,0:T(8,128)(2,1)} %bitcast.90, ...), custom_call_target="tpu_custom_call" | custom-call | tf_op jit(solution)/shard_map/wide_grads/pallas_call | solution.py:704
  586.4 26.9 %to_heads_back.1 = bf16[16,64,512]{2,1,0:T(8,128)(2,1)} custom-call(bf16[8,2,64,512]{3,2,1,0:T(8,128)(2,1)} %bitcast.122), custom_call_target="tpu_custom_call" | custom-call | tf_op jit(solution)/shard_map/to_heads_back/pallas_call | solution.py:704
  613.2 15.9 %attend_back.1 = (bf16[1024,512]{1,0:T(8,128)(2,1)}, bf16[1024,512]{1,0:T(8,128)(2,1)}, bf16[1024,512]{1,0:T(8,128)(2,1)}) custom-call(bf16[1024,512]{1,0:T(8,128)(2,1)} %bitcast.96, bf16[1024,512]{1,0:T(8,128)(2,1)} %bitcast.98, bf16[1024,512]{1,0:T(8,128)(2,1)} %bitcast.100, bf16[1024,512]{1,0:T(8,128)(2,1)} %bitcast.101, ...), custom_call_target="tpu_custom_call" | custom-call | tf_op jit(solution)/shard_map/attend_back/pallas_call | solution.py:178
  629.1 63.3 %from_heads_back.1 = (bf16[8,2,64,512]{3,2,1,0:T(8,128)(2,1)}, bf16[8,2,64,512]{3,2,1,0:T(8,128)(2,1)}, bf16[8,2,64,512]{3,2,1,0:T(8,128)(2,1)}) custom-call(bf16[16,64,512]{2,1,0:T(8,128)(2,1)} %bitcast.118, bf16[16,64,512]{2,1,0:T(8,128)(2,1)} %bitcast.119, bf16[16,64,512]{2,1,0:T(8,128)(2,1)} %bitcast.120), custom_call_target="tpu_custom_call" | custom-call | tf_op jit(solution)/shard_map/from_heads_back/pallas_call | solution.py:704
  695.5 4.3 convolution_convert_fusion.6
  702.4 5.2 convolution_convert_fusion.5
  707.5 3.1 convolution_convert_fusion.4
  710.6 3.1 convolution_convert_fusion.3
  714.3 179.6 %narrow_grads.1 = (bf16[8,64,1600]{2,1,0:T(8,128)(2,1)}, bf16[8,200,512]{2,1,0:T(8,128)(2,1)}, bf16[8,200,512]{2,1,0:T(8,128)(2,1)}, bf16[8,200,512]{2,1,0:T(8,1...) custom-call(bf16[8,64,1600]{2,1,0:T(8,128)(2,1)} %bitcast.85, ...), custom_call_target="tpu_custom_call" | custom-call | tf_op jit(solution)/shard_map/narrow_grads/pallas_call | solution.py:704
  897.3 7.5 bitcast_convert_fusion
  911.4 13.7 %by_rows.1 = (f32[400,6400]{1,0:T(8,128)}, f32[400,1600]{1,0:T(8,128)}, f32[400,1600]{1,0:T(8,128)}, f32[400,1600]{1,0:T(8,128)}) custom-call(s32[4]{0:T(128)} %and_select_fusion.order_ref, bf16[8,200,1600]{2,1,0:T(8,128)(2,1)} %get-tuple-element.88.refs_0_.refs_1_.refs_2_.refs_3_, bf16[8,200,1600]{2,1,0:T(8,128)(2,1)} %get-tuple-element.88.refs_0_.refs_1_.refs_2_.refs_3_, ...), custom_call_target="tpu_custom_call" | custom-call | tf_op jit(solution)/shard_map/by_rows/pallas_call | solution.py:945
  (103 shorter events, 35.2 us)
Async XLA Ops:
  0.7 16.1 %copy-start.1 = (bf16[2,128,1600]{1,2,0:T(8,128)(2,1)S(1)}, bf16[2,128,1600]{1,2,0:T(8,128)(2,1)}, u32[]{:S(2)}) copy-start(bf16[2,128,1600]{1,2,0:T(8,128)(2,1)} %param.17) | copy-start | bytes 2457604
  0.7 16.3 %copy-start.15 = (bf16[1600]{0:T(1024)(128)(2,1)S(1)}, bf16[1600]{0:T(1024)(128)(2,1)}, u32[]{:S(2)}) copy-start(bf16[1600]{0:T(1024)(128)(2,1)} %param.32) | copy-start | bytes 9604
  0.7 17.0 %copy-start.11 = (bf16[2,128,1600]{1,2,0:T(8,128)(2,1)S(1)}, bf16[2,128,1600]{1,2,0:T(8,128)(2,1)}, u32[]{:S(2)}) copy-start(bf16[2,128,1600]{1,2,0:T(8,128)(2,1)} %param.18) | copy-start | bytes 2457604
  16.7 4.2 copy-start
  17.1 105.5 %copy-start.12 = (f32[1,1600]{1,0:T(1,128)}, f32[1,1600]{1,0:T(1,128)S(1)}, u32[]{:S(2)}) copy-start(f32[1,1600]{1,0:T(1,128)S(1)} %stack_reshape_squeeze.10.refs_6_) | copy-start | bytes 19204
  110.9 5.7 copy-start.8
  110.9 5.7 copy-start.16
  116.6 3.0 copy-start.9
  214.2 96.6 %slice-start = ((s8[5324800]{0:T(1024)(128)(4,1)}), s8[1130496]{0:T(1024)(128)(4,1)S(1)}, s32[]{:S(2)}) async-start(s8[5324800]{0:T(1024)(128)(4,1)} %bitcast.136), calls=%async_computation | async-start | bytes 2260992
  298.9 11.9 %slice-start.1 = ((s8[5324800]{0:T(1024)(128)(4,1)}), s8[4194304]{0:T(1024)(128)(4,1)S(1)}, s32[]{:S(2)}) async-start(s8[5324800]{0:T(1024)(128)(4,1)} %bitcast.136), calls=%async_computation.1 | async-start | bytes 8388608
  298.9 22.0 %slice-start.2 = ((s8[5324800]{0:T(1024)(128)(4,1)}), s8[4194304]{0:T(1024)(128)(4,1)S(1)}, s32[]{:S(2)}) async-start(s8[5324800]{0:T(1024)(128)(4,1)} %bitcast.138), calls=%async_computation.2 | async-start | bytes 8388608
  310.8 10.1 %slice-start.3 = ((s8[5324800]{0:T(1024)(128)(4,1)}), s8[1130496]{0:T(1024)(128)(4,1)S(1)}, s32[]{:S(2)}) async-start(s8[5324800]{0:T(1024)(128)(4,1)} %bitcast.138), calls=%async_computation.3 | async-start | bytes 2260992
  310.8 10.1 %copy-start.18 = (bf16[4,256,1600]{2,1,0:T(8,128)(2,1)S(1)}, bf16[4,256,1600]{2,1,0:T(8,128)(2,1)}, u32[]{:S(2)}) copy-start(bf16[4,256,1600]{2,1,0:T(8,128)(2,1)} %get-tuple-element.71) | copy-start | bytes 9830404
  320.9 11.6 %copy-start.19 = (f32[1024,1600]{1,0:T(8,128)S(1)}, f32[1024,1600]{1,0:T(8,128)}, u32[]{:S(2)}) copy-start(f32[1024,1600]{1,0:T(8,128)} %fusion.13) | copy-start | bytes 19660804
  332.5 16.5 %copy-start.4 = (bf16[1024,1600]{1,0:T(8,128)(2,1)}, bf16[1024,1600]{1,0:T(8,128)(2,1)S(1)}, u32[]{:S(2)}) copy-start(bf16[1024,1600]{1,0:T(8,128)(2,1)S(1)} %get-tuple-element.173.refs_2_) | copy-start | bytes 9830404
  695.5 6.8 copy-start.2
  702.3 5.2 copy-start.10
  702.4 5.2 copy-start.17
  707.5 3.1 copy-start.3
  710.6 3.1 copy-start.13
  895.9 29.9 %collective-permute-start = (bf16[192,1600]{1,0:T(8,128)(2,1)}, bf16[192,1600]{1,0:T(8,128)(2,1)S(1)}, u32[]{:S(2)}, u32[]{:S(2)}) collective-permute-start(bf16[192,1600]{1,0:T(8,128)(2,1)} %bitcast.40), channel_id=1, source_target_pairs={{0,1},{1,2},{2,3},{4,5},{5,6},{6,7},{8,9},{9,10},{10,11},{12,13},{... | collective-permute-start | bytes 1843208 | tf_op jit(solution)/shard_map/ppermute | solution.py:1128
  897.3 7.5 copy-start.6
  897.3 7.5 copy-start.7
  906.3 4.0 copy-start.14
  (1 other events, 1.5 us)

commit v4 on v3

--- a/solution.py
+++ b/solution.py
@@ -212,6 +212,10 @@
         return (1 - odd) * (self.ctx // 2) + odd * (self.n_ctx - 1 - self.ctx // 2)
 
 
+def like(shape, dtype):
+    return jax.ShapeDtypeStruct(shape, dtype)
+
+
 def remote(source, target, send, recv, **where):
     return pltpu.make_async_remote_copy(
         src_ref=source,
@@ -360,10 +364,10 @@
         n, me = self.n, place.ctx
         every = [(i, half) for i in range(len(ins)) for half in range(2)]
 
-        def first():
-            def begin(step, _):
+        def begin(i):
+            def start(step, _):
                 other = (me + step) % n
-                for i, half in every:
+                for half in range(2):
                     remote(
                         self.source(ins[i], other, half),
                         self.target(outs[i], me, half),
@@ -373,9 +377,15 @@
                     ).start()
                 return 0
 
-            lax.fori_loop(1, n, begin, 0)
-            for i, half in every:
+            lax.fori_loop(1, n, start, 0)
+            for half in range(2):
                 self.target(outs[i], me, half)[...] = self.source(ins[i], me, half)[...]
+
+        def first():
+            for i in range(len(ins)):
+                begin(i)
+
+        self.begin = begin
 
         def second():
             def end(step, _):
@@ -537,106 +547,157 @@
 class Ring:
     reach = ("ring", "fsdp")
 
-    def __init__(self, streams):
-        self.n = lax.axis_size("ctx")
+    def __init__(self, products):
+        self.n = n = lax.axis_size("ctx")
         self.parts = lax.axis_size("fsdp")
-        self.per = self.n // self.parts
-        self.streams = []
-        self.ins, self.outs, self.scratch = [], [], []
-        for array, direction, crossing in streams:
-            n, rows, columns = array.shape
-            self.ins.append(array)
-            self.outs.append(jax.ShapeDtypeStruct(array.shape, array.dtype))
-            self.scratch.append(pltpu.VMEM((n - 1, rows, columns), array.dtype))
-            middle = (columns // 2 + LANES - 1) // LANES * LANES
-            for low, high in ((0, middle), (middle, columns)):
-                self.streams.append((len(self.ins) - 1, direction, crossing, slice(low, high)))
-        self.scratch += [pltpu.SemaphoreType.DMA((len(self.streams), 2, self.n))] * 2
+        self.per = n // self.parts
+        self.products, self.streams, lefts = [], [], []
+        self.ins, self.outs, slots, local, turned = [], [], [], [], []
+        ways = [direction for _, _, direction, _ in products]
+        for left, right, direction, crossing in products:
+            rows, columns = left.shape[1] // n, right.shape[1]
+            known = [k for k, other in enumerate(lefts) if other is left]
+            if not known:
+                lefts.append(left)
+                turned.append(pltpu.VMEM((n, rows, left.shape[0]), left.dtype))
+            index = len(self.products)
+            self.products.append((known[0] if known else len(lefts) - 1, direction, crossing))
+            self.ins.append(right)
+            self.outs.append(like((n, rows, columns), BF16))
+            slots.append(pltpu.VMEM((n - 1, rows, columns), BF16))
+            local.append(pltpu.VMEM((2, rows, columns), BF16))
+            middle = columns
+            if ways.count(direction) == 1:
+                middle = (columns // 2 + LANES - 1) // LANES * LANES
+            self.streams.append((index, slice(0, middle)))
+            if middle < columns:
+                self.streams.append((index, slice(middle, columns)))
+        self.counts = (len(lefts), len(products))
+        self.ins = lefts + self.ins
+        self.spaces = [pl.ANY] * len(self.outs)
+        self.scratch = turned + slots + local
+        self.scratch += [pltpu.SemaphoreType.DMA((len(self.streams), 2, n))] * 2
 
     def phases(self, place, ins, outs, scratch):
-        slots, (send, recv) = scratch[:-2], scratch[-2:]
+        n_left, n_product = self.counts
+        lefts, rights = ins[:n_left], ins[n_left:]
+        turned, scratch = scratch[:n_left], scratch[n_left:]
+        slots, scratch = scratch[:n_product], scratch[n_product:]
+        local, (send, recv) = scratch[:n_product], scratch[n_product:]
         n, parts, per, here = self.n, self.parts, self.per, place.position
         shift = place.ctx // per
         owner = (place.part + shift) % parts
 
-        def slab(stream, position):
-            index = place.at(position)
-            return (index + per * place.part) % n if self.streams[stream][2] else index
+        def make(step):
+            for index, (left, direction, crosses) in enumerate(self.products):
+                slab = place.at(here - direction * (step + 1))
+                if crosses:
+                    slab = (slab + per * place.part) % n
+                local[index][step % 2] = dot(turned[left][slab], rights[index][...]).astype(BF16)
+
+        def way(stream):
+            return self.products[self.streams[stream][0]][1]
+
+        def crosses(stream):
+            return self.products[self.streams[stream][0]][2]
 
         def reducing(stream, step):
-            array, direction, _, columns = self.streams[stream]
-            if step == 0:
-                source = ins[array].at[slab(stream, here - direction), :, columns]
-            else:
-                source = slots[array].at[step - 1, :, columns]
+            index, columns = self.streams[stream]
+            source = local[index].at[0] if step == 0 else slots[index].at[step - 1]
             return remote(
-                source,
-                slots[array].at[step, :, columns],
+                source.at[:, columns],
+                slots[index].at[step, :, columns],
                 send.at[stream, 0, step],
                 recv.at[stream, 0, step],
-                ctx=place.at(here + direction),
+                ctx=place.at(here + way(stream)),
             )
 
+        def last(stream):
+            index, columns = self.streams[stream]
+            return slots[index].at[n - 2, :, columns]
+
+        def mine(stream):
+            index, columns = self.streams[stream]
+            return outs[index].at[place.ctx, :, columns]
+
         def crossing(stream):
-            array, _, _, columns = self.streams[stream]
             return remote(
-                slots[array].at[n - 2, :, columns],
-                outs[array].at[place.ctx, :, columns],
+                last(stream),
+                mine(stream),
                 send.at[stream, 0, n - 1],
                 recv.at[stream, 0, n - 1],
                 fsdp=owner,
             )
 
+        def keeping(stream):
+            return pltpu.make_async_copy(last(stream), mine(stream), send.at[stream, 0, n - 1])
+
         def gathering(stream, step, back=0):
-            array, direction, _, columns = self.streams[stream]
-            index = place.at(here - direction * (step + back))
+            index, columns = self.streams[stream]
+            slab = place.at(here - way(stream) * (step + back))
+            block = outs[index].at[slab, :, columns]
+            source = block
+            if step == 0 and back == 0 and not crosses(stream):
+                source = last(stream)
             return remote(
-                outs[array].at[index, :, columns],
-                outs[array].at[index, :, columns],
+                source,
+                block,
                 send.at[stream, 1, step],
                 recv.at[stream, 1, step],
-                ctx=place.at(here + direction),
+                ctx=place.at(here + way(stream)),
             )
 
         every = range(len(self.streams))
 
         def begin():
+            for left, target in zip(lefts, turned):
+                rows = target.shape[1]
+                for k in range(n):
+                    target[k] = jnp.transpose(left[:, k * rows : (k + 1) * rows])
+            make(0)
             for stream in every:
                 reducing(stream, 0).start()
+            make(1)
 
         def add(stream, step):
-            array, direction, _, columns = self.streams[stream]
+            index, columns = self.streams[stream]
             reducing(stream, step).wait_recv()
-            own = ins[array][slab(stream, here - direction * (step + 2)), :, columns]
-            return (slots[array][step, :, columns].astype(F32) + own.astype(F32)).astype(own.dtype)
+            total = slots[index][step, :, columns].astype(F32)
+            total = total + local[index][(step + 1) % 2, :, columns].astype(F32)
+            slots[index][step, :, columns] = total.astype(BF16)
 
         def reduce(step):
             for stream in every:
-                array, _, _, columns = self.streams[stream]
-                slots[array][step - 1, :, columns] = add(stream, step - 1)
+                add(stream, step - 1)
                 reducing(stream, step).start()
+            if step == 1:
+                for stream in every:
+                    reducing(stream, 0).wait_send()
+            make(step + 1)
 
         def turn():
             for stream in every:
-                array, _, crosses, columns = self.streams[stream]
-                total = add(stream, n - 2)
-                if not crosses:
-                    outs[array][place.ctx, :, columns] = total
+                add(stream, n - 2)
+                if not crosses(stream):
                     gathering(stream, 0).start()
+                    keeping(stream).start()
                     continue
 
                 @pl.when(shift == 0)
                 def _():
-                    outs[array][place.ctx, :, columns] = total
+                    keeping(stream).start()
 
                 @pl.when(shift != 0)
                 def _():
-                    slots[array][n - 2, :, columns] = total
                     crossing(stream).start()
 
         def launch():
             for stream in every:
-                if self.streams[stream][2]:
+                if crosses(stream):
+
+                    @pl.when(shift == 0)
+                    def _():
+                        keeping(stream).wait()
 
                     @pl.when(shift != 0)
                     def _():
@@ -653,8 +714,11 @@
             for stream in every:
                 gathering(stream, n - 2, 1).wait_recv()
             for stream in every:
+                if not crosses(stream):
+                    keeping(stream).wait()
                 for step in range(n - 1):
-                    reducing(stream, step).wait_send()
+                    if step:
+                        reducing(stream, step).wait_send()
                     gathering(stream, step).wait_send()
 
         steps = [begin]
@@ -664,8 +728,10 @@
         return steps + [end]
 
 
-def exchange_kernel(transfers, *refs):
+def exchange_kernel(transfers, places, *refs):
     refs = list(refs)
+    inputs = refs[: max(places) + 1]
+    refs = [inputs[index] for index in places] + refs[len(inputs) :]
 
     def take(lists):
         taken = []
@@ -699,13 +765,21 @@
 
 def exchange(number, name, *transfers):
     memory = pl.BlockSpec(memory_space=pltpu.VMEM)
-    ins = [a for t in transfers for a in t.ins]
+    ins, places = [], []
+    for array in [a for t in transfers for a in t.ins]:
+        known = [k for k, other in enumerate(ins) if other is array]
+        places.append(known[0] if known else len(ins))
+        if not known:
+            ins.append(array)
     outs = [a for t in transfers for a in t.outs]
+    spaces = []
+    for t in transfers:
+        spaces += getattr(t, "spaces", [pltpu.VMEM] * len(t.outs))
     results = pl.pallas_call(
-        functools.partial(exchange_kernel, transfers),
+        functools.partial(exchange_kernel, transfers, places),
         out_shape=outs,
         in_specs=[memory] * len(ins),
-        out_specs=[memory] * len(outs),
+        out_specs=[pl.BlockSpec(memory_space=space) for space in spaces],
         scratch_shapes=[s for t in transfers for s in t.scratch],
         compiler_params=pltpu.CompilerParams(collective_id=number, has_side_effects=True),
         name=name,
@@ -716,10 +790,6 @@
         split.append(results[: len(t.outs)])
         del results[: len(t.outs)]
     return split
-
-
-def like(shape, dtype):
-    return jax.ShapeDtypeStruct(shape, dtype)
 
 
 def share(transfer, place, refs, ins, outs):
@@ -804,6 +874,28 @@
         return heads + scattered(place, partial, part, scatter) + [norm] + gather
 
 
+class Product:
+    reach = ("fsdp",)
+
+    def __init__(self, left, right, own):
+        parts, width = lax.axis_size("fsdp"), right.shape[1]
+        self.own = own
+        self.scatter = Scatter(like((parts, own, width), BF16))
+        self.ins = [left, right]
+        self.outs = [like((own, width), F32)]
+        self.scratch = [pltpu.VMEM((parts, own, width), BF16), *self.scatter.scratch]
+
+    def phases(self, place, ins, outs, scratch):
+        left, right = ins
+        part, *rest = scratch
+        scatter = share(self.scatter, place, rest, [part], outs)
+
+        def partial(index):
+            return dot(left[quarter_rows(index, self.own), :], right[...])
+
+        return scattered(place, partial, part, scatter)
+
+
 class SecondBack:
     reach = ("fsdp",)
 
@@ -912,6 +1004,226 @@
 
         phases = scattered(place, partial, part, scatter) + [norm] + small_scatter
         return phases + [pack, total[1]]
+
+
+class Later:
+    def __init__(self, transfer, *steps):
+        self.transfer, self.steps = transfer, steps
+        self.reach = transfer.reach
+        self.ins, self.outs, self.scratch = transfer.ins, transfer.outs, transfer.scratch
+
+    def phases(self, place, ins, outs, scratch):
+        phases = [lambda: None] * (self.steps[-1] + 1)
+        for step, phase in zip(self.steps, self.transfer.phases(place, ins, outs, scratch)):
+            phases[step] = phase
+        return phases
+
+
+class Spread:
+    reach = ("fsdp", "ring")
+
+    def __init__(self, arrays, live, wide):
+        self.n = lax.axis_size("ctx")
+        self.parts = lax.axis_size("fsdp")
+        self.live, self.wide = live, wide
+        self.across = wide // LANES
+        self.down = self.n // self.across
+        self.rows = arrays[0].shape[0] // self.down
+        self.ins = list(arrays)
+        shape = (self.parts, self.down, self.rows, wide)
+        self.outs = [like(shape, a.dtype) for a in arrays]
+        self.scratch = [pltpu.VMEM(shape, a.dtype) for a in arrays]
+        self.scratch += [pltpu.SemaphoreType.DMA((len(arrays), self.parts + self.n))] * 2
+
+    @staticmethod
+    def fits(rows, wide):
+        across = wide // LANES
+        n = lax.axis_size("ctx")
+        return n % across == 0 and rows % (n // across) == 0 and rows // (n // across) % 8 == 0
+
+    def phases(self, place, ins, outs, scratch):
+        stages, (send, recv) = scratch[:-2], scratch[-2:]
+        n, parts, here = self.n, self.parts, place.position
+        every = range(len(ins))
+
+        def of(ctx):
+            column = pl.multiple_of(ctx % self.across * LANES, LANES)
+            return (ctx // self.across, slice(None), pl.ds(column, LANES))
+
+        def piece(i, step, index):
+            other = (place.part + step) % parts
+            mine = of(place.ctx)
+            return remote(
+                stages[i].at[(other, *mine)],
+                outs[i].at[(index, *mine)],
+                send.at[i, step],
+                recv.at[i, step],
+                fsdp=other,
+            )
+
+        def passing(i, step, back=0):
+            direction = 1 - 2 * (i % 2)
+            block = outs[i].at[(slice(None), *of(place.at(here - direction * (step + back))))]
+            return remote(
+                block,
+                block,
+                send.at[i, parts + step],
+                recv.at[i, parts + step],
+                ctx=place.at(here + direction),
+            )
+
+        def first():
+            for i in every:
+                for part in range(parts):
+                    start = part * self.live
+                    stop = min(start + self.live, ins[i].shape[1])
+                    for half in range(self.down):
+                        rows = slice(half * self.rows, (half + 1) * self.rows)
+                        block = ins[i][rows, start:stop]
+                        stages[i][part, half, :, : stop - start] = block
+                        if stop - start < self.wide:
+                            zeros = jnp.zeros((self.rows, self.wide - stop + start), block.dtype)
+                            stages[i][part, half, :, stop - start :] = zeros
+                for step in (2, 3, 1):
+                    piece(i, step, place.part).start()
+                mine = of(place.ctx)
+                outs[i][(place.part, *mine)] = stages[i][(place.part, *mine)]
+
+        def turn():
+            for i in every:
+                for step in (1, 2, 3):
+                    piece(i, step, (place.part + parts - step) % parts).wait_recv()
+                passing(i, 0).start()
+
+        def forward(step):
+            for i in every:
+                passing(i, step - 1, 1).wait_recv()
+                passing(i, step).start()
+
+        def end():
+            for i in every:
+                passing(i, n - 2, 1).wait_recv()
+            for i in every:
+                for step in (1, 2, 3):
+                    piece(i, step, place.part).wait_send()
+                for step in range(n - 1):
+                    passing(i, step).wait_send()
+
+        return [first, turn] + [functools.partial(forward, s) for s in range(1, n - 1)] + [end]
+
+
+class First:
+    reach = ("fsdp", "ctx", "ring")
+
+    def __init__(self, inputs, vectors, weights, live, cols, seqs):
+        own, width = inputs.shape
+        self.parts = parts = lax.axis_size("fsdp")
+        self.n = lax.axis_size("ctx")
+        self.own, self.live, self.count = own, live, len(vectors)
+        quarter = width // parts
+        self.spread = Spread(weights[1:], live, cols) if Spread.fits(quarter, cols) else None
+        self.swap = Swap(weights[:1] if self.spread else weights, live, cols)
+        self.small = Gather(like((len(vectors), quarter), BF16))
+        self.gather = Gather(like((own, width), BF16))
+        token = like((seqs, 2, own // (seqs // parts) // 2, cols), BF16)
+        self.heads = ToHeads([token] * 3)
+        self.ins = [inputs, *vectors, *weights]
+        self.outs = [
+            *[like((width, cols), BF16)] * 3,
+            like((own, width), F32),
+            like((own, 1), F32),
+            self.gather.outs[0],
+            like((len(vectors), width), F32),
+            *self.heads.outs,
+        ]
+        self.scratch = [
+            pltpu.VMEM((len(vectors), quarter), BF16),
+            pltpu.VMEM((parts, len(vectors), quarter), BF16),
+            pltpu.VMEM((own, width), BF16),
+            pltpu.VMEM((2, cols), F32),
+        ]
+        self.scratch += [pltpu.VMEM(token.shape, BF16)] * 3
+        self.moved = [*self.swap.outs, *(self.spread.outs if self.spread else [])]
+        self.scratch += [pltpu.VMEM(out.shape, BF16) for out in self.moved]
+        for transfer in (self.swap, self.small, self.gather, self.heads):
+            self.scratch += transfer.scratch
+        if self.spread:
+            self.scratch += self.spread.scratch
+
+    def phases(self, place, ins, outs, scratch):
+        inputs, vectors, weights = ins[0], ins[1 : 1 + self.count], ins[1 + self.count :]
+        qkv, (hat, inv, normed_all, full), heads_out = outs[:3], outs[3:7], outs[7:]
+        small_own, small_all, normed, bias, *rest = scratch
+        tokens, rest = rest[:3], rest[3:]
+        moved, rest = rest[:3], rest[3:]
+        swapped = moved[: len(self.swap.outs)]
+        swap = share(self.swap, place, rest, weights[: len(swapped)], swapped)
+        small = share(self.small, place, rest, [small_own], [small_all])
+        gather = share(self.gather, place, rest, [normed], [normed_all])
+        heads = share(self.heads, place, rest, tokens, heads_out)
+        begin_heads = self.heads.begin
+        spread = []
+        if self.spread:
+            spread = share(self.spread, place, rest, weights[1:], moved[1:])
+        parts, live, own = self.parts, self.live, self.own
+        quarter = small_own.shape[1]
+        group = tokens[0].shape[0] // parts
+
+        def begin():
+            for index, vector in enumerate(vectors):
+                small_own[index : index + 1] = vector[...]
+            small[0]()
+            if spread:
+                spread[0]()
+            swap[0]()
+            hat[...], inv[...] = normalize(inputs[...].astype(F32))
+
+        def norm():
+            small[1]()
+            small[2]()
+            for part in range(parts):
+                full[:, part * quarter : (part + 1) * quarter] = small_all[part].astype(F32)
+            normed[...] = (hat[...] * full[0:1] + full[1:2]).astype(BF16)
+            gather[0]()
+            bias[...] = jnp.zeros_like(bias)
+            for part in range(parts):
+
+                @pl.when(place.part == part)
+                def _():
+                    stop = min(live, full.shape[1] - part * live)
+                    bias[:, :stop] = full[2:4, part * live : part * live + stop]
+
+        def arrive():
+            gather[1]()
+            gather[2]()
+            swap[1]()
+
+        def unpack(i):
+            source, target = moved[i], qkv[i]
+            if len(source.shape) == 3:
+                rows = source.shape[1]
+                for part in range(parts):
+                    target[part * rows : (part + 1) * rows] = source[part]
+                return
+            _, down, rows, _ = source.shape
+            for part in range(parts):
+                for half in range(down):
+                    start = (part * down + half) * rows
+                    target[start : start + rows] = source[part, half]
+
+        def project(i):
+            unpack(i)
+            for part in range(parts):
+                rows = dot(normed_all[part], qkv[i][...])
+                if i != 1:
+                    rows = rows + bias[i // 2 : i // 2 + 1]
+                shape = (group, *tokens[i].shape[1:])
+                tokens[i][part * group : (part + 1) * group] = rows.astype(BF16).reshape(shape)
+            begin_heads(i)
+
+        phases = [begin, norm] + spread[1:] + [arrive]
+        self.ready = len(phases)
+        return phases + [functools.partial(project, i) for i in range(3)] + [heads[1]]
 
 
 def results_kernel(widths, parts, order_ref, *refs):
@@ -997,51 +1309,33 @@
     per = n_ctx // parts
     slab = width // n_ctx
 
-    def to_slots(vector):
-        vector = jnp.pad(vector, (0, parts * live - width)).reshape(parts, live)
-        return jnp.pad(vector, ((0, 0), (0, cols - live)))[me_part]
-
-    def by_parts(array):
-        return array.astype(BF16).reshape(parts, own, width)
-
     def by_sequences(array):
         return array.reshape(all_seqs, 2, half_rows, cols)
 
-    def by_slabs(array, count):
-        return array.astype(BF16).reshape(count, -1, array.shape[1])
-
-    small = jnp.concatenate(
-        [ln1_gain, ln1_bias, query_bias, value_bias, out_bias, ln2_gain, ln2_bias, proj_bias]
-    )[None, :]
-    small = lax.all_gather(small, "fsdp", axis=0, tiled=True).astype(F32).reshape(parts, 8, quarter)
-    gain_one, shift_one, bias_query, bias_value, bias_out, gain_two, shift_two, bias_proj = [
-        small[:, i].reshape(-1) for i in range(8)
-    ]
-    bias_query, bias_value = to_slots(bias_query), to_slots(bias_value)
+    x_full = inputs.astype(F32).reshape(own, width)
+    vectors = [ln1_gain, ln1_bias, query_bias, value_bias, out_bias, ln2_gain, ln2_bias, proj_bias]
+    first = First(
+        inputs.reshape(own, width),
+        [vector[None] for vector in vectors],
+        [w_query, w_key, w_value],
+        live,
+        cols,
+        all_seqs,
+    )
+    steps = 3 + (n_ctx if first.spread else 0)
+    (*qkv, hat_one, inv_one, normed_one, full, q_heads, k_heads, v_heads), (fc,), (out_w,) = exchange(
+        0,
+        "first",
+        first,
+        Later(Swap([w_fc], hidden_part, hidden_part), steps, steps + 3),
+        Later(Window(w_out, live, cols), steps, steps + 3),
+    )
+    gain_one, gain_two, bias_proj = full[0], full[5], full[7]
     bias_fc = fc_bias.astype(F32)
-
-    x_full = inputs.astype(F32).reshape(own, width)
-    hat_one, inv_one = normalize(x_full)
-    qkv, (out_w,), (normed_one,) = exchange(
-        0,
-        "start",
-        Swap([w_query, w_key, w_value], live, cols),
-        Window(w_out, live, cols),
-        Gather((hat_one * gain_one + shift_one).astype(BF16)),
-    )
-    qkv = [weight.reshape(width, cols) for weight in qkv]
     normed_one = normed_one.reshape(tokens, width)
-    queries = (dot(normed_one, qkv[0]) + bias_query).astype(BF16)
-    keys = dot(normed_one, qkv[1]).astype(BF16)
-    values = (dot(normed_one, qkv[2]) + bias_value).astype(BF16)
-    heads, (fc,) = exchange(
-        1,
-        "to_heads",
-        ToHeads([by_sequences(a) for a in (queries, keys, values)]),
-        Swap([w_fc], hidden_part, hidden_part),
-    )
     fc = fc.reshape(width, hidden_part)
     proj = w_proj
+    heads = [q_heads, k_heads, v_heads]
 
     q_seq, k_seq, v_seq = [a.reshape(length, piece) for a in heads]
     o_seq, ot, lse = attend(q_seq, k_seq, v_seq, heads_here)
@@ -1052,7 +1346,7 @@
     (attended, resid, hat_two, inv_two, normed_two), (grad_y,) = exchange(
         2,
         "middle",
-        Middle(blocks(o_seq), all_seqs, out_w, x_full, jnp.stack([bias_out, gain_two, shift_two])),
+        Middle(blocks(o_seq), all_seqs, out_w, x_full, full[4:7]),
         Gather(cotangent.reshape(own, width)),
     )
     attended = attended.reshape(tokens, cols)
@@ -1062,16 +1356,13 @@
     pre_act = dot(normed_two, fc) + bias_fc
     value, slope = gelu_both(pre_act)
     activated = value.astype(BF16)
-    mlp = by_parts(dot(activated, proj))
 
     grad_pre = (dot_nt(grad_y, proj) * slope).astype(BF16)
     grad_bias_fc = jnp.sum(grad_pre.astype(F32), axis=0)
-    proj_part = by_slabs(dot_tn(activated, grad_y), n_ctx)
-    fc_part = by_slabs(dot_tn(normed_two, grad_pre), n_ctx)
     (proj_grad, fc_grad), (grad_resid, grad_branch, grad_attended, sums_two) = exchange(
         3,
         "wide_grads",
-        Ring([(proj_part, 1, False), (fc_part, -1, True)]),
+        Ring([(activated, grad_y, 1, False), (normed_two, grad_pre, -1, True)]),
         SecondBack(
             grad_pre, fc, hat_two, inv_two, gain_two[None], cotangent.reshape(own, width), out_w
         ),
@@ -1082,9 +1373,13 @@
     dq_seq, dk_seq, dv_seq = attend_back(
         q_seq, k_seq, v_seq, grad_heads.reshape(length, piece), ot, lse, heads_here
     )
-    (grad_qkv,) = exchange(
-        5, "from_heads_back", FromHeads([blocks(a) for a in (dq_seq, dk_seq, dv_seq)], all_seqs)
+    grad_qkv, (mlp,) = exchange(
+        5,
+        "from_heads_back",
+        Later(FromHeads([blocks(a) for a in (dq_seq, dk_seq, dv_seq)], all_seqs), 0, 4),
+        Product(activated, proj, own),
     )
+    outputs = (resid + mlp + bias_proj).astype(BF16).reshape(seqs, rows, width)
     grad_qkv = [a.reshape(tokens, cols) for a in grad_qkv]
     grad_bias_query = jnp.sum(grad_qkv[0].astype(F32), axis=0)
     grad_bias_value = jnp.sum(grad_qkv[2].astype(F32), axis=0)
@@ -1097,12 +1392,17 @@
         [window(grad_bias_query)[None], window(grad_bias_value)[None], sums_two]
     )
 
-    q_part, k_part, v_part = [by_slabs(dot_tn(normed_one, a), n_ctx) for a in grad_qkv]
-    out_part = by_slabs(dot_tn(attended, grad_branch), n_ctx)
-    (out_grad, q_grad, k_grad, v_grad), (input_grad, small_grads), (mlp,) = exchange(
+    (out_grad, q_grad, k_grad, v_grad), (input_grad, small_grads) = exchange(
         6,
         "narrow_grads",
-        Ring([(out_part, 1, False), (q_part, 1, True), (k_part, -1, True), (v_part, -1, True)]),
+        Ring(
+            [
+                (attended, grad_branch, 1, False),
+                (normed_one, grad_qkv[0], 1, True),
+                (normed_one, grad_qkv[1], -1, True),
+                (normed_one, grad_qkv[2], -1, True),
+            ]
+        ),
         FirstBack(
             grad_qkv,
             qkv,
@@ -1113,9 +1413,7 @@
             small_grads,
             grad_bias_fc.reshape(-1, quarter),
         ),
-        Scatter(mlp),
     )
-    outputs = (resid + mlp + bias_proj).astype(BF16).reshape(seqs, rows, width)
     input_grad = input_grad.reshape(seqs, rows, width)
     fc_out, q_out, k_out, v_out = by_rows(
         [fc_grad, q_grad, k_grad, v_grad],

time: 943 us -> 827 us (0.88)
  matrix products: 81.3 us -> 22 us
  Pallas kernels: 791 us -> 759 us
    dot_general x6 -> x0, matrix products: 36.2 us -> none  [dot_tn(): lax.dot_general(left, right, (((0,), (0,)), ((), ())), preferred_element_...]
    pallas_call x7 -> x6, Pallas kernels: 743 us -> 710 us  [exchange(): pl.pallas_call(functools.partial(exchange_kernel, transfers, places), out...]
    dot_general x5 -> x1, matrix products: 33.6 us -> 11.5 us  [dot(): return jnp.dot(left, right, preferred_element_type=F32)]
    broadcast_in_dim x0 -> x8, local copies, waits for them, and re-layouts: none -> 10.1 us  [on_device(): vector[None]]
  transfers between devices with their start and end apart: 1 -> 1, of which waited for: 0 -> 0; matrix products, arithmetic and copies ran while one was open for 1% -> 2% of each run, Pallas kernels for 1% -> 2%
where the time goes in v4:
time: 827 us; the launch traced here: 821 us
  Pallas kernels  759 us (92%)
  local copies, waits for them, and re-layouts  24.2 us (3%)
  matrix products  22 us (3%)
  other arithmetic  14.1 us (2%)
    pallas_call x6, Pallas kernels, exchange(): pl.pallas_call(functools.partial(exchange_kernel, transfers, places), out...  710 us
    pallas_call x1, Pallas kernels, attend(): pl.pallas_call(functools.partial(attend_kernel, block, heads), grid=(pair...  18.6 us
  transfers between devices with their start and end apart: 1, of which 0 were waited for; matrix products, arithmetic and copies ran while one was open for 2% of the time, Pallas kernels for 2%

profile of v4, /device:TPU:0, one launch (start us, length us, event | category | flops | bytes accessed | tf_op | source)
XLA Modules:
  0.0 821.4 jit_solution(9404080095903207954)
XLA Ops:
  0.7 1.5 copy.34
  2.2 1.3 broadcast_in_dim.31.refs_1_
  3.5 1.3 broadcast_in_dim.32.refs_2_
  4.7 1.3 broadcast_in_dim.33.refs_3_
  12.3 1.4 bitcast_convert_fusion.1.refs_2_
  13.6 135.2 %first.1 = (bf16[1600,512]{1,0:T(8,128)(2,1)}, bf16[1600,512]{1,0:T(8,128)(2,1)}, bf16[1600,512]{1,0:T(8,128)(2,1)}, f32[256,1600]{1,0:T(8,128)}, f32[256,1]{1,0...) custom-call(bf16[256,1600]{1,0:T(8,128)(2,1)} %bitcast.42, ...), custom_call_target="tpu_custom_call" | custom-call | tf_op jit(solution)/shard_map/first/pallas_call | solution.py:778
  148.9 1.4 slice.64.refs_3_
  150.3 1.5 fusion.10
  153.1 18.6 %attend.1 = (bf16[1024,512]{1,0:T(8,128)(2,1)}, f32[4,128,1024]{2,1,0:T(8,128)}, f32[4,2,1024]{2,1,0:T(2,128)}) custom-call(bf16[1024,512]{1,0:T(8,128)(2,1)} %bitcast.52, bf16[1024,512]{1,0:T(8,128)(2,1)} %bitcast.54, bf16[1024,512]{1,0:T(8,128)(2,1)} %bitcast.56), custom_call_target="tpu_custom_call" | custom-call | tf_op jit(solution)/shard_map/attend/pallas_call | solution.py:114
  171.7 80.5 %middle.1 = (bf16[8,2,64,512]{3,2,1,0:T(8,128)(2,1)}, f32[256,1600]{1,0:T(8,128)}, f32[256,1600]{1,0:T(8,128)}, f32[256,1]{1,0:T(8,128)}, bf16[4,256,1600]{2,1,0:T(8,128)(2,1)}, /*index=5*/bf16[4,256,1600]{2,1,0:T(8,128)(2,1)}) custom-call(bf16[16,64,512]{2,1,0:T(8,128)(2,1)} %bitcast.72, bf16[512,1600]{1,0:T(8,128)(2,1)} %get-tuple-element.65.refs_1_.refs_9_, ...), custom_call_target="tpu_custom_call" | custom-call | tf_op jit(solution)/shard_map/middle/pallas_call | solution.py:778
  252.2 11.5 %multiply_convert_fusion = (bf16[1024,1600]{1,0:T(8,128)(2,1)}, f32[1024,1600]{1,0:T(8,128)S(1)}) fusion(f32[1600]{0:T(1024)S(1)} %convert_element_type.33, bf16[1024,1600]{1,0:T(8,128)(2,1)} %bitcast.59, bf16[1600,1600]{1,0:T(8,128)(2,1)} %bitcast.46), kind=kOutput, calls=%fused_computation.10 | convolution fusion | flops 5259264000 | bytes 18233600 | tf_op jit(solution)/shard_map/dot_general | solution.py:49
  263.7 10.5 %convert_reduce_fusion = (f32[1600]{0:T(1024)S(1)}, bf16[1024,1600]{1,0:T(8,128)(2,1)}) fusion(f32[1024,1600]{1,0:T(8,128)S(1)} %get-tuple-element.134, f32[1600]{0:T(1024)S(1)} %convert_element_type.33, bf16[1024,1600]{1,0:T(8,128)(2,1)S(1)} %bitcast.62, bf16[1600,1600]{1,0:T(8,128)(2,1)S(1)} %bitcast.49), kind=kOutput, calls=%fused_computation.9 | convolution fusion | flops 5278923264 | bytes 18240000 | tf_op jit(solution)/shard_map/dot_general | solution.py:53
  274.2 230.0 %wide_grads.1 = (bf16[8,200,1600]{2,1,0:T(8,128)(2,1)}, bf16[8,200,1600]{2,1,0:T(8,128)(2,1)}, f32[256,1600]{1,0:T(8,128)}, bf16[4,256,1600]{2,1,0:T(8,128)(2,1)...) custom-call(bf16[1024,1600]{1,0:T(8,128)(2,1)} %get-tuple-element.133.refs_0_.refs_3_, bf16[1024,1600]{1,0:T(8,128)(2,1)} %bitcast.60, ...), custom_call_target="tpu_custom_call" | custom-call | tf_op jit(solution)/shard_map/wide_grads/pallas_call | solution.py:778
  504.2 27.0 %to_heads_back.1 = bf16[16,64,512]{2,1,0:T(8,128)(2,1)} custom-call(bf16[8,2,64,512]{3,2,1,0:T(8,128)(2,1)} %bitcast.73), custom_call_target="tpu_custom_call" | custom-call | tf_op jit(solution)/shard_map/to_heads_back/pallas_call | solution.py:778
  531.2 15.9 %attend_back.1 = (bf16[1024,512]{1,0:T(8,128)(2,1)}, bf16[1024,512]{1,0:T(8,128)(2,1)}, bf16[1024,512]{1,0:T(8,128)(2,1)}) custom-call(bf16[1024,512]{1,0:T(8,128)(2,1)} %bitcast.53, bf16[1024,512]{1,0:T(8,128)(2,1)} %bitcast.55, bf16[1024,512]{1,0:T(8,128)(2,1)} %bitcast.57, bf16[1024,512]{1,0:T(8,128)(2,1)} %bitcast.58, ...), custom_call_target="tpu_custom_call" | custom-call | tf_op jit(solution)/shard_map/attend_back/pallas_call | solution.py:178
  547.1 78.4 %from_heads_back.1 = (bf16[8,2,64,512]{3,2,1,0:T(8,128)(2,1)}, bf16[8,2,64,512]{3,2,1,0:T(8,128)(2,1)}, bf16[8,2,64,512]{3,2,1,0:T(8,128)(2,1)}, f32[256,1600]{1,0:T(8,128)}) custom-call(bf16[16,64,512]{2,1,0:T(8,128)(2,1)} %bitcast.69, bf16[16,64,512]{2,1,0:T(8,128)(2,1)} %bitcast.70, bf16[16,64,512]{2,1,0:T(8,128)(2,1)} %bitcast.71, ...), custom_call_target="tpu_custom_call" | custom-call | tf_op jit(solution)/shard_map/from_heads_back/pallas_call | solution.py:778
  625.5 1.9 convert_reduce_fusion.1
  629.2 159.3 %narrow_grads.1 = (bf16[8,64,1600]{2,1,0:T(8,128)(2,1)}, bf16[8,200,512]{2,1,0:T(8,128)(2,1)}, bf16[8,200,512]{2,1,0:T(8,128)(2,1)}, bf16[8,200,512]{2,1,0:T(8,1...) custom-call(bf16[1024,512]{1,0:T(8,128)(2,1)} %bitcast.67, bf16[1024,1600]{1,0:T(8,128)(2,1)} %bitcast.64, ...), custom_call_target="tpu_custom_call" | custom-call | tf_op jit(solution)/shard_map/narrow_grads/pallas_call | solution.py:778
  788.5 2.0 slice.72
  790.4 1.3 collective-permute-start
  791.8 7.5 bitcast_convert_fusion
  799.6 2.6 copy.39
  804.6 13.7 %by_rows.1 = (f32[400,6400]{1,0:T(8,128)}, f32[400,1600]{1,0:T(8,128)}, f32[400,1600]{1,0:T(8,128)}, f32[400,1600]{1,0:T(8,128)}) custom-call(s32[4]{0:T(128)} %and_select_fusion.order_ref, bf16[8,200,1600]{2,1,0:T(8,128)(2,1)} %get-tuple-element.94.refs_0_.refs_1_.refs_2_.refs_3_, bf16[8,200,1600]{2,1,0:T(8,128)(2,1)} %get-tuple-element.94.refs_0_.refs_1_.refs_2_.refs_3_, ...), custom_call_target="tpu_custom_call" | custom-call | tf_op jit(solution)/shard_map/by_rows/pallas_call | solution.py:1257
  819.0 2.0 fusion.8
  (46 shorter events, 12.7 us)
Async XLA Ops:
  2.2 11.5 %copy-start = (bf16[2,128,1600]{2,1,0:T(8,128)(2,1)}, bf16[2,128,1600]{2,1,0:T(8,128)(2,1)S(1)}, u32[]{:S(2)}) copy-start(bf16[2,128,1600]{2,1,0:T(8,128)(2,1)S(1)} %copy.34) | copy-start | bytes 2457604
  13.6 138.2 %copy-start.5 = (bf16[2,128,1600]{1,2,0:T(8,128)(2,1)S(1)}, bf16[2,128,1600]{1,2,0:T(8,128)(2,1)}, u32[]{:S(2)}) copy-start(bf16[2,128,1600]{1,2,0:T(8,128)(2,1)} %param.18) | copy-start | bytes 2457604
  13.6 139.4 %copy-start.8 = (bf16[1600]{0:T(1024)(128)(2,1)S(1)}, bf16[1600]{0:T(1024)(128)(2,1)}, u32[]{:S(2)}) copy-start(bf16[1600]{0:T(1024)(128)(2,1)} %param.32) | copy-start | bytes 9604
  171.6 92.1 %slice-start = ((s8[5324800]{0:T(1024)(128)(4,1)}), s8[1130496]{0:T(1024)(128)(4,1)S(1)}, s32[]{:S(2)}) async-start(s8[5324800]{0:T(1024)(128)(4,1)} %bitcast.48), calls=%async_computation | async-start | bytes 2260992
  252.2 11.5 %slice-start.1 = ((s8[5324800]{0:T(1024)(128)(4,1)}), s8[4194304]{0:T(1024)(128)(4,1)S(1)}, s32[]{:S(2)}) async-start(s8[5324800]{0:T(1024)(128)(4,1)} %bitcast.48), calls=%async_computation.1 | async-start | bytes 8388608
  252.2 11.5 %copy-start.1 = (bf16[4,256,1600]{2,1,0:T(8,128)(2,1)S(1)}, bf16[4,256,1600]{2,1,0:T(8,128)(2,1)}, u32[]{:S(2)}) copy-start(bf16[4,256,1600]{2,1,0:T(8,128)(2,1)} %get-tuple-element.70) | copy-start | bytes 9830404
  547.1 81.4 %copy-start.6 = (f32[4,1600]{1,0:T(4,128)S(1)}, f32[4,1600]{1,0:T(4,128)}, u32[]{:S(2)}) copy-start(f32[4,1600]{1,0:T(4,128)} %get-tuple-element.92) | copy-start | bytes 76804
  790.4 28.6 %collective-permute-start = (bf16[192,1600]{1,0:T(8,128)(2,1)}, bf16[192,1600]{1,0:T(8,128)(2,1)S(1)}, u32[]{:S(2)}, u32[]{:S(2)}) collective-permute-start(bf16[192,1600]{1,0:T(8,128)(2,1)} %bitcast.22), channel_id=1, source_target_pairs={{0,1},{1,2},{2,3},{4,5},{5,6},{6,7},{8,9},{9,10},{10,11},{12,13},{... | collective-permute-start | bytes 1843208 | tf_op jit(solution)/shard_map/ppermute | solution.py:1426
  791.8 7.5 copy-start.3
  791.8 7.5 copy-start.4
  791.8 7.7 copy-start.2
  799.3 3.0 copy-start.7

commit v5 on v4

--- a/solution.py
+++ b/solution.py
@@ -382,8 +382,21 @@
                 self.target(outs[i], me, half)[...] = self.source(ins[i], me, half)[...]
 
         def first():
-            for i in range(len(ins)):
-                begin(i)
+            def start(step, _):
+                other = (me + step) % n
+                for i, half in every:
+                    remote(
+                        self.source(ins[i], other, half),
+                        self.target(outs[i], me, half),
+                        send.at[i, half, step],
+                        recv.at[i, half, step],
+                        ctx=other,
+                    ).start()
+                return 0
+
+            lax.fori_loop(1, n, start, 0)
+            for i, half in every:
+                self.target(outs[i], me, half)[...] = self.source(ins[i], me, half)[...]
 
         self.begin = begin
 
@@ -553,25 +566,24 @@
         self.per = n // self.parts
         self.products, self.streams, lefts = [], [], []
         self.ins, self.outs, slots, local, turned = [], [], [], [], []
-        ways = [direction for _, _, direction, _ in products]
-        for left, right, direction, crossing in products:
+        for left, right, widths, crossing in products:
             rows, columns = left.shape[1] // n, right.shape[1]
             known = [k for k, other in enumerate(lefts) if other is left]
             if not known:
                 lefts.append(left)
                 turned.append(pltpu.VMEM((n, rows, left.shape[0]), left.dtype))
             index = len(self.products)
-            self.products.append((known[0] if known else len(lefts) - 1, direction, crossing))
+            self.products.append((known[0] if known else len(lefts) - 1, crossing))
             self.ins.append(right)
             self.outs.append(like((n, rows, columns), BF16))
             slots.append(pltpu.VMEM((n - 1, rows, columns), BF16))
             local.append(pltpu.VMEM((2, rows, columns), BF16))
-            middle = columns
-            if ways.count(direction) == 1:
-                middle = (columns // 2 + LANES - 1) // LANES * LANES
-            self.streams.append((index, slice(0, middle)))
-            if middle < columns:
-                self.streams.append((index, slice(middle, columns)))
+            start = 0
+            for direction, count in zip((1, -1), widths):
+                if count:
+                    self.streams.append((index, slice(start, start + count), direction))
+                start += count
+        self.streams.sort(key=lambda stream: not self.products[stream[0]][1])
         self.counts = (len(lefts), len(products))
         self.ins = lefts + self.ins
         self.spaces = [pl.ANY] * len(self.outs)
@@ -589,20 +601,22 @@
         owner = (place.part + shift) % parts
 
         def make(step):
-            for index, (left, direction, crosses) in enumerate(self.products):
+            for stream, (index, columns, direction) in enumerate(self.streams):
                 slab = place.at(here - direction * (step + 1))
-                if crosses:
+                if crosses(stream):
                     slab = (slab + per * place.part) % n
-                local[index][step % 2] = dot(turned[left][slab], rights[index][...]).astype(BF16)
+                left = turned[self.products[index][0]]
+                own = dot(left[slab], rights[index][:, columns])
+                local[index][step % 2, :, columns] = own.astype(BF16)
 
         def way(stream):
+            return self.streams[stream][2]
+
+        def crosses(stream):
             return self.products[self.streams[stream][0]][1]
 
-        def crosses(stream):
-            return self.products[self.streams[stream][0]][2]
-
         def reducing(stream, step):
-            index, columns = self.streams[stream]
+            index, columns, _ = self.streams[stream]
             source = local[index].at[0] if step == 0 else slots[index].at[step - 1]
             return remote(
                 source.at[:, columns],
@@ -613,11 +627,11 @@
             )
 
         def last(stream):
-            index, columns = self.streams[stream]
+            index, columns, _ = self.streams[stream]
             return slots[index].at[n - 2, :, columns]
 
         def mine(stream):
-            index, columns = self.streams[stream]
+            index, columns, _ = self.streams[stream]
             return outs[index].at[place.ctx, :, columns]
 
         def crossing(stream):
@@ -633,7 +647,7 @@
             return pltpu.make_async_copy(last(stream), mine(stream), send.at[stream, 0, n - 1])
 
         def gathering(stream, step, back=0):
-            index, columns = self.streams[stream]
+            index, columns, _ = self.streams[stream]
             slab = place.at(here - way(stream) * (step + back))
             block = outs[index].at[slab, :, columns]
             source = block
@@ -660,7 +674,7 @@
             make(1)
 
         def add(stream, step):
-            index, columns = self.streams[stream]
+            index, columns, _ = self.streams[stream]
             reducing(stream, step).wait_recv()
             total = slots[index][step, :, columns].astype(F32)
             total = total + local[index][(step + 1) % 2, :, columns].astype(F32)
@@ -691,24 +705,25 @@
                 def _():
                     crossing(stream).start()
 
-        def launch():
-            for stream in every:
-                if crosses(stream):
-
-                    @pl.when(shift == 0)
-                    def _():
-                        keeping(stream).wait()
-
-                    @pl.when(shift != 0)
-                    def _():
-                        crossing(stream).wait()
-
-                    gathering(stream, 0).start()
-
-        def forward(step):
-            for stream in every:
-                gathering(stream, step - 1, 1).wait_recv()
-                gathering(stream, step).start()
+        def launch(stream):
+            @pl.when(shift == 0)
+            def _():
+                keeping(stream).wait()
+
+            @pl.when(shift != 0)
+            def _():
+                crossing(stream).wait()
+
+            gathering(stream, 0).start()
+
+        def forward(turn):
+            for stream in [s for s in every if not crosses(s)] + [s for s in every if crosses(s)]:
+                step = turn - 1 if crosses(stream) else turn
+                if step == 0:
+                    launch(stream)
+                elif step < n - 1:
+                    gathering(stream, step - 1, 1).wait_recv()
+                    gathering(stream, step).start()
 
         def end():
             for stream in every:
@@ -723,8 +738,8 @@
 
         steps = [begin]
         steps += [functools.partial(reduce, step) for step in range(1, n - 1)]
-        steps += [turn, launch]
-        steps += [functools.partial(forward, step) for step in range(1, n - 1)]
+        steps += [turn]
+        steps += [functools.partial(forward, step) for step in range(1, n)]
         return steps + [end]
 
 
@@ -1171,7 +1186,7 @@
 
         def begin():
             for index, vector in enumerate(vectors):
-                small_own[index : index + 1] = vector[...]
+                small_own[index : index + 1] = vector[...].reshape(1, quarter)
             small[0]()
             if spread:
                 spread[0]()
@@ -1312,11 +1327,15 @@
     def by_sequences(array):
         return array.reshape(all_seqs, 2, half_rows, cols)
 
+    def uneven(columns, more=1):
+        low = (columns // 2 + more * (LANES - 1)) // LANES * LANES
+        return (low, columns - low)
+
     x_full = inputs.astype(F32).reshape(own, width)
     vectors = [ln1_gain, ln1_bias, query_bias, value_bias, out_bias, ln2_gain, ln2_bias, proj_bias]
     first = First(
         inputs.reshape(own, width),
-        [vector[None] for vector in vectors],
+        vectors,
         [w_query, w_key, w_value],
         live,
         cols,
@@ -1362,7 +1381,12 @@
     (proj_grad, fc_grad), (grad_resid, grad_branch, grad_attended, sums_two) = exchange(
         3,
         "wide_grads",
-        Ring([(activated, grad_y, 1, False), (normed_two, grad_pre, -1, True)]),
+        Ring(
+            [
+                (activated, grad_y, uneven(width), False),
+                (normed_two, grad_pre, uneven(hidden_part, 0), True),
+            ]
+        ),
         SecondBack(
             grad_pre, fc, hat_two, inv_two, gain_two[None], cotangent.reshape(own, width), out_w
         ),
@@ -1397,10 +1421,10 @@
         "narrow_grads",
         Ring(
             [
-                (attended, grad_branch, 1, False),
-                (normed_one, grad_qkv[0], 1, True),
-                (normed_one, grad_qkv[1], -1, True),
-                (normed_one, grad_qkv[2], -1, True),
+                (attended, grad_branch, uneven(width), False),
+                (normed_one, grad_qkv[0], (cols, 0), True),
+                (normed_one, grad_qkv[1], (0, cols), True),
+                (normed_one, grad_qkv[2], uneven(cols), True),
             ]
         ),
         FirstBack(

time: 827 us -> 808 us (0.977)
  local copies, waits for them, and re-layouts: 24.2 us -> 14.1 us
  Pallas kernels: 759 us -> 750 us
    broadcast_in_dim x8 -> x0, local copies, waits for them, and re-layouts: 10.1 us -> none  [on_device(): vector[None]]
    pallas_call x6, Pallas kernels: 710 us -> 702 us  [exchange(): pl.pallas_call(functools.partial(exchange_kernel, transfers, places), out...]
where the time goes in v5:
time: 808 us; the launch traced here: 803 us
  Pallas kernels  750 us (93%)
  matrix products  22 us (3%)
  other arithmetic  14.2 us (2%)
  local copies, waits for them, and re-layouts  14.1 us (2%)
    pallas_call x6, Pallas kernels, exchange(): pl.pallas_call(functools.partial(exchange_kernel, transfers, places), out...  702 us
    pallas_call x1, Pallas kernels, attend(): pl.pallas_call(functools.partial(attend_kernel, block, heads), grid=(pair...  18.6 us
  transfers between devices with their start and end apart: 1, of which 0 were waited for; matrix products, arithmetic and copies ran while one was open for 2% of the time, Pallas kernels for 2%

profile of v5, /device:TPU:0, one launch (start us, length us, event | category | flops | bytes accessed | tf_op | source)
XLA Modules:
  0.0 803.0 jit_solution(9574543274616184384)
XLA Ops:
  0.7 1.5 copy.34
  2.2 1.5 bitcast_convert_fusion.1.refs_2_
  3.6 135.2 %first.1 = (bf16[1600,512]{1,0:T(8,128)(2,1)}, bf16[1600,512]{1,0:T(8,128)(2,1)}, bf16[1600,512]{1,0:T(8,128)(2,1)}, f32[256,1600]{1,0:T(8,128)}, f32[256,1]{1,0...) custom-call(bf16[256,1600]{1,0:T(8,128)(2,1)} %bitcast.44, ...), custom_call_target="tpu_custom_call" | custom-call | tf_op jit(solution)/shard_map/first/pallas_call | solution.py:793
  138.9 1.4 slice.64.refs_3_
  140.3 1.5 fusion.10
  141.8 1.2 copy.35
  143.1 18.6 %attend.1 = (bf16[1024,512]{1,0:T(8,128)(2,1)}, f32[4,128,1024]{2,1,0:T(8,128)}, f32[4,2,1024]{2,1,0:T(2,128)}) custom-call(bf16[1024,512]{1,0:T(8,128)(2,1)} %bitcast.52, bf16[1024,512]{1,0:T(8,128)(2,1)} %bitcast.54, bf16[1024,512]{1,0:T(8,128)(2,1)} %bitcast.56), custom_call_target="tpu_custom_call" | custom-call | tf_op jit(solution)/shard_map/attend/pallas_call | solution.py:114
  161.6 80.5 %middle.1 = (bf16[8,2,64,512]{3,2,1,0:T(8,128)(2,1)}, f32[256,1600]{1,0:T(8,128)}, f32[256,1600]{1,0:T(8,128)}, f32[256,1]{1,0:T(8,128)}, bf16[4,256,1600]{2,1,0:T(8,128)(2,1)}, /*index=5*/bf16[4,256,1600]{2,1,0:T(8,128)(2,1)}) custom-call(bf16[16,64,512]{2,1,0:T(8,128)(2,1)} %bitcast.72, bf16[512,1600]{1,0:T(8,128)(2,1)} %get-tuple-element.65.refs_1_.refs_9_, ...), custom_call_target="tpu_custom_call" | custom-call | tf_op jit(solution)/shard_map/middle/pallas_call | solution.py:793
  242.2 11.5 %multiply_convert_fusion = (bf16[1024,1600]{1,0:T(8,128)(2,1)}, f32[1024,1600]{1,0:T(8,128)S(1)}) fusion(f32[1600]{0:T(1024)S(1)} %convert_element_type.33, bf16[1024,1600]{1,0:T(8,128)(2,1)} %bitcast.59, bf16[1600,1600]{1,0:T(8,128)(2,1)} %bitcast.46), kind=kOutput, calls=%fused_computation.10 | convolution fusion | flops 5259264000 | bytes 18233600 | tf_op jit(solution)/shard_map/dot_general | solution.py:49
  253.7 10.5 %convert_reduce_fusion = (f32[1600]{0:T(1024)S(1)}, bf16[1024,1600]{1,0:T(8,128)(2,1)}) fusion(f32[1024,1600]{1,0:T(8,128)S(1)} %get-tuple-element.134, f32[1600]{0:T(1024)S(1)} %convert_element_type.33, bf16[1024,1600]{1,0:T(8,128)(2,1)S(1)} %bitcast.62, bf16[1600,1600]{1,0:T(8,128)(2,1)S(1)} %bitcast.49), kind=kOutput, calls=%fused_computation.9 | convolution fusion | flops 5278923264 | bytes 18240000 | tf_op jit(solution)/shard_map/dot_general | solution.py:53
  264.2 229.4 %wide_grads.1 = (bf16[8,200,1600]{2,1,0:T(8,128)(2,1)}, bf16[8,200,1600]{2,1,0:T(8,128)(2,1)}, f32[256,1600]{1,0:T(8,128)}, bf16[4,256,1600]{2,1,0:T(8,128)(2,1)...) custom-call(bf16[1024,1600]{1,0:T(8,128)(2,1)} %get-tuple-element.133.refs_0_.refs_3_, bf16[1024,1600]{1,0:T(8,128)(2,1)} %bitcast.60, ...), custom_call_target="tpu_custom_call" | custom-call | tf_op jit(solution)/shard_map/wide_grads/pallas_call | solution.py:793
  493.7 21.0 %to_heads_back.1 = bf16[16,64,512]{2,1,0:T(8,128)(2,1)} custom-call(bf16[8,2,64,512]{3,2,1,0:T(8,128)(2,1)} %bitcast.73), custom_call_target="tpu_custom_call" | custom-call | tf_op jit(solution)/shard_map/to_heads_back/pallas_call | solution.py:793
  514.7 15.9 %attend_back.1 = (bf16[1024,512]{1,0:T(8,128)(2,1)}, bf16[1024,512]{1,0:T(8,128)(2,1)}, bf16[1024,512]{1,0:T(8,128)(2,1)}) custom-call(bf16[1024,512]{1,0:T(8,128)(2,1)} %bitcast.53, bf16[1024,512]{1,0:T(8,128)(2,1)} %bitcast.55, bf16[1024,512]{1,0:T(8,128)(2,1)} %bitcast.57, bf16[1024,512]{1,0:T(8,128)(2,1)} %bitcast.58, ...), custom_call_target="tpu_custom_call" | custom-call | tf_op jit(solution)/shard_map/attend_back/pallas_call | solution.py:178
  530.6 66.5 %from_heads_back.1 = (bf16[8,2,64,512]{3,2,1,0:T(8,128)(2,1)}, bf16[8,2,64,512]{3,2,1,0:T(8,128)(2,1)}, bf16[8,2,64,512]{3,2,1,0:T(8,128)(2,1)}, f32[256,1600]{1,0:T(8,128)}) custom-call(bf16[16,64,512]{2,1,0:T(8,128)(2,1)} %bitcast.69, bf16[16,64,512]{2,1,0:T(8,128)(2,1)} %bitcast.70, bf16[16,64,512]{2,1,0:T(8,128)(2,1)} %bitcast.71, ...), custom_call_target="tpu_custom_call" | custom-call | tf_op jit(solution)/shard_map/from_heads_back/pallas_call | solution.py:793
  597.1 1.9 convert_reduce_fusion.1
  600.8 169.2 %narrow_grads.1 = (bf16[8,64,1600]{2,1,0:T(8,128)(2,1)}, bf16[8,200,512]{2,1,0:T(8,128)(2,1)}, bf16[8,200,512]{2,1,0:T(8,128)(2,1)}, bf16[8,200,512]{2,1,0:T(8,1...) custom-call(bf16[1024,512]{1,0:T(8,128)(2,1)} %bitcast.67, bf16[1024,1600]{1,0:T(8,128)(2,1)} %bitcast.64, ...), custom_call_target="tpu_custom_call" | custom-call | tf_op jit(solution)/shard_map/narrow_grads/pallas_call | solution.py:793
  770.0 2.0 slice.72
  772.0 1.3 collective-permute-start
  773.3 7.5 bitcast_convert_fusion
  781.1 2.6 copy.39
  783.8 0.7 reshape.141
  784.5 1.2 copy.38
  786.2 13.7 %by_rows.1 = (f32[400,6400]{1,0:T(8,128)}, f32[400,1600]{1,0:T(8,128)}, f32[400,1600]{1,0:T(8,128)}, f32[400,1600]{1,0:T(8,128)}) custom-call(s32[4]{0:T(128)} %and_select_fusion.order_ref, bf16[8,200,1600]{2,1,0:T(8,128)(2,1)} %get-tuple-element.94.refs_0_.refs_1_.refs_2_.refs_3_, bf16[8,200,1600]{2,1,0:T(8,128)(2,1)} %get-tuple-element.94.refs_0_.refs_1_.refs_2_.refs_3_, ...), custom_call_target="tpu_custom_call" | custom-call | tf_op jit(solution)/shard_map/by_rows/pallas_call | solution.py:1272
  800.5 2.0 fusion.8
  (38 shorter events, 3.2 us)
Async XLA Ops:
  2.2 1.5 copy-start
  3.6 138.2 %copy-start.5 = (bf16[2,128,1600]{1,2,0:T(8,128)(2,1)S(1)}, bf16[2,128,1600]{1,2,0:T(8,128)(2,1)}, u32[]{:S(2)}) copy-start(bf16[2,128,1600]{1,2,0:T(8,128)(2,1)} %param.18) | copy-start | bytes 2457604
  3.6 139.4 %copy-start.8 = (bf16[1600]{0:T(1024)(128)(2,1)S(1)}, bf16[1600]{0:T(1024)(128)(2,1)}, u32[]{:S(2)}) copy-start(bf16[1600]{0:T(1024)(128)(2,1)} %param.32) | copy-start | bytes 9604
  161.6 92.1 %slice-start = ((s8[5324800]{0:T(1024)(128)(4,1)}), s8[1130496]{0:T(1024)(128)(4,1)S(1)}, s32[]{:S(2)}) async-start(s8[5324800]{0:T(1024)(128)(4,1)} %bitcast.48), calls=%async_computation | async-start | bytes 2260992
  242.2 11.5 %slice-start.1 = ((s8[5324800]{0:T(1024)(128)(4,1)}), s8[4194304]{0:T(1024)(128)(4,1)S(1)}, s32[]{:S(2)}) async-start(s8[5324800]{0:T(1024)(128)(4,1)} %bitcast.48), calls=%async_computation.1 | async-start | bytes 8388608
  242.2 11.5 %copy-start.1 = (bf16[4,256,1600]{2,1,0:T(8,128)(2,1)S(1)}, bf16[4,256,1600]{2,1,0:T(8,128)(2,1)}, u32[]{:S(2)}) copy-start(bf16[4,256,1600]{2,1,0:T(8,128)(2,1)} %get-tuple-element.70) | copy-start | bytes 9830404
  530.6 69.5 %copy-start.6 = (f32[4,1600]{1,0:T(4,128)S(1)}, f32[4,1600]{1,0:T(4,128)}, u32[]{:S(2)}) copy-start(f32[4,1600]{1,0:T(4,128)} %get-tuple-element.92) | copy-start | bytes 76804
  772.0 28.6 %collective-permute-start = (bf16[192,1600]{1,0:T(8,128)(2,1)}, bf16[192,1600]{1,0:T(8,128)(2,1)S(1)}, u32[]{:S(2)}, u32[]{:S(2)}) collective-permute-start(bf16[192,1600]{1,0:T(8,128)(2,1)} %bitcast.22), channel_id=1, source_target_pairs={{0,1},{1,2},{2,3},{4,5},{5,6},{6,7},{8,9},{9,10},{10,11},{12,13},{... | collective-permute-start | bytes 1843208 | tf_op jit(solution)/shard_map/ppermute | solution.py:1450
  773.3 7.5 copy-start.3
  773.3 7.5 copy-start.4
  773.3 7.7 copy-start.2
  780.8 3.0 copy-start.7

commit v6 on v5

--- a/solution.py
+++ b/solution.py
@@ -566,7 +566,7 @@
         self.per = n // self.parts
         self.products, self.streams, lefts = [], [], []
         self.ins, self.outs, slots, local, turned = [], [], [], [], []
-        for left, right, widths, crossing in products:
+        for left, right, heights, crossing in products:
             rows, columns = left.shape[1] // n, right.shape[1]
             known = [k for k, other in enumerate(lefts) if other is left]
             if not known:
@@ -579,7 +579,7 @@
             slots.append(pltpu.VMEM((n - 1, rows, columns), BF16))
             local.append(pltpu.VMEM((2, rows, columns), BF16))
             start = 0
-            for direction, count in zip((1, -1), widths):
+            for direction, count in zip((1, -1), heights):
                 if count:
                     self.streams.append((index, slice(start, start + count), direction))
                 start += count
@@ -601,13 +601,13 @@
         owner = (place.part + shift) % parts
 
         def make(step):
-            for stream, (index, columns, direction) in enumerate(self.streams):
+            for stream, (index, part, direction) in enumerate(self.streams):
                 slab = place.at(here - direction * (step + 1))
                 if crosses(stream):
                     slab = (slab + per * place.part) % n
                 left = turned[self.products[index][0]]
-                own = dot(left[slab], rights[index][:, columns])
-                local[index][step % 2, :, columns] = own.astype(BF16)
+                own = dot(left[slab, part], rights[index][...])
+                local[index][step % 2, part] = own.astype(BF16)
 
         def way(stream):
             return self.streams[stream][2]
@@ -616,23 +616,23 @@
             return self.products[self.streams[stream][0]][1]
 
         def reducing(stream, step):
-            index, columns, _ = self.streams[stream]
+            index, part, _ = self.streams[stream]
             source = local[index].at[0] if step == 0 else slots[index].at[step - 1]
             return remote(
-                source.at[:, columns],
-                slots[index].at[step, :, columns],
+                source.at[part],
+                slots[index].at[step, part],
                 send.at[stream, 0, step],
                 recv.at[stream, 0, step],
                 ctx=place.at(here + way(stream)),
             )
 
         def last(stream):
-            index, columns, _ = self.streams[stream]
-            return slots[index].at[n - 2, :, columns]
+            index, part, _ = self.streams[stream]
+            return slots[index].at[n - 2, part]
 
         def mine(stream):
-            index, columns, _ = self.streams[stream]
-            return outs[index].at[place.ctx, :, columns]
+            index, part, _ = self.streams[stream]
+            return outs[index].at[place.ctx, part]
 
         def crossing(stream):
             return remote(
@@ -647,9 +647,9 @@
             return pltpu.make_async_copy(last(stream), mine(stream), send.at[stream, 0, n - 1])
 
         def gathering(stream, step, back=0):
-            index, columns, _ = self.streams[stream]
+            index, part, _ = self.streams[stream]
             slab = place.at(here - way(stream) * (step + back))
-            block = outs[index].at[slab, :, columns]
+            block = outs[index].at[slab, part]
             source = block
             if step == 0 and back == 0 and not crosses(stream):
                 source = last(stream)
@@ -674,11 +674,11 @@
             make(1)
 
         def add(stream, step):
-            index, columns, _ = self.streams[stream]
+            index, part, _ = self.streams[stream]
             reducing(stream, step).wait_recv()
-            total = slots[index][step, :, columns].astype(F32)
-            total = total + local[index][(step + 1) % 2, :, columns].astype(F32)
-            slots[index][step, :, columns] = total.astype(BF16)
+            total = slots[index][step, part].astype(F32)
+            total = total + local[index][(step + 1) % 2, part].astype(F32)
+            slots[index][step, part] = total.astype(BF16)
 
         def reduce(step):
             for stream in every:
@@ -1327,9 +1327,9 @@
     def by_sequences(array):
         return array.reshape(all_seqs, 2, half_rows, cols)
 
-    def uneven(columns, more=1):
-        low = (columns // 2 + more * (LANES - 1)) // LANES * LANES
-        return (low, columns - low)
+    def split(rows, more):
+        low = (rows // 2 + 7 * more) // 8 * 8
+        return (low, rows - low)
 
     x_full = inputs.astype(F32).reshape(own, width)
     vectors = [ln1_gain, ln1_bias, query_bias, value_bias, out_bias, ln2_gain, ln2_bias, proj_bias]
@@ -1383,8 +1383,8 @@
         "wide_grads",
         Ring(
             [
-                (activated, grad_y, uneven(width), False),
-                (normed_two, grad_pre, uneven(hidden_part, 0), True),
+                (activated, grad_y, split(slab, 1), False),
+                (normed_two, grad_pre, split(slab, 0), True),
             ]
         ),
         SecondBack(
@@ -1421,10 +1421,10 @@
         "narrow_grads",
         Ring(
             [
-                (attended, grad_branch, uneven(width), False),
-                (normed_one, grad_qkv[0], (cols, 0), True),
-                (normed_one, grad_qkv[1], (0, cols), True),
-                (normed_one, grad_qkv[2], uneven(cols), True),
+                (attended, grad_branch, split(cols // n_ctx, 0), False),
+                (normed_one, grad_qkv[0], (slab, 0), True),
+                (normed_one, grad_qkv[1], (0, slab), True),
+                (normed_one, grad_qkv[2], split(slab, 1), True),
             ]
         ),
         FirstBack(

time: 808 us -> 807 us (level)
  no operation moved by 1% of the time
where the time goes in v6:
time: 807 us; the launch traced here: 803 us
  Pallas kernels  750 us (93%)
  matrix products  22 us (3%)
  local copies, waits for them, and re-layouts  14.3 us (2%)
  other arithmetic  14.2 us (2%)
    pallas_call x6, Pallas kernels, exchange(): pl.pallas_call(functools.partial(exchange_kernel, transfers, places), out...  701 us
    pallas_call x1, Pallas kernels, attend(): pl.pallas_call(functools.partial(attend_kernel, block, heads), grid=(pair...  18.6 us
  transfers between devices with their start and end apart: 1, of which 0 were waited for; matrix products, arithmetic and copies ran while one was open for 2% of the time, Pallas kernels for 2%

profile of v6, /device:TPU:0, one launch (start us, length us, event | category | flops | bytes accessed | tf_op | source)
XLA Modules:
  0.0 802.7 jit_solution(18349568864230017179)
XLA Ops:
  0.7 1.5 copy.34
  2.2 1.5 bitcast_convert_fusion.1.refs_2_
  3.6 135.5 %first.1 = (bf16[1600,512]{1,0:T(8,128)(2,1)}, bf16[1600,512]{1,0:T(8,128)(2,1)}, bf16[1600,512]{1,0:T(8,128)(2,1)}, f32[256,1600]{1,0:T(8,128)}, f32[256,1]{1,0...) custom-call(bf16[256,1600]{1,0:T(8,128)(2,1)} %bitcast.44, ...), custom_call_target="tpu_custom_call" | custom-call | tf_op jit(solution)/shard_map/first/pallas_call | solution.py:793
  139.2 1.4 slice.64.refs_3_
  140.6 1.5 fusion.10
  142.2 1.2 copy.35
  143.4 18.6 %attend.1 = (bf16[1024,512]{1,0:T(8,128)(2,1)}, f32[4,128,1024]{2,1,0:T(8,128)}, f32[4,2,1024]{2,1,0:T(2,128)}) custom-call(bf16[1024,512]{1,0:T(8,128)(2,1)} %bitcast.52, bf16[1024,512]{1,0:T(8,128)(2,1)} %bitcast.54, bf16[1024,512]{1,0:T(8,128)(2,1)} %bitcast.56), custom_call_target="tpu_custom_call" | custom-call | tf_op jit(solution)/shard_map/attend/pallas_call | solution.py:114
  162.0 80.8 %middle.1 = (bf16[8,2,64,512]{3,2,1,0:T(8,128)(2,1)}, f32[256,1600]{1,0:T(8,128)}, f32[256,1600]{1,0:T(8,128)}, f32[256,1]{1,0:T(8,128)}, bf16[4,256,1600]{2,1,0:T(8,128)(2,1)}, /*index=5*/bf16[4,256,1600]{2,1,0:T(8,128)(2,1)}) custom-call(bf16[16,64,512]{2,1,0:T(8,128)(2,1)} %bitcast.72, bf16[512,1600]{1,0:T(8,128)(2,1)} %get-tuple-element.65.refs_1_.refs_9_, ...), custom_call_target="tpu_custom_call" | custom-call | tf_op jit(solution)/shard_map/middle/pallas_call | solution.py:793
  242.8 11.5 %multiply_convert_fusion = (bf16[1024,1600]{1,0:T(8,128)(2,1)}, f32[1024,1600]{1,0:T(8,128)S(1)}) fusion(f32[1600]{0:T(1024)S(1)} %convert_element_type.33, bf16[1024,1600]{1,0:T(8,128)(2,1)} %bitcast.59, bf16[1600,1600]{1,0:T(8,128)(2,1)} %bitcast.46), kind=kOutput, calls=%fused_computation.10 | convolution fusion | flops 5259264000 | bytes 18233600 | tf_op jit(solution)/shard_map/dot_general | solution.py:49
  254.4 10.5 %convert_reduce_fusion = (f32[1600]{0:T(1024)S(1)}, bf16[1024,1600]{1,0:T(8,128)(2,1)}) fusion(f32[1024,1600]{1,0:T(8,128)S(1)} %get-tuple-element.134, f32[1600]{0:T(1024)S(1)} %convert_element_type.33, bf16[1024,1600]{1,0:T(8,128)(2,1)S(1)} %bitcast.62, bf16[1600,1600]{1,0:T(8,128)(2,1)S(1)} %bitcast.49), kind=kOutput, calls=%fused_computation.9 | convolution fusion | flops 5278923264 | bytes 18240000 | tf_op jit(solution)/shard_map/dot_general | solution.py:53
  264.9 229.5 %wide_grads.1 = (bf16[8,200,1600]{2,1,0:T(8,128)(2,1)}, bf16[8,200,1600]{2,1,0:T(8,128)(2,1)}, f32[256,1600]{1,0:T(8,128)}, bf16[4,256,1600]{2,1,0:T(8,128)(2,1)...) custom-call(bf16[1024,1600]{1,0:T(8,128)(2,1)} %get-tuple-element.133.refs_0_.refs_3_, bf16[1024,1600]{1,0:T(8,128)(2,1)} %bitcast.60, ...), custom_call_target="tpu_custom_call" | custom-call | tf_op jit(solution)/shard_map/wide_grads/pallas_call | solution.py:793
  494.3 20.4 %to_heads_back.1 = bf16[16,64,512]{2,1,0:T(8,128)(2,1)} custom-call(bf16[8,2,64,512]{3,2,1,0:T(8,128)(2,1)} %bitcast.73), custom_call_target="tpu_custom_call" | custom-call | tf_op jit(solution)/shard_map/to_heads_back/pallas_call | solution.py:793
  514.8 15.9 %attend_back.1 = (bf16[1024,512]{1,0:T(8,128)(2,1)}, bf16[1024,512]{1,0:T(8,128)(2,1)}, bf16[1024,512]{1,0:T(8,128)(2,1)}) custom-call(bf16[1024,512]{1,0:T(8,128)(2,1)} %bitcast.53, bf16[1024,512]{1,0:T(8,128)(2,1)} %bitcast.55, bf16[1024,512]{1,0:T(8,128)(2,1)} %bitcast.57, bf16[1024,512]{1,0:T(8,128)(2,1)} %bitcast.58, ...), custom_call_target="tpu_custom_call" | custom-call | tf_op jit(solution)/shard_map/attend_back/pallas_call | solution.py:178
  530.7 66.5 %from_heads_back.1 = (bf16[8,2,64,512]{3,2,1,0:T(8,128)(2,1)}, bf16[8,2,64,512]{3,2,1,0:T(8,128)(2,1)}, bf16[8,2,64,512]{3,2,1,0:T(8,128)(2,1)}, f32[256,1600]{1,0:T(8,128)}) custom-call(bf16[16,64,512]{2,1,0:T(8,128)(2,1)} %bitcast.69, bf16[16,64,512]{2,1,0:T(8,128)(2,1)} %bitcast.70, bf16[16,64,512]{2,1,0:T(8,128)(2,1)} %bitcast.71, ...), custom_call_target="tpu_custom_call" | custom-call | tf_op jit(solution)/shard_map/from_heads_back/pallas_call | solution.py:793
  597.1 1.9 convert_reduce_fusion.1
  601.0 168.7 %narrow_grads.1 = (bf16[8,64,1600]{2,1,0:T(8,128)(2,1)}, bf16[8,200,512]{2,1,0:T(8,128)(2,1)}, bf16[8,200,512]{2,1,0:T(8,128)(2,1)}, bf16[8,200,512]{2,1,0:T(8,1...) custom-call(bf16[1024,512]{1,0:T(8,128)(2,1)} %bitcast.67, bf16[1024,1600]{1,0:T(8,128)(2,1)} %bitcast.64, ...), custom_call_target="tpu_custom_call" | custom-call | tf_op jit(solution)/shard_map/narrow_grads/pallas_call | solution.py:793
  769.7 2.0 slice.72
  771.7 1.5 collective-permute-start
  773.2 7.5 bitcast_convert_fusion
  781.1 2.6 copy.39
  783.7 0.7 reshape.141
  784.4 1.2 copy.38
  786.1 13.7 %by_rows.1 = (f32[400,6400]{1,0:T(8,128)}, f32[400,1600]{1,0:T(8,128)}, f32[400,1600]{1,0:T(8,128)}, f32[400,1600]{1,0:T(8,128)}) custom-call(s32[4]{0:T(128)} %and_select_fusion.order_ref, bf16[8,200,1600]{2,1,0:T(8,128)(2,1)} %get-tuple-element.94.refs_0_.refs_1_.refs_2_.refs_3_, bf16[8,200,1600]{2,1,0:T(8,128)(2,1)} %get-tuple-element.94.refs_0_.refs_1_.refs_2_.refs_3_, ...), custom_call_target="tpu_custom_call" | custom-call | tf_op jit(solution)/shard_map/by_rows/pallas_call | solution.py:1272
  800.5 2.0 fusion.8
  (38 shorter events, 3.4 us)
Async XLA Ops:
  2.2 1.5 copy-start
  3.6 138.5 %copy-start.5 = (bf16[2,128,1600]{1,2,0:T(8,128)(2,1)S(1)}, bf16[2,128,1600]{1,2,0:T(8,128)(2,1)}, u32[]{:S(2)}) copy-start(bf16[2,128,1600]{1,2,0:T(8,128)(2,1)} %param.18) | copy-start | bytes 2457604
  3.6 139.8 %copy-start.8 = (bf16[1600]{0:T(1024)(128)(2,1)S(1)}, bf16[1600]{0:T(1024)(128)(2,1)}, u32[]{:S(2)}) copy-start(bf16[1600]{0:T(1024)(128)(2,1)} %param.32) | copy-start | bytes 9604
  162.0 92.4 %slice-start = ((s8[5324800]{0:T(1024)(128)(4,1)}), s8[1130496]{0:T(1024)(128)(4,1)S(1)}, s32[]{:S(2)}) async-start(s8[5324800]{0:T(1024)(128)(4,1)} %bitcast.48), calls=%async_computation | async-start | bytes 2260992
  242.8 11.5 %slice-start.1 = ((s8[5324800]{0:T(1024)(128)(4,1)}), s8[4194304]{0:T(1024)(128)(4,1)S(1)}, s32[]{:S(2)}) async-start(s8[5324800]{0:T(1024)(128)(4,1)} %bitcast.48), calls=%async_computation.1 | async-start | bytes 8388608
  242.8 11.5 %copy-start.1 = (bf16[4,256,1600]{2,1,0:T(8,128)(2,1)S(1)}, bf16[4,256,1600]{2,1,0:T(8,128)(2,1)}, u32[]{:S(2)}) copy-start(bf16[4,256,1600]{2,1,0:T(8,128)(2,1)} %get-tuple-element.70) | copy-start | bytes 9830404
  530.7 69.7 %copy-start.6 = (f32[4,1600]{1,0:T(4,128)S(1)}, f32[4,1600]{1,0:T(4,128)}, u32[]{:S(2)}) copy-start(f32[4,1600]{1,0:T(4,128)} %get-tuple-element.92) | copy-start | bytes 76804
  771.7 28.8 %collective-permute-start = (bf16[192,1600]{1,0:T(8,128)(2,1)}, bf16[192,1600]{1,0:T(8,128)(2,1)S(1)}, u32[]{:S(2)}, u32[]{:S(2)}) collective-permute-start(bf16[192,1600]{1,0:T(8,128)(2,1)} %bitcast.22), channel_id=1, source_target_pairs={{0,1},{1,2},{2,3},{4,5},{5,6},{6,7},{8,9},{9,10},{10,11},{12,13},{... | collective-permute-start | bytes 1843208 | tf_op jit(solution)/shard_map/ppermute | solution.py:1450
  773.2 7.5 copy-start.3
  773.2 7.5 copy-start.4
  773.2 7.7 copy-start.2
  780.7 3.0 copy-start.7

commit v7 on v6

--- a/solution.py
+++ b/solution.py
@@ -72,9 +72,8 @@
     return jnp.where(keys <= queries, scores, NEGATIVE)
 
 
-def attend_kernel(block, heads, q_ref, k_ref, v_ref, o_ref, ot_ref, lse_ref):
+def attend_pair(block, heads, pair, q_ref, k_ref, v_ref, o_ref, ot_ref, lse_ref):
     length = q_ref.shape[0]
-    pair = pl.program_id(0)
     v_t = jnp.transpose(v_ref[...].astype(F32)).astype(BF16)
 
     def one_head(half):
@@ -106,34 +105,10 @@
     o_ref[...] = jnp.transpose(ot_ref[0]).astype(BF16)
 
 
-def attend(queries, keys, values, heads):
-    length, width = queries.shape
-    pairs = width // LANES
-    block = min(256, length)
-    column = pl.BlockSpec((length, LANES), lambda p: (0, p))
-    return pl.pallas_call(
-        functools.partial(attend_kernel, block, heads),
-        grid=(pairs,),
-        in_specs=[column] * 3,
-        out_specs=[
-            column,
-            pl.BlockSpec((1, LANES, length), lambda p: (p, 0, 0)),
-            pl.BlockSpec((1, 2, length), lambda p: (p, 0, 0)),
-        ],
-        out_shape=[
-            jax.ShapeDtypeStruct((length, width), BF16),
-            jax.ShapeDtypeStruct((pairs, LANES, length), F32),
-            jax.ShapeDtypeStruct((pairs, 2, length), F32),
-        ],
-        name="attend",
-    )(queries, keys, values)
-
-
-def attend_back_kernel(
-    block, heads, q_ref, k_ref, v_ref, do_ref, ot_ref, lse_ref, dq_ref, dk_ref, dv_ref, dk_sum, dv_sum
+def attend_back_pair(
+    block, heads, pair, q_ref, k_ref, v_ref, do_ref, ot_ref, lse_ref, dq_ref, dk_ref, dv_ref, dk_sum, dv_sum
 ):
     length = q_ref.shape[0]
-    pair = pl.program_id(0)
     k_t = jnp.transpose(k_ref[...].astype(F32)).astype(BF16)
     do_t = jnp.transpose(do_ref[...].astype(F32))
     dk_sum[...] = jnp.zeros_like(dk_sum)
@@ -170,26 +145,6 @@
     dv_ref[...] = dv_sum[...].astype(BF16)
 
 
-def attend_back(queries, keys, values, grad, ot, lse, heads):
-    length, width = queries.shape
-    pairs = width // LANES
-    block = min(256, length)
-    column = pl.BlockSpec((length, LANES), lambda p: (0, p))
-    return pl.pallas_call(
-        functools.partial(attend_back_kernel, block, heads),
-        grid=(pairs,),
-        in_specs=[column] * 4
-        + [
-            pl.BlockSpec((1, LANES, length), lambda p: (p, 0, 0)),
-            pl.BlockSpec((1, 2, length), lambda p: (p, 0, 0)),
-        ],
-        out_specs=[column] * 3,
-        out_shape=[jax.ShapeDtypeStruct((length, width), BF16)] * 3,
-        scratch_shapes=[pltpu.VMEM((length, LANES), F32)] * 2,
-        name="attend_back",
-    )(queries, keys, values, grad, ot, lse)
-
-
 class Place:
     def __init__(self):
         self.parts = lax.axis_size("fsdp")
@@ -418,24 +373,6 @@
             lax.fori_loop(1, n, end, 0)
 
         return [first, second]
-
-
-class FromHeads(ToHeads):
-    def __init__(self, arrays, seqs):
-        blocks, half, piece = arrays[0].shape
-        self.n = blocks // 2
-        self.groups = self.n // seqs
-        self.piece = piece
-        self.ins = list(arrays)
-        shape = (seqs, 2, half, piece * self.groups)
-        self.outs = [jax.ShapeDtypeStruct(shape, a.dtype) for a in arrays]
-        self.scratch = [pltpu.SemaphoreType.DMA((len(arrays), 2, self.n))] * 2
-
-    def source(self, ref, other, half):
-        return self.block(ref, other, half)
-
-    def target(self, ref, other, half):
-        return self.whole(ref, other, half)
 
 
 class Swap:
@@ -840,19 +777,153 @@
     return [begin, middle, later, fourth]
 
 
+class Sender:
+    def __init__(self, count, seqs, half, piece):
+        self.n = n = lax.axis_size("ctx")
+        self.half, self.piece, self.pairs = half, piece, piece // LANES
+        self.groups = n // seqs
+        self.count = count
+        self.outs = [like((seqs, 2, half, piece * self.groups), BF16)] * count
+        self.scratch = [pltpu.VMEM((2 * n * half, piece), BF16)] * count
+        self.scratch += [pltpu.SemaphoreType.DMA((count, 2, self.pairs, n))] * 2
+
+    def bind(self, place, outs, scratch):
+        held, (send, recv) = scratch[: self.count], scratch[self.count :]
+        n, me, half = self.n, place.ctx, self.half
+        every = [(i, side) for i in range(self.count) for side in range(2)]
+
+        def block(ref, pair, other, side):
+            index = other if side == 0 else 2 * n - 1 - other
+            rows = pl.ds(pl.multiple_of(index * half, half), half)
+            return ref.at[rows, pl.ds(pl.multiple_of(pair * LANES, LANES), LANES)]
+
+        def place_of(ref, pair, other, side):
+            column = pl.multiple_of(other % self.groups * self.piece + pair * LANES, LANES)
+            return ref.at[other // self.groups, side, :, pl.ds(column, LANES)]
+
+        def copy(i, side, pair, step, index):
+            other = (me + step) % n
+            return remote(
+                block(held[i], pair, other, side),
+                place_of(outs[i], pair, index, side),
+                send.at[i, side, pair, step],
+                recv.at[i, side, pair, step],
+                ctx=other,
+            )
+
+        def begin(pair):
+            def start(step, _):
+                for i, side in every:
+                    copy(i, side, pair, step, me).start()
+                return 0
+
+            lax.fori_loop(1, n, start, 0)
+            for i, side in every:
+                place_of(outs[i], pair, me, side)[...] = block(held[i], pair, me, side)[...]
+
+        def end():
+            def pair_end(pair, _):
+                def step_end(step, _):
+                    for i, side in every:
+                        copy(i, side, pair, step, (me + n - step) % n).wait_recv()
+                        copy(i, side, pair, step, me).wait_send()
+                    return 0
+
+                lax.fori_loop(1, n, step_end, 0)
+                return 0
+
+            lax.fori_loop(0, self.pairs, pair_end, 0)
+
+        return held, begin, end
+
+
+def lanes(ref, pair):
+    return ref.at[:, pl.ds(pl.multiple_of(pair * LANES, LANES), LANES)]
+
+
+class Attend:
+    reach = ("ctx",)
+
+    def __init__(self, queries, keys, values, heads, seqs, half):
+        length, piece = queries.shape
+        self.block, self.heads = min(256, length), heads
+        self.sender = Sender(1, seqs, half, piece)
+        pairs = self.sender.pairs
+        self.ins = [queries, keys, values]
+        self.outs = [
+            *self.sender.outs,
+            like((pairs, LANES, length), F32),
+            like((pairs, 2, length), F32),
+        ]
+        self.scratch = self.sender.scratch
+
+    def phases(self, place, ins, outs, scratch):
+        out, ot, lse = outs
+        held, begin, end = self.sender.bind(place, [out], scratch)
+
+        def run():
+            def one(pair, _):
+                columns = [lanes(ref, pair) for ref in (*ins, held[0])]
+                own = pl.ds(pair, 1)
+                attend_pair(self.block, self.heads, pair, *columns, ot.at[own], lse.at[own])
+                begin(pair)
+                return 0
+
+            lax.fori_loop(0, self.sender.pairs, one, 0)
+
+        return [run, end]
+
+
+class AttendBack:
+    reach = ("ctx",)
+
+    def __init__(self, queries, keys, values, grad, ot, lse, heads, seqs, half):
+        length, piece = queries.shape
+        self.block, self.heads = min(256, length), heads
+        self.sender = Sender(3, seqs, half, piece)
+        self.ins = [queries, keys, values, grad, ot, lse]
+        self.outs = self.sender.outs
+        self.scratch = [pltpu.VMEM((length, LANES), F32)] * 2 + self.sender.scratch
+
+    def phases(self, place, ins, outs, scratch):
+        *given, ot, lse = ins
+        sums, scratch = scratch[:2], scratch[2:]
+        held, begin, end = self.sender.bind(place, outs, scratch)
+
+        def run():
+            def one(pair, _):
+                own = pl.ds(pair, 1)
+                attend_back_pair(
+                    self.block,
+                    self.heads,
+                    pair,
+                    *[lanes(ref, pair) for ref in given],
+                    ot.at[own],
+                    lse.at[own],
+                    *[lanes(ref, pair) for ref in held],
+                    *sums,
+                )
+                begin(pair)
+                return 0
+
+            lax.fori_loop(0, self.sender.pairs, one, 0)
+
+        return [run, end]
+
+
 class Middle:
     reach = ("fsdp", "ctx")
 
-    def __init__(self, blocks, seqs, out_w, x_full, vectors):
+    def __init__(self, heads, out_w, x_full, vectors):
         own, width = x_full.shape
         parts = lax.axis_size("fsdp")
         self.own, self.parts = own, parts
-        self.heads = FromHeads([blocks], seqs)
+        self.heads = heads
         self.scatter = Scatter(like((parts, own, width), BF16))
         self.gather = Gather(like((own, width), BF16))
-        self.ins = [blocks, out_w, x_full, vectors]
+        self.ins = [*heads.ins, out_w, x_full, vectors]
         self.outs = [
-            self.heads.outs[0],
+            *heads.outs,
             like((own, width), F32),
             like((own, width), F32),
             like((own, 1), F32),
@@ -867,10 +938,10 @@
             self.scratch += transfer.scratch
 
     def phases(self, place, ins, outs, scratch):
-        blocks, out_w, x_full, vectors = ins
-        attended, resid, hat, inv, normed_all = outs
+        *given, out_w, x_full, vectors = ins
+        attended, ot, lse, resid, hat, inv, normed_all = outs
         part, branch, normed, *rest = scratch
-        heads = share(self.heads, place, rest, [blocks], [attended])
+        heads = share(self.heads, place, rest, given, [attended, ot, lse])
         scatter = share(self.scatter, place, rest, [part], [branch])
         gather = share(self.gather, place, rest, [normed], [normed_all])
         seqs, _, half, cols = attended.shape
@@ -1357,15 +1428,12 @@
     heads = [q_heads, k_heads, v_heads]
 
     q_seq, k_seq, v_seq = [a.reshape(length, piece) for a in heads]
-    o_seq, ot, lse = attend(q_seq, k_seq, v_seq, heads_here)
-
-    def blocks(array):
-        return array.reshape(2 * n_ctx, half_rows, piece)
-
-    (attended, resid, hat_two, inv_two, normed_two), (grad_y,) = exchange(
+    (attended, ot, lse, resid, hat_two, inv_two, normed_two), (grad_y,) = exchange(
         2,
         "middle",
-        Middle(blocks(o_seq), all_seqs, out_w, x_full, full[4:7]),
+        Middle(
+            Attend(q_seq, k_seq, v_seq, heads_here, all_seqs, half_rows), out_w, x_full, full[4:7]
+        ),
         Gather(cotangent.reshape(own, width)),
     )
     attended = attended.reshape(tokens, cols)
@@ -1394,13 +1462,21 @@
     grad_branch = grad_branch.reshape(tokens, width)
 
     ((grad_heads,),) = exchange(4, "to_heads_back", ToHeads([by_sequences(grad_attended)]))
-    dq_seq, dk_seq, dv_seq = attend_back(
-        q_seq, k_seq, v_seq, grad_heads.reshape(length, piece), ot, lse, heads_here
+    back = AttendBack(
+        q_seq,
+        k_seq,
+        v_seq,
+        grad_heads.reshape(length, piece),
+        ot,
+        lse,
+        heads_here,
+        all_seqs,
+        half_rows,
     )
     grad_qkv, (mlp,) = exchange(
         5,
         "from_heads_back",
-        Later(FromHeads([blocks(a) for a in (dq_seq, dk_seq, dv_seq)], all_seqs), 0, 4),
+        Later(back, 0, 4),
         Product(activated, proj, own),
     )
     outputs = (resid + mlp + bias_proj).astype(BF16).reshape(seqs, rows, width)

time: 807 us -> 794 us (0.984)
  Pallas kernels: 750 us -> 737 us
    pallas_call x2 -> x0, Pallas kernels: 34.4 us -> none  [the longest x1 18.6 us: attend(): pl.pallas_call(functools.partial(attend_kernel, block, heads), grid=(pair...]
    pallas_call x6, Pallas kernels: 701 us -> 723 us  [exchange(): pl.pallas_call(functools.partial(exchange_kernel, transfers, places), out...]
where the time goes in v7:
time: 794 us; the launch traced here: 790 us
  Pallas kernels  737 us (93%)
  matrix products  22 us (3%)
  local copies, waits for them, and re-layouts  14.3 us (2%)
  other arithmetic  14.2 us (2%)
    pallas_call x6, Pallas kernels, exchange(): pl.pallas_call(functools.partial(exchange_kernel, transfers, places), out...  723 us
  transfers between devices with their start and end apart: 1, of which 0 were waited for; matrix products, arithmetic and copies ran while one was open for 2% of the time, Pallas kernels for 2%

profile of v7, /device:TPU:0, one launch (start us, length us, event | category | flops | bytes accessed | tf_op | source)
XLA Modules:
  0.0 789.9 jit_solution(929516146684770762)
XLA Ops:
  0.7 1.5 copy.34
  2.2 1.5 bitcast_convert_fusion.1.refs_4_
  3.6 135.5 %first.1 = (bf16[1600,512]{1,0:T(8,128)(2,1)}, bf16[1600,512]{1,0:T(8,128)(2,1)}, bf16[1600,512]{1,0:T(8,128)(2,1)}, f32[256,1600]{1,0:T(8,128)}, f32[256,1]{1,0...) custom-call(bf16[256,1600]{1,0:T(8,128)(2,1)} %bitcast.40, ...), custom_call_target="tpu_custom_call" | custom-call | tf_op jit(solution)/shard_map/first/pallas_call | solution.py:730
  139.2 1.4 slice.64.refs_5_
  140.6 1.5 fusion.10
  142.1 1.2 copy.35
  143.4 100.2 %middle.1 = (bf16[8,2,64,512]{3,2,1,0:T(8,128)(2,1)}, f32[4,128,1024]{2,1,0:T(8,128)}, f32[4,2,1024]{2,1,0:T(2,128)}, f32[256,1600]{1,0:T(8,128)}, f32[256,1600]...) custom-call(bf16[1024,512]{1,0:T(8,128)(2,1)} %bitcast.46, ...), custom_call_target="tpu_custom_call" | custom-call | tf_op jit(solution)/shard_map/middle/pallas_call | solution.py:730
  243.6 11.5 %multiply_convert_fusion = (bf16[1024,1600]{1,0:T(8,128)(2,1)}, f32[1024,1600]{1,0:T(8,128)S(1)}) fusion(f32[1600]{0:T(1024)S(1)} %convert_element_type.33, bf16[1024,1600]{1,0:T(8,128)(2,1)} %bitcast.55, bf16[1600,1600]{1,0:T(8,128)(2,1)} %bitcast.42), kind=kOutput, calls=%fused_computation.10 | convolution fusion | flops 5259264000 | bytes 18233600 | tf_op jit(solution)/shard_map/dot_general | solution.py:49
  255.2 10.5 %convert_reduce_fusion = (f32[1600]{0:T(1024)S(1)}, bf16[1024,1600]{1,0:T(8,128)(2,1)}) fusion(f32[1024,1600]{1,0:T(8,128)S(1)} %get-tuple-element.126, f32[1600]{0:T(1024)S(1)} %convert_element_type.33, bf16[1024,1600]{1,0:T(8,128)(2,1)S(1)} %bitcast.58, bf16[1600,1600]{1,0:T(8,128)(2,1)S(1)} %bitcast.45), kind=kOutput, calls=%fused_computation.9 | convolution fusion | flops 5278923264 | bytes 18240000 | tf_op jit(solution)/shard_map/dot_general | solution.py:53
  265.7 225.4 %wide_grads.1 = (bf16[8,200,1600]{2,1,0:T(8,128)(2,1)}, bf16[8,200,1600]{2,1,0:T(8,128)(2,1)}, f32[256,1600]{1,0:T(8,128)}, bf16[4,256,1600]{2,1,0:T(8,128)(2,1)...) custom-call(bf16[1024,1600]{1,0:T(8,128)(2,1)} %get-tuple-element.125.refs_0_.refs_6_, bf16[1024,1600]{1,0:T(8,128)(2,1)} %bitcast.56, ...), custom_call_target="tpu_custom_call" | custom-call | tf_op jit(solution)/shard_map/wide_grads/pallas_call | solution.py:730
  491.0 20.0 %to_heads_back.1 = bf16[16,64,512]{2,1,0:T(8,128)(2,1)} custom-call(bf16[8,2,64,512]{3,2,1,0:T(8,128)(2,1)} %bitcast.65), custom_call_target="tpu_custom_call" | custom-call | tf_op jit(solution)/shard_map/to_heads_back/pallas_call | solution.py:730
  511.1 87.8 %from_heads_back.1 = (bf16[8,2,64,512]{3,2,1,0:T(8,128)(2,1)}, bf16[8,2,64,512]{3,2,1,0:T(8,128)(2,1)}, bf16[8,2,64,512]{3,2,1,0:T(8,128)(2,1)}, f32[256,1600]{1,0:T(8,128)}) custom-call(bf16[1024,512]{1,0:T(8,128)(2,1)} %bitcast.47, bf16[1024,512]{1,0:T(8,128)(2,1)} %bitcast.49, bf16[1024,512]{1,0:T(8,128)(2,1)} %bitcast.51, bf16[1024,512]{1,0:T(8,128)(2,1)} %bitcast.54, ...), custom_call_target="tpu_custom_call" | custom-call | tf_op jit(solution)/shard_map/from_heads_back/pallas_call | solution.py:730
  598.8 1.9 convert_reduce_fusion.1
  601.4 0.7 reshape.123.refs_14_
  602.1 0.6 pad_maximum_fusion.refs_13_
  602.7 154.2 %narrow_grads.1 = (bf16[8,64,1600]{2,1,0:T(8,128)(2,1)}, bf16[8,200,512]{2,1,0:T(8,128)(2,1)}, bf16[8,200,512]{2,1,0:T(8,128)(2,1)}, bf16[8,200,512]{2,1,0:T(8,1...) custom-call(bf16[1024,512]{1,0:T(8,128)(2,1)} %bitcast.63, bf16[1024,1600]{1,0:T(8,128)(2,1)} %bitcast.60, ...), custom_call_target="tpu_custom_call" | custom-call | tf_op jit(solution)/shard_map/narrow_grads/pallas_call | solution.py:730
  756.9 2.0 slice.72
  758.9 1.5 collective-permute-start
  760.5 7.5 bitcast_convert_fusion
  768.3 2.6 copy.39
  770.9 0.7 reshape.125
  771.6 1.2 copy.38
  773.3 13.7 %by_rows.1 = (f32[400,6400]{1,0:T(8,128)}, f32[400,1600]{1,0:T(8,128)}, f32[400,1600]{1,0:T(8,128)}, f32[400,1600]{1,0:T(8,128)}) custom-call(s32[4]{0:T(128)} %and_select_fusion.order_ref, bf16[8,200,1600]{2,1,0:T(8,128)(2,1)} %get-tuple-element.86.refs_0_.refs_1_.refs_2_.refs_3_, bf16[8,200,1600]{2,1,0:T(8,128)(2,1)} %get-tuple-element.86.refs_0_.refs_1_.refs_2_.refs_3_, ...), custom_call_target="tpu_custom_call" | custom-call | tf_op jit(solution)/shard_map/by_rows/pallas_call | solution.py:1343
  787.7 2.0 fusion.8
  (36 shorter events, 2.1 us)
Async XLA Ops:
  2.2 1.5 copy-start
  3.6 138.5 %copy-start.5 = (bf16[2,128,1600]{1,2,0:T(8,128)(2,1)S(1)}, bf16[2,128,1600]{1,2,0:T(8,128)(2,1)}, u32[]{:S(2)}) copy-start(bf16[2,128,1600]{1,2,0:T(8,128)(2,1)} %param.18) | copy-start | bytes 2457604
  3.6 139.7 %copy-start.8 = (bf16[1600]{0:T(1024)(128)(2,1)S(1)}, bf16[1600]{0:T(1024)(128)(2,1)}, u32[]{:S(2)}) copy-start(bf16[1600]{0:T(1024)(128)(2,1)} %param.32) | copy-start | bytes 9604
  143.4 111.8 %slice-start = ((s8[5324800]{0:T(1024)(128)(4,1)}), s8[1130496]{0:T(1024)(128)(4,1)S(1)}, s32[]{:S(2)}) async-start(s8[5324800]{0:T(1024)(128)(4,1)} %bitcast.44), calls=%async_computation | async-start | bytes 2260992
  243.6 11.5 %slice-start.1 = ((s8[5324800]{0:T(1024)(128)(4,1)}), s8[4194304]{0:T(1024)(128)(4,1)S(1)}, s32[]{:S(2)}) async-start(s8[5324800]{0:T(1024)(128)(4,1)} %bitcast.44), calls=%async_computation.1 | async-start | bytes 8388608
  243.6 11.5 %copy-start.1 = (bf16[4,256,1600]{2,1,0:T(8,128)(2,1)S(1)}, bf16[4,256,1600]{2,1,0:T(8,128)(2,1)}, u32[]{:S(2)}) copy-start(bf16[4,256,1600]{2,1,0:T(8,128)(2,1)} %get-tuple-element.65) | copy-start | bytes 9830404
  511.0 91.0 %copy-start.6 = (f32[4,1600]{1,0:T(4,128)S(1)}, f32[4,1600]{1,0:T(4,128)}, u32[]{:S(2)}) copy-start(f32[4,1600]{1,0:T(4,128)} %get-tuple-element.84) | copy-start | bytes 76804
  758.9 28.8 %collective-permute-start = (bf16[192,1600]{1,0:T(8,128)(2,1)}, bf16[192,1600]{1,0:T(8,128)(2,1)S(1)}, u32[]{:S(2)}, u32[]{:S(2)}) collective-permute-start(bf16[192,1600]{1,0:T(8,128)(2,1)} %bitcast.18), channel_id=1, source_target_pairs={{0,1},{1,2},{2,3},{4,5},{5,6},{6,7},{8,9},{9,10},{10,11},{12,13},{... | collective-permute-start | bytes 1843208 | tf_op jit(solution)/shard_map/ppermute | solution.py:1526
  760.4 7.5 copy-start.3
  760.4 7.5 copy-start.4
  760.4 7.7 copy-start.2
  767.9 3.0 copy-start.7

commit v8 on v7

--- a/solution.py
+++ b/solution.py
@@ -1417,8 +1417,8 @@
         0,
         "first",
         first,
-        Later(Swap([w_fc], hidden_part, hidden_part), steps, steps + 3),
-        Later(Window(w_out, live, cols), steps, steps + 3),
+        Later(Swap([w_fc], hidden_part, hidden_part), steps + 2, steps + 3),
+        Later(Window(w_out, live, cols), steps + 2, steps + 3),
     )
     gain_one, gain_two, bias_proj = full[0], full[5], full[7]
     bias_fc = fc_bias.astype(F32)
@@ -1428,13 +1428,13 @@
     heads = [q_heads, k_heads, v_heads]
 
     q_seq, k_seq, v_seq = [a.reshape(length, piece) for a in heads]
-    (attended, ot, lse, resid, hat_two, inv_two, normed_two), (grad_y,) = exchange(
+    (grad_y,), (attended, ot, lse, resid, hat_two, inv_two, normed_two) = exchange(
         2,
         "middle",
+        Gather(cotangent.reshape(own, width)),
         Middle(
             Attend(q_seq, k_seq, v_seq, heads_here, all_seqs, half_rows), out_w, x_full, full[4:7]
         ),
-        Gather(cotangent.reshape(own, width)),
     )
     attended = attended.reshape(tokens, cols)
     normed_two = normed_two.reshape(tokens, width)

time: 794 us -> 788 us (level)
  no operation moved by 1% of the time
where the time goes in v8:
time: 788 us; the launch traced here: 783 us
  Pallas kernels  730 us (93%)
  matrix products  22 us (3%)
  local copies, waits for them, and re-layouts  14.3 us (2%)
  other arithmetic  14.2 us (2%)
    pallas_call x6, Pallas kernels, exchange(): pl.pallas_call(functools.partial(exchange_kernel, transfers, places), out...  716 us
  transfers between devices with their start and end apart: 1, of which 0 were waited for; matrix products, arithmetic and copies ran while one was open for 2% of the time, Pallas kernels for 2%

profile of v8, /device:TPU:0, one launch (start us, length us, event | category | flops | bytes accessed | tf_op | source)
XLA Modules:
  0.0 782.6 jit_solution(7515124820000370667)
XLA Ops:
  0.7 1.5 copy.35
  2.2 1.5 bitcast_convert_fusion.1.refs_5_
  3.6 140.0 %first.1 = (bf16[1600,512]{1,0:T(8,128)(2,1)}, bf16[1600,512]{1,0:T(8,128)(2,1)}, bf16[1600,512]{1,0:T(8,128)(2,1)}, f32[256,1600]{1,0:T(8,128)}, f32[256,1]{1,0...) custom-call(bf16[256,1600]{1,0:T(8,128)(2,1)} %bitcast.40, ...), custom_call_target="tpu_custom_call" | custom-call | tf_op jit(solution)/shard_map/first/pallas_call | solution.py:730
  143.6 1.4 slice.64.refs_6_
  145.1 1.5 fusion.10
  146.6 1.2 copy.34
  147.9 86.8 %middle.1 = (bf16[4,256,1600]{2,1,0:T(8,128)(2,1)}, bf16[8,2,64,512]{3,2,1,0:T(8,128)(2,1)}, f32[4,128,1024]{2,1,0:T(8,128)}, f32[4,2,1024]{2,1,0:T(2,128)}, f32...) custom-call(bf16[256,1600]{1,0:T(8,128)(2,1)} %bitcast.38, ...), custom_call_target="tpu_custom_call" | custom-call | tf_op jit(solution)/shard_map/middle/pallas_call | solution.py:730
  234.7 11.5 %multiply_convert_fusion = (bf16[1024,1600]{1,0:T(8,128)(2,1)}, f32[1024,1600]{1,0:T(8,128)S(1)}) fusion(f32[1600]{0:T(1024)S(1)} %convert_element_type.33, bf16[1024,1600]{1,0:T(8,128)(2,1)} %bitcast.57, bf16[1600,1600]{1,0:T(8,128)(2,1)} %bitcast.42), kind=kOutput, calls=%fused_computation.10 | convolution fusion | flops 5259264000 | bytes 18233600 | tf_op jit(solution)/shard_map/dot_general | solution.py:49
  246.2 10.5 %convert_reduce_fusion = (f32[1600]{0:T(1024)S(1)}, bf16[1024,1600]{1,0:T(8,128)(2,1)}) fusion(f32[1024,1600]{1,0:T(8,128)S(1)} %get-tuple-element.126, f32[1600]{0:T(1024)S(1)} %convert_element_type.33, bf16[1024,1600]{1,0:T(8,128)(2,1)S(1)} %bitcast.56, bf16[1600,1600]{1,0:T(8,128)(2,1)S(1)} %bitcast.45), kind=kOutput, calls=%fused_computation.9 | convolution fusion | flops 5278923264 | bytes 18240000 | tf_op jit(solution)/shard_map/dot_general | solution.py:53
  256.8 226.6 %wide_grads.1 = (bf16[8,200,1600]{2,1,0:T(8,128)(2,1)}, bf16[8,200,1600]{2,1,0:T(8,128)(2,1)}, f32[256,1600]{1,0:T(8,128)}, bf16[4,256,1600]{2,1,0:T(8,128)(2,1)...) custom-call(bf16[1024,1600]{1,0:T(8,128)(2,1)} %get-tuple-element.125.refs_0_.refs_6_, bf16[1024,1600]{1,0:T(8,128)(2,1)} %bitcast.58, ...), custom_call_target="tpu_custom_call" | custom-call | tf_op jit(solution)/shard_map/wide_grads/pallas_call | solution.py:730
  483.4 20.3 %to_heads_back.1 = bf16[16,64,512]{2,1,0:T(8,128)(2,1)} custom-call(bf16[8,2,64,512]{3,2,1,0:T(8,128)(2,1)} %bitcast.65), custom_call_target="tpu_custom_call" | custom-call | tf_op jit(solution)/shard_map/to_heads_back/pallas_call | solution.py:730
  503.8 88.1 %from_heads_back.1 = (bf16[8,2,64,512]{3,2,1,0:T(8,128)(2,1)}, bf16[8,2,64,512]{3,2,1,0:T(8,128)(2,1)}, bf16[8,2,64,512]{3,2,1,0:T(8,128)(2,1)}, f32[256,1600]{1,0:T(8,128)}) custom-call(bf16[1024,512]{1,0:T(8,128)(2,1)} %bitcast.47, bf16[1024,512]{1,0:T(8,128)(2,1)} %bitcast.49, bf16[1024,512]{1,0:T(8,128)(2,1)} %bitcast.51, bf16[1024,512]{1,0:T(8,128)(2,1)} %bitcast.54, ...), custom_call_target="tpu_custom_call" | custom-call | tf_op jit(solution)/shard_map/from_heads_back/pallas_call | solution.py:730
  591.8 1.9 convert_reduce_fusion.1
  594.4 0.7 reshape.123.refs_14_
  595.1 0.6 pad_maximum_fusion.refs_13_
  595.7 153.9 %narrow_grads.1 = (bf16[8,64,1600]{2,1,0:T(8,128)(2,1)}, bf16[8,200,512]{2,1,0:T(8,128)(2,1)}, bf16[8,200,512]{2,1,0:T(8,128)(2,1)}, bf16[8,200,512]{2,1,0:T(8,1...) custom-call(bf16[1024,512]{1,0:T(8,128)(2,1)} %bitcast.63, bf16[1024,1600]{1,0:T(8,128)(2,1)} %bitcast.60, ...), custom_call_target="tpu_custom_call" | custom-call | tf_op jit(solution)/shard_map/narrow_grads/pallas_call | solution.py:730
  749.7 2.0 slice.72
  751.6 1.5 collective-permute-start
  753.2 7.5 bitcast_convert_fusion
  761.0 2.6 copy.39
  763.6 0.7 reshape.125
  764.3 1.2 copy.38
  766.1 13.7 %by_rows.1 = (f32[400,6400]{1,0:T(8,128)}, f32[400,1600]{1,0:T(8,128)}, f32[400,1600]{1,0:T(8,128)}, f32[400,1600]{1,0:T(8,128)}) custom-call(s32[4]{0:T(128)} %and_select_fusion.order_ref, bf16[8,200,1600]{2,1,0:T(8,128)(2,1)} %get-tuple-element.86.refs_0_.refs_1_.refs_2_.refs_3_, bf16[8,200,1600]{2,1,0:T(8,128)(2,1)} %get-tuple-element.86.refs_0_.refs_1_.refs_2_.refs_3_, ...), custom_call_target="tpu_custom_call" | custom-call | tf_op jit(solution)/shard_map/by_rows/pallas_call | solution.py:1343
  780.4 2.0 fusion.8
  (36 shorter events, 2.1 us)
Async XLA Ops:
  2.2 1.5 copy-start
  3.6 142.9 %copy-start.5 = (bf16[2,128,1600]{1,2,0:T(8,128)(2,1)S(1)}, bf16[2,128,1600]{1,2,0:T(8,128)(2,1)}, u32[]{:S(2)}) copy-start(bf16[2,128,1600]{1,2,0:T(8,128)(2,1)} %param.18) | copy-start | bytes 2457604
  3.6 144.2 %copy-start.8 = (bf16[1600]{0:T(1024)(128)(2,1)S(1)}, bf16[1600]{0:T(1024)(128)(2,1)}, u32[]{:S(2)}) copy-start(bf16[1600]{0:T(1024)(128)(2,1)} %param.32) | copy-start | bytes 9604
  147.9 98.4 %slice-start = ((s8[5324800]{0:T(1024)(128)(4,1)}), s8[1130496]{0:T(1024)(128)(4,1)S(1)}, s32[]{:S(2)}) async-start(s8[5324800]{0:T(1024)(128)(4,1)} %bitcast.44), calls=%async_computation | async-start | bytes 2260992
  234.7 11.5 %slice-start.1 = ((s8[5324800]{0:T(1024)(128)(4,1)}), s8[4194304]{0:T(1024)(128)(4,1)S(1)}, s32[]{:S(2)}) async-start(s8[5324800]{0:T(1024)(128)(4,1)} %bitcast.44), calls=%async_computation.1 | async-start | bytes 8388608
  234.7 11.5 %copy-start.1 = (bf16[4,256,1600]{2,1,0:T(8,128)(2,1)S(1)}, bf16[4,256,1600]{2,1,0:T(8,128)(2,1)}, u32[]{:S(2)}) copy-start(bf16[4,256,1600]{2,1,0:T(8,128)(2,1)} %get-tuple-element.65) | copy-start | bytes 9830404
  503.8 91.3 %copy-start.6 = (f32[4,1600]{1,0:T(4,128)S(1)}, f32[4,1600]{1,0:T(4,128)}, u32[]{:S(2)}) copy-start(f32[4,1600]{1,0:T(4,128)} %get-tuple-element.84) | copy-start | bytes 76804
  751.6 28.8 %collective-permute-start = (bf16[192,1600]{1,0:T(8,128)(2,1)}, bf16[192,1600]{1,0:T(8,128)(2,1)S(1)}, u32[]{:S(2)}, u32[]{:S(2)}) collective-permute-start(bf16[192,1600]{1,0:T(8,128)(2,1)} %bitcast.18), channel_id=1, source_target_pairs={{0,1},{1,2},{2,3},{4,5},{5,6},{6,7},{8,9},{9,10},{10,11},{12,13},{... | collective-permute-start | bytes 1843208 | tf_op jit(solution)/shard_map/ppermute | solution.py:1526
  753.2 7.5 copy-start.3
  753.2 7.5 copy-start.4
  753.2 7.7 copy-start.2
  760.7 3.0 copy-start.7
